TPU v7x, 32 devices: a 4x4x1 block of a 4x4x8 slice. The times are simulated.
32 devices in a mesh: dp: 1 (over z), tp: 4 (over y), cp: 8 (over x, core).
Axes of the slice: x: 4, y: 4, z: 1, core: 2. Of those that a mesh axis runs over, the one named last changes fastest.
The devices are a block of a 4x4x8 slice.
Arguments:
- x_in: bfloat16 [1024, 4096], P(('dp', 'cp', 'tp'))
- w_query: bfloat16 [4096, 32, 128], P(None, 'tp')
- w_key: bfloat16 [4096, 32, 128], P(None, 'tp')
- w_value: bfloat16 [4096, 32, 128], P(None, 'tp')
- w_out: bfloat16 [32, 128, 4096], P('tp')
- d_out: bfloat16 [1024, 4096], P(('dp', 'cp', 'tp'))
Outputs:
- output 1: bfloat16 [1024, 4096], P(('dp', 'cp', 'tp'))
- output 2: bfloat16 [1024, 4096], P(('dp', 'cp', 'tp'))
- output 3: bfloat16 [8, 4096, 32, 128], P(('dp', 'cp'), None, 'tp')
- output 4: bfloat16 [8, 4096, 32, 128], P(('dp', 'cp'), None, 'tp')
- output 5: bfloat16 [8, 4096, 32, 128], P(('dp', 'cp'), None, 'tp')
- output 6: bfloat16 [8, 32, 128, 4096], P(('dp', 'cp'), 'tp')
All inputs are finite; a program needn't handle non-finite values.
Results may differ from a plain program's by a relative error of at most 0.0102951.
Values are sent between devices in bfloat16 or wider.
A program may use at most 768 MiB of HBM per device.

v0:
```python
import jax
import jax.numpy as jnp
from jax import lax
from jax.sharding import PartitionSpec as P

ROW_SPEC = P(("dp", "cp", "tp"), None)
HEAD_SPEC = P(None, "tp", None)
OUT_W_SPEC = P("tp", None, None)
GRAD_SPEC = P(("dp", "cp"), None, "tp", None)
GRAD_OUT_SPEC = P(("dp", "cp"), "tp", None, None)
COLS_CONTRACT = (((1,), (1,)), ((), ()))
ROWS_CONTRACT = (((0,), (0,)), ((), ()))


def causal_where(pos_pair, values, fill):
    q_pos, k_pos = pos_pair
    return jnp.where(q_pos[:, None, None, None] >= k_pos[None, None, None, :], values, fill)


def attend_update(softmax_state, q_rows, k_blk, v_blk, pos_pair):
    row_max, row_sum, out_acc = softmax_state
    attn_scale = q_rows.shape[-1] ** -0.5
    scores = jnp.einsum("qhgd,khd->qhgk", q_rows, k_blk, preferred_element_type=jnp.float32) * attn_scale
    if pos_pair is not None:
        scores = causal_where(pos_pair, scores, -jnp.inf)
    new_max = jnp.maximum(row_max, jnp.max(scores, axis=-1))
    prob_mat = jnp.exp(scores - new_max[..., None])
    factor = jnp.exp(row_max - new_max)
    new_sum = row_sum * factor + jnp.sum(prob_mat, axis=-1)
    pv_part = jnp.einsum("qhgk,khd->qhgd", prob_mat.astype(jnp.bfloat16), v_blk, preferred_element_type=jnp.float32)
    return new_max, new_sum, out_acc * factor[..., None] + pv_part


def grad_update(q_rows, do_rows, lse_rows, dot_rows, k_blk, v_blk, pos_pair):
    attn_scale = q_rows.shape[-1] ** -0.5
    scores = jnp.einsum("qhgd,khd->qhgk", q_rows, k_blk, preferred_element_type=jnp.float32) * attn_scale
    prob_mat = jnp.exp(scores - lse_rows[..., None])
    if pos_pair is not None:
        prob_mat = causal_where(pos_pair, prob_mat, 0.0)
    d_probs = jnp.einsum("qhgd,khd->qhgk", do_rows, v_blk, preferred_element_type=jnp.float32)
    d_scores = (prob_mat * (d_probs - dot_rows[..., None])).astype(jnp.bfloat16)
    dv_part = jnp.einsum("qhgk,qhgd->khd", prob_mat.astype(jnp.bfloat16), do_rows, preferred_element_type=jnp.float32)
    dk_part = jnp.einsum("qhgk,qhgd->khd", d_scores, q_rows, preferred_element_type=jnp.float32) * attn_scale
    dq_part = jnp.einsum("qhgk,khd->qhgd", d_scores, k_blk, preferred_element_type=jnp.float32) * attn_scale
    return dq_part, dk_part, dv_part


def forward_branches(q_cur, half_rows, k_blk, v_blk):
    def from_earlier(state_old):
        return attend_update(state_old, q_cur, k_blk[:half_rows], v_blk[:half_rows], None)

    def from_later(state_old):
        tail_old = tuple(arr_part[half_rows:] for arr_part in state_old)
        tail_new = attend_update(tail_old, q_cur[half_rows:], k_blk, v_blk, None)
        return tuple(jnp.concatenate([old_part[:half_rows], new_part]) for old_part, new_part in zip(state_old, tail_new))

    return from_earlier, from_later


def backward_branches(q_cur, do_cur, log_norm, row_dots, half_rows, k_blk, v_blk):
    def from_earlier(grads_old):
        dq_old, dk_old, dv_old = grads_old
        dq_part, dk_part, dv_part = grad_update(q_cur, do_cur, log_norm, row_dots, k_blk[:half_rows], v_blk[:half_rows], None)
        return (dq_old + dq_part,
                jnp.concatenate([dk_old[:half_rows] + dk_part, dk_old[half_rows:]]),
                jnp.concatenate([dv_old[:half_rows] + dv_part, dv_old[half_rows:]]))

    def from_later(grads_old):
        dq_old, dk_old, dv_old = grads_old
        dq_part, dk_part, dv_part = grad_update(q_cur[half_rows:], do_cur[half_rows:], log_norm[half_rows:], row_dots[half_rows:], k_blk, v_blk, None)
        return (jnp.concatenate([dq_old[:half_rows], dq_old[half_rows:] + dq_part]), dk_old + dk_part, dv_old + dv_part)

    return from_earlier, from_later


def solution(mesh):
    seq_shards = mesh.shape["cp"]
    send_perm = [(src_idx, (src_idx + 1) % seq_shards) for src_idx in range(seq_shards)]

    def device_fn(x_blk, w_query, w_key, w_value, w_out, dy_blk):
        my_rank = lax.axis_index("cp")
        model_dim, q_heads, head_dim = w_query.shape
        kv_heads = w_key.shape[1]
        groups = q_heads // kv_heads
        wq_flat = w_query.reshape(model_dim, q_heads * head_dim)
        wk_flat = w_key.reshape(model_dim, kv_heads * head_dim)
        wv_flat = w_value.reshape(model_dim, kv_heads * head_dim)
        wo_flat = w_out.reshape(q_heads * head_dim, model_dim)

        x_rows = lax.all_gather(x_blk, "tp", axis=0, tiled=True)
        n_rows = x_rows.shape[0]
        half_rows = n_rows // 2
        q_cur = jnp.dot(x_rows, wq_flat, preferred_element_type=jnp.float32).astype(jnp.bfloat16).reshape(n_rows, kv_heads, groups, head_dim)
        k_own = jnp.dot(x_rows, wk_flat, preferred_element_type=jnp.float32).astype(jnp.bfloat16).reshape(n_rows, kv_heads, head_dim)
        v_own = jnp.dot(x_rows, wv_flat, preferred_element_type=jnp.float32).astype(jnp.bfloat16).reshape(n_rows, kv_heads, head_dim)
        offsets = jnp.arange(half_rows, dtype=jnp.int32)
        positions = jnp.concatenate([my_rank * half_rows + offsets, (2 * seq_shards - 1 - my_rank) * half_rows + offsets])
        own_pair = (positions, positions)

        stat_shape = (n_rows, kv_heads, groups)
        softmax_state = (jnp.full(stat_shape, -jnp.inf, jnp.float32), jnp.zeros(stat_shape, jnp.float32), jnp.zeros(q_cur.shape, jnp.float32))
        softmax_state = attend_update(softmax_state, q_cur, k_own, v_own, own_pair)

        def forward_step(step_idx, loop_carry):
            k_blk, v_blk, state_in = loop_carry
            k_blk = lax.ppermute(k_blk, "cp", send_perm)
            v_blk = lax.ppermute(v_blk, "cp", send_perm)
            source = (my_rank - step_idx) % seq_shards
            from_earlier, from_later = forward_branches(q_cur, half_rows, k_blk, v_blk)
            return k_blk, v_blk, lax.cond(source < my_rank, from_earlier, from_later, state_in)

        softmax_state = lax.fori_loop(1, seq_shards, forward_step, (k_own, v_own, softmax_state))[2]
        row_max, row_sum, out_acc = softmax_state
        log_norm = row_max + jnp.log(row_sum)
        o_cur = (out_acc / row_sum[..., None]).astype(jnp.bfloat16)
        o_flat = o_cur.reshape(n_rows, q_heads * head_dim)
        y_part = jnp.dot(o_flat, wo_flat, preferred_element_type=jnp.float32)
        y_blk = lax.psum_scatter(y_part, "tp", scatter_dimension=0, tiled=True).astype(jnp.bfloat16)

        dy_rows = lax.all_gather(dy_blk, "tp", axis=0, tiled=True)
        do_cur = lax.dot_general(dy_rows, wo_flat, COLS_CONTRACT, preferred_element_type=jnp.float32).astype(jnp.bfloat16).reshape(q_cur.shape)
        row_dots = jnp.sum(do_cur.astype(jnp.float32) * o_cur.astype(jnp.float32), axis=-1)
        dq_acc, dk_own, dv_own = grad_update(q_cur, do_cur, log_norm, row_dots, k_own, v_own, own_pair)

        def backward_step(step_idx, loop_carry):
            k_blk, v_blk, dk_blk, dv_blk, dq_in = loop_carry
            k_blk = lax.ppermute(k_blk, "cp", send_perm)
            v_blk = lax.ppermute(v_blk, "cp", send_perm)
            dk_blk = lax.ppermute(dk_blk, "cp", send_perm)
            dv_blk = lax.ppermute(dv_blk, "cp", send_perm)
            source = (my_rank - step_idx) % seq_shards
            from_earlier, from_later = backward_branches(q_cur, do_cur, log_norm, row_dots, half_rows, k_blk, v_blk)
            dq_out, dk_out, dv_out = lax.cond(source < my_rank, from_earlier, from_later, (dq_in, dk_blk, dv_blk))
            return k_blk, v_blk, dk_out, dv_out, dq_out

        loop_out = lax.fori_loop(1, seq_shards, backward_step, (k_own, v_own, dk_own, dv_own, dq_acc))
        dk_home = lax.ppermute(loop_out[2], "cp", send_perm)
        dv_home = lax.ppermute(loop_out[3], "cp", send_perm)
        dq_flat = loop_out[4].astype(jnp.bfloat16).reshape(n_rows, q_heads * head_dim)
        dk_flat = dk_home.astype(jnp.bfloat16).reshape(n_rows, kv_heads * head_dim)
        dv_flat = dv_home.astype(jnp.bfloat16).reshape(n_rows, kv_heads * head_dim)
        dx_part = (lax.dot_general(dq_flat, wq_flat, COLS_CONTRACT, preferred_element_type=jnp.float32)
                   + lax.dot_general(dk_flat, wk_flat, COLS_CONTRACT, preferred_element_type=jnp.float32)
                   + lax.dot_general(dv_flat, wv_flat, COLS_CONTRACT, preferred_element_type=jnp.float32))
        dx_blk = lax.psum_scatter(dx_part, "tp", scatter_dimension=0, tiled=True).astype(jnp.bfloat16)
        grad_wq = lax.dot_general(x_rows, dq_flat, ROWS_CONTRACT, preferred_element_type=jnp.float32).astype(jnp.bfloat16).reshape(model_dim, q_heads, head_dim)
        grad_wk = lax.dot_general(x_rows, dk_flat, ROWS_CONTRACT, preferred_element_type=jnp.float32).astype(jnp.bfloat16).reshape(model_dim, kv_heads, head_dim)
        grad_wv = lax.dot_general(x_rows, dv_flat, ROWS_CONTRACT, preferred_element_type=jnp.float32).astype(jnp.bfloat16).reshape(model_dim, kv_heads, head_dim)
        grad_wo = lax.dot_general(o_flat, dy_rows, ROWS_CONTRACT, preferred_element_type=jnp.float32).astype(jnp.bfloat16).reshape(q_heads, head_dim, model_dim)
        return y_blk, dx_blk, grad_wq[None], grad_wk[None], grad_wv[None], grad_wo[None]

    return jax.shard_map(device_fn, mesh=mesh,
                         in_specs=(ROW_SPEC, HEAD_SPEC, HEAD_SPEC, HEAD_SPEC, OUT_W_SPEC, ROW_SPEC),
                         out_specs=(ROW_SPEC, ROW_SPEC, GRAD_SPEC, GRAD_SPEC, GRAD_SPEC, GRAD_OUT_SPEC),
                         check_vma=False)
```

profile of v0, /device:TPU:97, one launch (start us, length us, event | category | flops | bytes accessed | tf_op | source)
XLA Modules:
  0.0 435.3 jit_solution(13215141205675425006)
XLA Ops:
  9.0 23.7 %all-gather.5.cloned.1.call-done = bf16[128,4096]{1,0:T(8,128)(2,1)} async-done(((bf16[32,4096]{1,0:T(8,128)(2,1)}), bf16[128,4096]{1,0:T(8,128)(2,1)}) %all-gather.5.cloned.1.call-update) | async-done | bytes 1048592 | tf_op jit(solution)/shard_map/all_gather | solution.py:120
  32.7 6.6 %convolution_convert_fusion.4 = bf16[128,1024]{1,0:T(8,128)(2,1)S(1)} fusion(bf16[128,4096]{1,0:T(8,128)(2,1)} %all-gather.5.cloned.1.call-done, bf16[1024,4096]{1,0:T(8,128)(2,1)} %bitcast.313), kind=kOutput, calls=%fused_computation.132 | convolution fusion | flops 1073872896 | bytes 9699328 | tf_op jit(solution)/shard_map/dot_general | solution.py:121
  40.3 15.8 %all-gather.3.cloned.1.call-done = bf16[128,4096]{1,0:T(8,128)(2,1)} async-done(((bf16[32,4096]{1,0:T(8,128)(2,1)}), bf16[128,4096]{1,0:T(8,128)(2,1)}) %all-gather.3.cloned.1.call-update) | async-done | bytes 1048592 | tf_op jit(solution)/shard_map/all_gather | solution.py:90
  56.2 5.1 %fusion.109 = bf16[16,8,8,128]{3,2,1,0:T(8,128)(2,1)S(1)} fusion(bf16[128,4096]{1,0:T(8,128)(2,1)} %all-gather.3.cloned.1.call-done, bf16[512,8,8,128]{3,2,1,0:T(8,128)(2,1)} %bitcast.320), kind=kOutput, calls=%fused_computation.134 | convolution fusion | flops 1073872896 | bytes 9699328 | tf_op jit(solution)/shard_map/dot_general | solution.py:95
  61.3 4.8 %fusion.112 = bf16[16,8,8,128]{3,2,1,0:T(8,128)(2,1)S(1)} fusion(bf16[128,4096]{1,0:T(8,128)(2,1)S(1)} %copy-done, bf16[512,8,8,128]{3,2,1,0:T(8,128)(2,1)} %bitcast.319), kind=kOutput, calls=%fused_computation.135 | convolution fusion | flops 1073872896 | bytes 9699328 | tf_op jit(solution)/shard_map/dot_general | solution.py:94
  70.6 92.5 %while.46 = (s32[]{:T(128)}, bf16[128,8,128]{2,0,1:T(8,128)(2,1)}, bf16[128,8,128]{2,0,1:T(8,128)(2,1)}, f32[128,8,1]{0,1,2:T(8,128)S(1)}, f32[128,8,1]{0,1,2:T(...) while((s32[]{:T(128)}, bf16[128,8,128]{2,0,1:T(8,128)(2,1)}, ...), condition=%wide.region_9.10_spmd, body=%wide.region_2.9_spmd.sunk | while | flops 34213392 | bytes 6746564 | solution.py:112
  70.6 4.0 collective-permute-start
  74.7 3.2 collective-permute-done
  77.9 2.8 collective-permute-done.1
  80.7 3.4 conditional.4
  86.3 2.5 collective-permute-start
  88.8 3.3 collective-permute-done
  92.1 2.8 collective-permute-done.1
  98.8 4.1 collective-permute-start
  103.0 3.3 collective-permute-done
  106.2 2.8 collective-permute-done.1
  113.0 2.5 collective-permute-start
  116.2 2.6 collective-permute-done
  118.8 2.8 collective-permute-done.1
  125.5 2.5 collective-permute-start
  128.7 2.6 collective-permute-done
  131.3 2.8 collective-permute-done.1
  138.0 2.5 collective-permute-start
  143.8 2.8 collective-permute-done.1
  150.6 2.5 collective-permute-start
  164.4 6.1 %fusion.133 = f32[128,4096]{1,0:T(8,128)} fusion(bf16[128,1024]{0,1:T(8,128)(2,1)S(1)} %bitcast.324, bf16[1024,4096]{1,0:T(8,128)(2,1)} %bitcast.314), kind=kOutput, calls=%fused_computation.166 | convolution fusion | flops 1073741824 | bytes 10747904 | tf_op jit(solution)/shard_map/dot_general | solution.py:117
  175.1 159.9 %while.47 = (s32[]{:T(128)}, bf16[128,8,128]{2,0,1:T(8,128)(2,1)}, bf16[128,8,128]{2,0,1:T(8,128)(2,1)S(1)}, f32[128,8,128]{2,0,1:T(8,128)}, f32[128,8,128]{2,0,...) while((s32[]{:T(128)}, bf16[128,8,128]{2,0,1:T(8,128)(2,1)}, ...), condition=%wide.region_15.16_spmd, body=%wide.region_12.15_spmd.sunk | while | flops 85000208 | bytes 15213148 | solution.py:136
  175.3 2.6 collective-permute-start.4
  180.2 2.5 collective-permute-start.2
  184.8 7.7 %collective-permute-done.2 = bf16[128,8,128]{2,0,1:T(8,128)(2,1)S(1)} collective-permute-done((bf16[128,8,128]{2,0,1:T(8,128)(2,1)}, bf16[128,8,128]{2,0,1:T(8,128)(2,1)S(1)}, u32[]{:S(2)}, u32[]{:S(2)}) %collective-permute-start.2) | collective-permute-done | bytes 262176 | tf_op jit(solution)/shard_map/while/body/eval_jaxpr/ppermute | solution.py:127
  197.7 2.5 collective-permute-start.4
  202.5 2.5 collective-permute-start.2
  207.1 7.6 %collective-permute-done.2 = bf16[128,8,128]{2,0,1:T(8,128)(2,1)S(1)} collective-permute-done((bf16[128,8,128]{2,0,1:T(8,128)(2,1)}, bf16[128,8,128]{2,0,1:T(8,128)(2,1)S(1)}, u32[]{:S(2)}, u32[]{:S(2)}) %collective-permute-start.2) | collective-permute-done | bytes 262176 | tf_op jit(solution)/shard_map/while/body/eval_jaxpr/ppermute | solution.py:127
  217.6 3.1 conditional.5
  224.9 2.5 collective-permute-start.2
  229.4 7.6 %collective-permute-done.2 = bf16[128,8,128]{2,0,1:T(8,128)(2,1)S(1)} collective-permute-done((bf16[128,8,128]{2,0,1:T(8,128)(2,1)}, bf16[128,8,128]{2,0,1:T(8,128)(2,1)S(1)}, u32[]{:S(2)}, u32[]{:S(2)}) %collective-permute-start.2) | collective-permute-done | bytes 262176 | tf_op jit(solution)/shard_map/while/body/eval_jaxpr/ppermute | solution.py:127
  239.9 3.1 conditional.5
  243.0 2.5 collective-permute-start.4
  247.2 2.5 collective-permute-start.2
  251.8 8.3 %collective-permute-done.2 = bf16[128,8,128]{2,0,1:T(8,128)(2,1)S(1)} collective-permute-done((bf16[128,8,128]{2,0,1:T(8,128)(2,1)}, bf16[128,8,128]{2,0,1:T(8,128)(2,1)S(1)}, u32[]{:S(2)}, u32[]{:S(2)}) %collective-permute-start.2) | collective-permute-done | bytes 262176 | tf_op jit(solution)/shard_map/while/body/eval_jaxpr/ppermute | solution.py:127
  262.9 3.1 conditional.5
  266.1 2.5 collective-permute-start.4
  274.1 9.0 %collective-permute-done.2 = bf16[128,8,128]{2,0,1:T(8,128)(2,1)S(1)} collective-permute-done((bf16[128,8,128]{2,0,1:T(8,128)(2,1)}, bf16[128,8,128]{2,0,1:T(8,128)(2,1)S(1)}, u32[]{:S(2)}, u32[]{:S(2)}) %collective-permute-start.2) | collective-permute-done | bytes 262176 | tf_op jit(solution)/shard_map/while/body/eval_jaxpr/ppermute | solution.py:127
  285.9 3.1 conditional.5
  289.1 2.5 collective-permute-start.4
  292.6 2.5 collective-permute-start.2
  296.4 9.7 %collective-permute-done.2 = bf16[128,8,128]{2,0,1:T(8,128)(2,1)S(1)} collective-permute-done((bf16[128,8,128]{2,0,1:T(8,128)(2,1)}, bf16[128,8,128]{2,0,1:T(8,128)(2,1)S(1)}, u32[]{:S(2)}, u32[]{:S(2)}) %collective-permute-start.2) | collective-permute-done | bytes 262176 | tf_op jit(solution)/shard_map/while/body/eval_jaxpr/ppermute | solution.py:127
  308.9 3.1 conditional.5
  312.1 2.5 collective-permute-start.4
  315.6 2.5 collective-permute-start.2
  319.4 10.4 %collective-permute-done.2 = bf16[128,8,128]{2,0,1:T(8,128)(2,1)S(1)} collective-permute-done((bf16[128,8,128]{2,0,1:T(8,128)(2,1)}, bf16[128,8,128]{2,0,1:T(8,128)(2,1)S(1)}, u32[]{:S(2)}, u32[]{:S(2)}) %collective-permute-start.2) | collective-permute-done | bytes 262176 | tf_op jit(solution)/shard_map/while/body/eval_jaxpr/ppermute | solution.py:127
  332.0 3.1 conditional.5
  336.3 2.6 collective-permute-start.6
  338.9 6.4 %fusion.64 = f32[128,4096]{1,0:T(8,128)S(1)} fusion(bf16[128,1024]{0,1:T(8,128)(2,1)S(1)} %bitcast.333, bf16[512,8,8,128]{3,2,1,0:T(8,128)(2,1)} %bitcast.347), kind=kOutput, calls=%fused_computation.92 | convolution fusion | flops 1073741824 | bytes 10747904 | tf_op jit(solution)/shard_map/dot_general | solution.py:142
  347.5 6.4 %collective-permute-done.6 = bf16[128,8,128]{2,0,1:T(8,128)(2,1)S(1)} collective-permute-done((bf16[128,8,128]{2,0,1:T(8,128)(2,1)S(1)}, bf16[128,8,128]{2,0,1:T(8,128)(2,1)S(1)}, u32[]{:S(2)}, u32[]{:S(2)}) %collective-permute-start.6) | collective-permute-done | bytes 262176 | tf_op jit(solution)/shard_map/ppermute | solution.py:137
  353.9 6.3 %fusion.89 = f32[128,4096]{1,0:T(8,128)S(1)} fusion(f32[128,4096]{1,0:T(8,128)S(1)} %fusion.64, bf16[128,8,128]{2,0,1:T(8,128)(2,1)S(1)} %collective-permute-done.6, bf16[4096,8,128]{2,1,0:T(8,128)(2,1)} %param.16), kind=kOutput, calls=%fused_computation.115 | convolution fusion | flops 1074266112 | bytes 12845056 | tf_op jit(solution)/shard_map/dot_general | solution.py:143
  361.5 4.3 fusion.86
  365.8 5.7 %convolution_convert_fusion.3 = bf16[1024,4096]{1,0:T(8,128)(2,1)} fusion(bf16[128,1024]{0,1:T(8,128)(2,1)S(1)} %bitcast.334, bf16[128,4096]{1,0:T(8,128)(2,1)S(1)} %copy-done.1), kind=kOutput, calls=%fused_computation.109 | convolution fusion | flops 1077936128 | bytes 9699328 | tf_op jit(solution)/shard_map/dot_general | solution.py:146
  371.6 12.1 %copy.71 = bf16[1,4096,8,128]{3,2,1,0:T(8,128)(2,1)} copy(bf16[1,4096,8,128]{1,3,2,0:T(8,128)(2,1)} %bitcast.316) | data formatting | bytes 16777216
  383.7 5.7 %convolution_convert_fusion = bf16[1024,4096]{1,0:T(8,128)(2,1)} fusion(bf16[128,1024]{0,1:T(8,128)(2,1)S(1)} %bitcast.325, bf16[128,4096]{1,0:T(8,128)(2,1)S(1)} %copy-done.2), kind=kOutput, calls=%fused_computation.106 | convolution fusion | flops 1077936128 | bytes 9699328 | tf_op jit(solution)/shard_map/dot_general | solution.py:149
  389.6 5.7 %convolution_convert_fusion.2 = bf16[1024,4096]{1,0:T(8,128)(2,1)} fusion(bf16[128,1024]{0,1:T(8,128)(2,1)S(1)} %bitcast.336, bf16[128,4096]{1,0:T(8,128)(2,1)S(1)} %copy-done.1), kind=kOutput, calls=%fused_computation.108 | convolution fusion | flops 1077936128 | bytes 9699328 | tf_op jit(solution)/shard_map/dot_general | solution.py:147
  395.3 12.0 %copy.72 = bf16[1,4096,8,128]{3,2,1,0:T(8,128)(2,1)} copy(bf16[1,4096,8,128]{1,3,2,0:T(8,128)(2,1)} %bitcast.317) | data formatting | bytes 16777216
  407.5 5.6 %convolution_convert_fusion.1 = bf16[1024,4096]{1,0:T(8,128)(2,1)} fusion(bf16[128,1024]{0,1:T(8,128)(2,1)S(1)} %bitcast.335, bf16[128,4096]{1,0:T(8,128)(2,1)S(1)} %copy-done.1), kind=kOutput, calls=%fused_computation.107 | convolution fusion | flops 1077936128 | bytes 9699328 | tf_op jit(solution)/shard_map/dot_general | solution.py:148
  413.1 12.0 %copy.73 = bf16[1,4096,8,128]{3,2,1,0:T(8,128)(2,1)} copy(bf16[1,4096,8,128]{1,3,2,0:T(8,128)(2,1)} %bitcast.315) | data formatting | bytes 16777216
  (271 shorter events, 143.4 us)
Async XLA Ops:
  7.2 25.5 %all-gather.5.cloned.1.call-start = ((), (), s32[]{:S(2)}) async-start(), calls=%async_computation.4 | async-start | bytes 1310720 | tf_op jit(solution)/shard_map/all_gather | solution.py:120
  8.0 48.2 %all-gather.3.cloned.1.call-start = ((), (), s32[]{:S(2)}) async-start(), calls=%async_computation.2 | async-start | bytes 1310720 | tf_op jit(solution)/shard_map/all_gather | solution.py:90
  8.8 416.4 %reduce-scatter.3.cloned.1.call-start = ((), (), s32[]{:S(2)}) async-start(), calls=%async_computation.3 | async-start | bytes 2621440 | tf_op jit(solution)/shard_map/reduce_scatter | solution.py:118
  56.2 5.1 %copy-start = (bf16[128,4096]{1,0:T(8,128)(2,1)S(1)}, bf16[128,4096]{1,0:T(8,128)(2,1)}, u32[]{:S(2)}) copy-start(bf16[128,4096]{1,0:T(8,128)(2,1)} %all-gather.3.cloned.1.call-done) | copy-start | bytes 3145732
  56.2 11.5 %slice-start.2 = ((s8[8388608]{0:T(1024)(128)(4,1)}), s8[4194304]{0:T(1024)(128)(4,1)S(1)}, s32[]{:S(2)}) async-start(s8[8388608]{0:T(1024)(128)(4,1)} %bitcast.348), calls=%async_computation.8 | async-start | bytes 8388608
  61.3 6.4 %slice-start.3 = ((s8[8388608]{0:T(1024)(128)(4,1)}), s8[4194304]{0:T(1024)(128)(4,1)S(1)}, s32[]{:S(2)}) async-start(s8[8388608]{0:T(1024)(128)(4,1)} %bitcast.348), calls=%async_computation.9 | async-start | bytes 8388608
  66.1 3.9 copy-start.6
  66.2 1.4 copy-start.3
  69.2 0.7 copy-start.4
  70.6 7.3 %collective-permute-start = (bf16[128,8,128]{2,0,1:T(8,128)(2,1)}, bf16[128,8,128]{2,0,1:T(8,128)(2,1)S(1)}, u32[]{:S(2)}, u32[]{:S(2)}) collective-permute-start(bf16[128,8,128]{2,0,1:T(8,128)(2,1)} %get-tuple-element.872), channel_id=1, source_target_pairs={{0,1},{1,2},{2,3},{3,4},{4,5},{5,6},{6,7},{7,0},{8,9},{9,10},{10,1... | collective-permute-start | bytes 786440 | tf_op jit(solution)/shard_map/while/body/eval_jaxpr/ppermute | solution.py:106
  74.6 6.1 %collective-permute-start.1 = (bf16[128,8,128]{2,0,1:T(8,128)(2,1)}, bf16[128,8,128]{2,0,1:T(8,128)(2,1)S(1)}, u32[]{:S(2)}, u32[]{:S(2)}) collective-permute-start(bf16[128,8,128]{2,0,1:T(8,128)(2,1)} %get-tuple-element.873), channel_id=1, source_target_pairs={{0,1},{1,2},{2,3},{3,4},{4,5},{5,6},{6,7},{7,0},{8,9},{9,10},{10,1... | collective-permute-start | bytes 786440 | tf_op jit(solution)/shard_map/while/body/eval_jaxpr/ppermute | solution.py:107
  86.3 5.8 %collective-permute-start = (bf16[128,8,128]{2,0,1:T(8,128)(2,1)}, bf16[128,8,128]{2,0,1:T(8,128)(2,1)S(1)}, u32[]{:S(2)}, u32[]{:S(2)}) collective-permute-start(bf16[128,8,128]{2,0,1:T(8,128)(2,1)} %get-tuple-element.872), channel_id=1, source_target_pairs={{0,1},{1,2},{2,3},{3,4},{4,5},{5,6},{6,7},{7,0},{8,9},{9,10},{10,1... | collective-permute-start | bytes 786440 | tf_op jit(solution)/shard_map/while/body/eval_jaxpr/ppermute | solution.py:106
  88.8 6.1 %collective-permute-start.1 = (bf16[128,8,128]{2,0,1:T(8,128)(2,1)}, bf16[128,8,128]{2,0,1:T(8,128)(2,1)S(1)}, u32[]{:S(2)}, u32[]{:S(2)}) collective-permute-start(bf16[128,8,128]{2,0,1:T(8,128)(2,1)} %get-tuple-element.873), channel_id=1, source_target_pairs={{0,1},{1,2},{2,3},{3,4},{4,5},{5,6},{6,7},{7,0},{8,9},{9,10},{10,1... | collective-permute-start | bytes 786440 | tf_op jit(solution)/shard_map/while/body/eval_jaxpr/ppermute | solution.py:107
  98.8 7.4 %collective-permute-start = (bf16[128,8,128]{2,0,1:T(8,128)(2,1)}, bf16[128,8,128]{2,0,1:T(8,128)(2,1)S(1)}, u32[]{:S(2)}, u32[]{:S(2)}) collective-permute-start(bf16[128,8,128]{2,0,1:T(8,128)(2,1)} %get-tuple-element.872), channel_id=1, source_target_pairs={{0,1},{1,2},{2,3},{3,4},{4,5},{5,6},{6,7},{7,0},{8,9},{9,10},{10,1... | collective-permute-start | bytes 786440 | tf_op jit(solution)/shard_map/while/body/eval_jaxpr/ppermute | solution.py:106
  103.0 6.1 %collective-permute-start.1 = (bf16[128,8,128]{2,0,1:T(8,128)(2,1)}, bf16[128,8,128]{2,0,1:T(8,128)(2,1)S(1)}, u32[]{:S(2)}, u32[]{:S(2)}) collective-permute-start(bf16[128,8,128]{2,0,1:T(8,128)(2,1)} %get-tuple-element.873), channel_id=1, source_target_pairs={{0,1},{1,2},{2,3},{3,4},{4,5},{5,6},{6,7},{7,0},{8,9},{9,10},{10,1... | collective-permute-start | bytes 786440 | tf_op jit(solution)/shard_map/while/body/eval_jaxpr/ppermute | solution.py:107
  113.0 5.8 %collective-permute-start = (bf16[128,8,128]{2,0,1:T(8,128)(2,1)}, bf16[128,8,128]{2,0,1:T(8,128)(2,1)S(1)}, u32[]{:S(2)}, u32[]{:S(2)}) collective-permute-start(bf16[128,8,128]{2,0,1:T(8,128)(2,1)} %get-tuple-element.872), channel_id=1, source_target_pairs={{0,1},{1,2},{2,3},{3,4},{4,5},{5,6},{6,7},{7,0},{8,9},{9,10},{10,1... | collective-permute-start | bytes 786440 | tf_op jit(solution)/shard_map/while/body/eval_jaxpr/ppermute | solution.py:106
  115.5 6.1 %collective-permute-start.1 = (bf16[128,8,128]{2,0,1:T(8,128)(2,1)}, bf16[128,8,128]{2,0,1:T(8,128)(2,1)S(1)}, u32[]{:S(2)}, u32[]{:S(2)}) collective-permute-start(bf16[128,8,128]{2,0,1:T(8,128)(2,1)} %get-tuple-element.873), channel_id=1, source_target_pairs={{0,1},{1,2},{2,3},{3,4},{4,5},{5,6},{6,7},{7,0},{8,9},{9,10},{10,1... | collective-permute-start | bytes 786440 | tf_op jit(solution)/shard_map/while/body/eval_jaxpr/ppermute | solution.py:107
  125.5 5.8 %collective-permute-start = (bf16[128,8,128]{2,0,1:T(8,128)(2,1)}, bf16[128,8,128]{2,0,1:T(8,128)(2,1)S(1)}, u32[]{:S(2)}, u32[]{:S(2)}) collective-permute-start(bf16[128,8,128]{2,0,1:T(8,128)(2,1)} %get-tuple-element.872), channel_id=1, source_target_pairs={{0,1},{1,2},{2,3},{3,4},{4,5},{5,6},{6,7},{7,0},{8,9},{9,10},{10,1... | collective-permute-start | bytes 786440 | tf_op jit(solution)/shard_map/while/body/eval_jaxpr/ppermute | solution.py:106
  128.0 6.1 %collective-permute-start.1 = (bf16[128,8,128]{2,0,1:T(8,128)(2,1)}, bf16[128,8,128]{2,0,1:T(8,128)(2,1)S(1)}, u32[]{:S(2)}, u32[]{:S(2)}) collective-permute-start(bf16[128,8,128]{2,0,1:T(8,128)(2,1)} %get-tuple-element.873), channel_id=1, source_target_pairs={{0,1},{1,2},{2,3},{3,4},{4,5},{5,6},{6,7},{7,0},{8,9},{9,10},{10,1... | collective-permute-start | bytes 786440 | tf_op jit(solution)/shard_map/while/body/eval_jaxpr/ppermute | solution.py:107
  138.0 5.8 %collective-permute-start = (bf16[128,8,128]{2,0,1:T(8,128)(2,1)}, bf16[128,8,128]{2,0,1:T(8,128)(2,1)S(1)}, u32[]{:S(2)}, u32[]{:S(2)}) collective-permute-start(bf16[128,8,128]{2,0,1:T(8,128)(2,1)} %get-tuple-element.872), channel_id=1, source_target_pairs={{0,1},{1,2},{2,3},{3,4},{4,5},{5,6},{6,7},{7,0},{8,9},{9,10},{10,1... | collective-permute-start | bytes 786440 | tf_op jit(solution)/shard_map/while/body/eval_jaxpr/ppermute | solution.py:106
  140.5 6.1 %collective-permute-start.1 = (bf16[128,8,128]{2,0,1:T(8,128)(2,1)}, bf16[128,8,128]{2,0,1:T(8,128)(2,1)S(1)}, u32[]{:S(2)}, u32[]{:S(2)}) collective-permute-start(bf16[128,8,128]{2,0,1:T(8,128)(2,1)} %get-tuple-element.873), channel_id=1, source_target_pairs={{0,1},{1,2},{2,3},{3,4},{4,5},{5,6},{6,7},{7,0},{8,9},{9,10},{10,1... | collective-permute-start | bytes 786440 | tf_op jit(solution)/shard_map/while/body/eval_jaxpr/ppermute | solution.py:107
  150.6 6.5 %collective-permute-start = (bf16[128,8,128]{2,0,1:T(8,128)(2,1)}, bf16[128,8,128]{2,0,1:T(8,128)(2,1)S(1)}, u32[]{:S(2)}, u32[]{:S(2)}) collective-permute-start(bf16[128,8,128]{2,0,1:T(8,128)(2,1)} %get-tuple-element.872), channel_id=1, source_target_pairs={{0,1},{1,2},{2,3},{3,4},{4,5},{5,6},{6,7},{7,0},{8,9},{9,10},{10,1... | collective-permute-start | bytes 786440 | tf_op jit(solution)/shard_map/while/body/eval_jaxpr/ppermute | solution.py:106
  153.1 6.1 %collective-permute-start.1 = (bf16[128,8,128]{2,0,1:T(8,128)(2,1)}, bf16[128,8,128]{2,0,1:T(8,128)(2,1)S(1)}, u32[]{:S(2)}, u32[]{:S(2)}) collective-permute-start(bf16[128,8,128]{2,0,1:T(8,128)(2,1)} %get-tuple-element.873), channel_id=1, source_target_pairs={{0,1},{1,2},{2,3},{3,4},{4,5},{5,6},{6,7},{7,0},{8,9},{9,10},{10,1... | collective-permute-start | bytes 786440 | tf_op jit(solution)/shard_map/while/body/eval_jaxpr/ppermute | solution.py:107
  164.4 6.7 %copy-start.5 = (bf16[128,1024]{0,1:T(8,128)(2,1)S(1)}, bf16[128,1024]{0,1:T(8,128)(2,1)}, u32[]{:S(2)}) copy-start(bf16[128,1024]{0,1:T(8,128)(2,1)} %copy-done.4) | copy-start | bytes 786436
  170.5 256.4 %reduce-scatter.5.cloned.1.call-start = ((), (), s32[]{:S(2)}) async-start(), calls=%async_computation.5 | async-start | bytes 2621440 | tf_op jit(solution)/shard_map/reduce_scatter | solution.py:145
  175.3 19.9 %collective-permute-start.4 = (f32[128,8,128]{2,0,1:T(8,128)}, f32[128,8,128]{2,0,1:T(8,128)S(1)}, u32[]{:S(2)}, u32[]{:S(2)}) collective-permute-start(f32[128,8,128]{2,0,1:T(8,128)} %get-tuple-element.913), channel_id=1, source_target_pairs={{0,1},{1,2},{2,3},{3,4},{4,5},{5,6},{6,7},{7,0},{8,9},{9,10},{10,1... | collective-permute-start | bytes 1572872 | tf_op jit(solution)/shard_map/while/body/eval_jaxpr/ppermute | solution.py:129
  177.9 17.4 %collective-permute-start.5 = (f32[128,8,128]{2,0,1:T(8,128)}, f32[128,8,128]{2,0,1:T(8,128)S(1)}, u32[]{:S(2)}, u32[]{:S(2)}) collective-permute-start(f32[128,8,128]{2,0,1:T(8,128)} %get-tuple-element.914), channel_id=1, source_target_pairs={{0,1},{1,2},{2,3},{3,4},{4,5},{5,6},{6,7},{7,0},{8,9},{9,10},{10,1... | collective-permute-start | bytes 1572872 | tf_op jit(solution)/shard_map/while/body/eval_jaxpr/ppermute | solution.py:130
  180.2 12.2 %collective-permute-start.2 = (bf16[128,8,128]{2,0,1:T(8,128)(2,1)}, bf16[128,8,128]{2,0,1:T(8,128)(2,1)S(1)}, u32[]{:S(2)}, u32[]{:S(2)}) collective-permute-start(bf16[128,8,128]{2,0,1:T(8,128)(2,1)} %get-tuple-element.911), channel_id=1, source_target_pairs={{0,1},{1,2},{2,3},{3,4},{4,5},{5,6},{6,7},{7,0},{8,9},{9,10},{10,1... | collective-permute-start | bytes 786440 | tf_op jit(solution)/shard_map/while/body/eval_jaxpr/ppermute | solution.py:127
  182.7 12.5 %collective-permute-start.3 = (bf16[128,8,128]{2,0,1:T(8,128)(2,1)S(1)}, bf16[128,8,128]{2,0,1:T(8,128)(2,1)S(1)}, u32[]{:S(2)}, u32[]{:S(2)}) collective-permute-start(bf16[128,8,128]{2,0,1:T(8,128)(2,1)S(1)} %get-tuple-element.912), channel_id=1, source_target_pairs={{0,1},{1,2},{2,3},{3,4},{4,5},{5,6},{6,7},{7,0},{8,9},{9,10},{10,1... | collective-permute-start | bytes 786440 | tf_op jit(solution)/shard_map/while/body/eval_jaxpr/ppermute | solution.py:128
  197.7 19.9 %collective-permute-start.4 = (f32[128,8,128]{2,0,1:T(8,128)}, f32[128,8,128]{2,0,1:T(8,128)S(1)}, u32[]{:S(2)}, u32[]{:S(2)}) collective-permute-start(f32[128,8,128]{2,0,1:T(8,128)} %get-tuple-element.913), channel_id=1, source_target_pairs={{0,1},{1,2},{2,3},{3,4},{4,5},{5,6},{6,7},{7,0},{8,9},{9,10},{10,1... | collective-permute-start | bytes 1572872 | tf_op jit(solution)/shard_map/while/body/eval_jaxpr/ppermute | solution.py:129
  200.2 17.4 %collective-permute-start.5 = (f32[128,8,128]{2,0,1:T(8,128)}, f32[128,8,128]{2,0,1:T(8,128)S(1)}, u32[]{:S(2)}, u32[]{:S(2)}) collective-permute-start(f32[128,8,128]{2,0,1:T(8,128)} %get-tuple-element.914), channel_id=1, source_target_pairs={{0,1},{1,2},{2,3},{3,4},{4,5},{5,6},{6,7},{7,0},{8,9},{9,10},{10,1... | collective-permute-start | bytes 1572872 | tf_op jit(solution)/shard_map/while/body/eval_jaxpr/ppermute | solution.py:130
  202.5 12.2 %collective-permute-start.2 = (bf16[128,8,128]{2,0,1:T(8,128)(2,1)}, bf16[128,8,128]{2,0,1:T(8,128)(2,1)S(1)}, u32[]{:S(2)}, u32[]{:S(2)}) collective-permute-start(bf16[128,8,128]{2,0,1:T(8,128)(2,1)} %get-tuple-element.911), channel_id=1, source_target_pairs={{0,1},{1,2},{2,3},{3,4},{4,5},{5,6},{6,7},{7,0},{8,9},{9,10},{10,1... | collective-permute-start | bytes 786440 | tf_op jit(solution)/shard_map/while/body/eval_jaxpr/ppermute | solution.py:127
  205.1 12.5 %collective-permute-start.3 = (bf16[128,8,128]{2,0,1:T(8,128)(2,1)S(1)}, bf16[128,8,128]{2,0,1:T(8,128)(2,1)S(1)}, u32[]{:S(2)}, u32[]{:S(2)}) collective-permute-start(bf16[128,8,128]{2,0,1:T(8,128)(2,1)S(1)} %get-tuple-element.912), channel_id=1, source_target_pairs={{0,1},{1,2},{2,3},{3,4},{4,5},{5,6},{6,7},{7,0},{8,9},{9,10},{10,1... | collective-permute-start | bytes 786440 | tf_op jit(solution)/shard_map/while/body/eval_jaxpr/ppermute | solution.py:128
  220.7 19.2 %collective-permute-start.4 = (f32[128,8,128]{2,0,1:T(8,128)}, f32[128,8,128]{2,0,1:T(8,128)S(1)}, u32[]{:S(2)}, u32[]{:S(2)}) collective-permute-start(f32[128,8,128]{2,0,1:T(8,128)} %get-tuple-element.913), channel_id=1, source_target_pairs={{0,1},{1,2},{2,3},{3,4},{4,5},{5,6},{6,7},{7,0},{8,9},{9,10},{10,1... | collective-permute-start | bytes 1572872 | tf_op jit(solution)/shard_map/while/body/eval_jaxpr/ppermute | solution.py:129
  222.5 17.4 %collective-permute-start.5 = (f32[128,8,128]{2,0,1:T(8,128)}, f32[128,8,128]{2,0,1:T(8,128)S(1)}, u32[]{:S(2)}, u32[]{:S(2)}) collective-permute-start(f32[128,8,128]{2,0,1:T(8,128)} %get-tuple-element.914), channel_id=1, source_target_pairs={{0,1},{1,2},{2,3},{3,4},{4,5},{5,6},{6,7},{7,0},{8,9},{9,10},{10,1... | collective-permute-start | bytes 1572872 | tf_op jit(solution)/shard_map/while/body/eval_jaxpr/ppermute | solution.py:130
  224.9 12.2 %collective-permute-start.2 = (bf16[128,8,128]{2,0,1:T(8,128)(2,1)}, bf16[128,8,128]{2,0,1:T(8,128)(2,1)S(1)}, u32[]{:S(2)}, u32[]{:S(2)}) collective-permute-start(bf16[128,8,128]{2,0,1:T(8,128)(2,1)} %get-tuple-element.911), channel_id=1, source_target_pairs={{0,1},{1,2},{2,3},{3,4},{4,5},{5,6},{6,7},{7,0},{8,9},{9,10},{10,1... | collective-permute-start | bytes 786440 | tf_op jit(solution)/shard_map/while/body/eval_jaxpr/ppermute | solution.py:127
  227.4 12.5 %collective-permute-start.3 = (bf16[128,8,128]{2,0,1:T(8,128)(2,1)S(1)}, bf16[128,8,128]{2,0,1:T(8,128)(2,1)S(1)}, u32[]{:S(2)}, u32[]{:S(2)}) collective-permute-start(bf16[128,8,128]{2,0,1:T(8,128)(2,1)S(1)} %get-tuple-element.912), channel_id=1, source_target_pairs={{0,1},{1,2},{2,3},{3,4},{4,5},{5,6},{6,7},{7,0},{8,9},{9,10},{10,1... | collective-permute-start | bytes 786440 | tf_op jit(solution)/shard_map/while/body/eval_jaxpr/ppermute | solution.py:128
  243.0 19.9 %collective-permute-start.4 = (f32[128,8,128]{2,0,1:T(8,128)}, f32[128,8,128]{2,0,1:T(8,128)S(1)}, u32[]{:S(2)}, u32[]{:S(2)}) collective-permute-start(f32[128,8,128]{2,0,1:T(8,128)} %get-tuple-element.913), channel_id=1, source_target_pairs={{0,1},{1,2},{2,3},{3,4},{4,5},{5,6},{6,7},{7,0},{8,9},{9,10},{10,1... | collective-permute-start | bytes 1572872 | tf_op jit(solution)/shard_map/while/body/eval_jaxpr/ppermute | solution.py:129
  245.5 17.4 %collective-permute-start.5 = (f32[128,8,128]{2,0,1:T(8,128)}, f32[128,8,128]{2,0,1:T(8,128)S(1)}, u32[]{:S(2)}, u32[]{:S(2)}) collective-permute-start(f32[128,8,128]{2,0,1:T(8,128)} %get-tuple-element.914), channel_id=1, source_target_pairs={{0,1},{1,2},{2,3},{3,4},{4,5},{5,6},{6,7},{7,0},{8,9},{9,10},{10,1... | collective-permute-start | bytes 1572872 | tf_op jit(solution)/shard_map/while/body/eval_jaxpr/ppermute | solution.py:130
  247.2 12.9 %collective-permute-start.2 = (bf16[128,8,128]{2,0,1:T(8,128)(2,1)}, bf16[128,8,128]{2,0,1:T(8,128)(2,1)S(1)}, u32[]{:S(2)}, u32[]{:S(2)}) collective-permute-start(bf16[128,8,128]{2,0,1:T(8,128)(2,1)} %get-tuple-element.911), channel_id=1, source_target_pairs={{0,1},{1,2},{2,3},{3,4},{4,5},{5,6},{6,7},{7,0},{8,9},{9,10},{10,1... | collective-permute-start | bytes 786440 | tf_op jit(solution)/shard_map/while/body/eval_jaxpr/ppermute | solution.py:127
  249.7 13.2 %collective-permute-start.3 = (bf16[128,8,128]{2,0,1:T(8,128)(2,1)S(1)}, bf16[128,8,128]{2,0,1:T(8,128)(2,1)S(1)}, u32[]{:S(2)}, u32[]{:S(2)}) collective-permute-start(bf16[128,8,128]{2,0,1:T(8,128)(2,1)S(1)} %get-tuple-element.912), channel_id=1, source_target_pairs={{0,1},{1,2},{2,3},{3,4},{4,5},{5,6},{6,7},{7,0},{8,9},{9,10},{10,1... | collective-permute-start | bytes 786440 | tf_op jit(solution)/shard_map/while/body/eval_jaxpr/ppermute | solution.py:128
  266.1 19.9 %collective-permute-start.4 = (f32[128,8,128]{2,0,1:T(8,128)}, f32[128,8,128]{2,0,1:T(8,128)S(1)}, u32[]{:S(2)}, u32[]{:S(2)}) collective-permute-start(f32[128,8,128]{2,0,1:T(8,128)} %get-tuple-element.913), channel_id=1, source_target_pairs={{0,1},{1,2},{2,3},{3,4},{4,5},{5,6},{6,7},{7,0},{8,9},{9,10},{10,1... | collective-permute-start | bytes 1572872 | tf_op jit(solution)/shard_map/while/body/eval_jaxpr/ppermute | solution.py:129
  268.6 17.4 %collective-permute-start.5 = (f32[128,8,128]{2,0,1:T(8,128)}, f32[128,8,128]{2,0,1:T(8,128)S(1)}, u32[]{:S(2)}, u32[]{:S(2)}) collective-permute-start(f32[128,8,128]{2,0,1:T(8,128)} %get-tuple-element.914), channel_id=1, source_target_pairs={{0,1},{1,2},{2,3},{3,4},{4,5},{5,6},{6,7},{7,0},{8,9},{9,10},{10,1... | collective-permute-start | bytes 1572872 | tf_op jit(solution)/shard_map/while/body/eval_jaxpr/ppermute | solution.py:130
  270.2 12.9 %collective-permute-start.2 = (bf16[128,8,128]{2,0,1:T(8,128)(2,1)}, bf16[128,8,128]{2,0,1:T(8,128)(2,1)S(1)}, u32[]{:S(2)}, u32[]{:S(2)}) collective-permute-start(bf16[128,8,128]{2,0,1:T(8,128)(2,1)} %get-tuple-element.911), channel_id=1, source_target_pairs={{0,1},{1,2},{2,3},{3,4},{4,5},{5,6},{6,7},{7,0},{8,9},{9,10},{10,1... | collective-permute-start | bytes 786440 | tf_op jit(solution)/shard_map/while/body/eval_jaxpr/ppermute | solution.py:127
  272.1 13.8 %collective-permute-start.3 = (bf16[128,8,128]{2,0,1:T(8,128)(2,1)S(1)}, bf16[128,8,128]{2,0,1:T(8,128)(2,1)S(1)}, u32[]{:S(2)}, u32[]{:S(2)}) collective-permute-start(bf16[128,8,128]{2,0,1:T(8,128)(2,1)S(1)} %get-tuple-element.912), channel_id=1, source_target_pairs={{0,1},{1,2},{2,3},{3,4},{4,5},{5,6},{6,7},{7,0},{8,9},{9,10},{10,1... | collective-permute-start | bytes 786440 | tf_op jit(solution)/shard_map/while/body/eval_jaxpr/ppermute | solution.py:128
  289.1 19.9 %collective-permute-start.4 = (f32[128,8,128]{2,0,1:T(8,128)}, f32[128,8,128]{2,0,1:T(8,128)S(1)}, u32[]{:S(2)}, u32[]{:S(2)}) collective-permute-start(f32[128,8,128]{2,0,1:T(8,128)} %get-tuple-element.913), channel_id=1, source_target_pairs={{0,1},{1,2},{2,3},{3,4},{4,5},{5,6},{6,7},{7,0},{8,9},{9,10},{10,1... | collective-permute-start | bytes 1572872 | tf_op jit(solution)/shard_map/while/body/eval_jaxpr/ppermute | solution.py:129
  291.6 17.4 %collective-permute-start.5 = (f32[128,8,128]{2,0,1:T(8,128)}, f32[128,8,128]{2,0,1:T(8,128)S(1)}, u32[]{:S(2)}, u32[]{:S(2)}) collective-permute-start(f32[128,8,128]{2,0,1:T(8,128)} %get-tuple-element.914), channel_id=1, source_target_pairs={{0,1},{1,2},{2,3},{3,4},{4,5},{5,6},{6,7},{7,0},{8,9},{9,10},{10,1... | collective-permute-start | bytes 1572872 | tf_op jit(solution)/shard_map/while/body/eval_jaxpr/ppermute | solution.py:130
  292.6 13.5 %collective-permute-start.2 = (bf16[128,8,128]{2,0,1:T(8,128)(2,1)}, bf16[128,8,128]{2,0,1:T(8,128)(2,1)S(1)}, u32[]{:S(2)}, u32[]{:S(2)}) collective-permute-start(bf16[128,8,128]{2,0,1:T(8,128)(2,1)} %get-tuple-element.911), channel_id=1, source_target_pairs={{0,1},{1,2},{2,3},{3,4},{4,5},{5,6},{6,7},{7,0},{8,9},{9,10},{10,1... | collective-permute-start | bytes 786440 | tf_op jit(solution)/shard_map/while/body/eval_jaxpr/ppermute | solution.py:127
  295.1 13.8 %collective-permute-start.3 = (bf16[128,8,128]{2,0,1:T(8,128)(2,1)S(1)}, bf16[128,8,128]{2,0,1:T(8,128)(2,1)S(1)}, u32[]{:S(2)}, u32[]{:S(2)}) collective-permute-start(bf16[128,8,128]{2,0,1:T(8,128)(2,1)S(1)} %get-tuple-element.912), channel_id=1, source_target_pairs={{0,1},{1,2},{2,3},{3,4},{4,5},{5,6},{6,7},{7,0},{8,9},{9,10},{10,1... | collective-permute-start | bytes 786440 | tf_op jit(solution)/shard_map/while/body/eval_jaxpr/ppermute | solution.py:128
  312.1 19.9 %collective-permute-start.4 = (f32[128,8,128]{2,0,1:T(8,128)}, f32[128,8,128]{2,0,1:T(8,128)S(1)}, u32[]{:S(2)}, u32[]{:S(2)}) collective-permute-start(f32[128,8,128]{2,0,1:T(8,128)} %get-tuple-element.913), channel_id=1, source_target_pairs={{0,1},{1,2},{2,3},{3,4},{4,5},{5,6},{6,7},{7,0},{8,9},{9,10},{10,1... | collective-permute-start | bytes 1572872 | tf_op jit(solution)/shard_map/while/body/eval_jaxpr/ppermute | solution.py:129
  314.6 17.4 %collective-permute-start.5 = (f32[128,8,128]{2,0,1:T(8,128)}, f32[128,8,128]{2,0,1:T(8,128)S(1)}, u32[]{:S(2)}, u32[]{:S(2)}) collective-permute-start(f32[128,8,128]{2,0,1:T(8,128)} %get-tuple-element.914), channel_id=1, source_target_pairs={{0,1},{1,2},{2,3},{3,4},{4,5},{5,6},{6,7},{7,0},{8,9},{9,10},{10,1... | collective-permute-start | bytes 1572872 | tf_op jit(solution)/shard_map/while/body/eval_jaxpr/ppermute | solution.py:130
  315.6 14.3 %collective-permute-start.2 = (bf16[128,8,128]{2,0,1:T(8,128)(2,1)}, bf16[128,8,128]{2,0,1:T(8,128)(2,1)S(1)}, u32[]{:S(2)}, u32[]{:S(2)}) collective-permute-start(bf16[128,8,128]{2,0,1:T(8,128)(2,1)} %get-tuple-element.911), channel_id=1, source_target_pairs={{0,1},{1,2},{2,3},{3,4},{4,5},{5,6},{6,7},{7,0},{8,9},{9,10},{10,1... | collective-permute-start | bytes 786440 | tf_op jit(solution)/shard_map/while/body/eval_jaxpr/ppermute | solution.py:127
  318.1 13.8 %collective-permute-start.3 = (bf16[128,8,128]{2,0,1:T(8,128)(2,1)S(1)}, bf16[128,8,128]{2,0,1:T(8,128)(2,1)S(1)}, u32[]{:S(2)}, u32[]{:S(2)}) collective-permute-start(bf16[128,8,128]{2,0,1:T(8,128)(2,1)S(1)} %get-tuple-element.912), channel_id=1, source_target_pairs={{0,1},{1,2},{2,3},{3,4},{4,5},{5,6},{6,7},{7,0},{8,9},{9,10},{10,1... | collective-permute-start | bytes 786440 | tf_op jit(solution)/shard_map/while/body/eval_jaxpr/ppermute | solution.py:128
  336.3 17.5 %collective-permute-start.6 = (bf16[128,8,128]{2,0,1:T(8,128)(2,1)S(1)}, bf16[128,8,128]{2,0,1:T(8,128)(2,1)S(1)}, u32[]{:S(2)}, u32[]{:S(2)}) collective-permute-start(bf16[128,8,128]{2,0,1:T(8,128)(2,1)S(1)} %convert.8), channel_id=1, source_target_pairs={{0,1},{1,2},{2,3},{3,4},{4,5},{5,6},{6,7},{7,0},{8,9},{9,10},{10,1... | collective-permute-start | bytes 786440 | tf_op jit(solution)/shard_map/ppermute | solution.py:137
  338.9 22.6 %slice-start = ((s8[8388608]{0:T(1024)(128)(4,1)}), s8[4194304]{0:T(1024)(128)(4,1)S(1)}, s32[]{:S(2)}) async-start(s8[8388608]{0:T(1024)(128)(4,1)} %bitcast.321), calls=%async_computation.6 | async-start | bytes 8388608
  346.4 15.1 %slice-start.1 = ((s8[8388608]{0:T(1024)(128)(4,1)}), s8[4194304]{0:T(1024)(128)(4,1)S(1)}, s32[]{:S(2)}) async-start(s8[8388608]{0:T(1024)(128)(4,1)} %bitcast.321), calls=%async_computation.7 | async-start | bytes 8388608
  346.4 15.1 %collective-permute-start.7 = (bf16[128,8,128]{2,0,1:T(8,128)(2,1)S(1)}, bf16[128,8,128]{2,0,1:T(8,128)(2,1)S(1)}, u32[]{:S(2)}, u32[]{:S(2)}) collective-permute-start(bf16[128,8,128]{2,0,1:T(8,128)(2,1)S(1)} %convert.9), channel_id=1, source_target_pairs={{0,1},{1,2},{2,3},{3,4},{4,5},{5,6},{6,7},{7,0},{8,9},{9,10},{10,1... | collective-permute-start | bytes 786440 | tf_op jit(solution)/shard_map/ppermute | solution.py:138
  360.2 5.7 %copy-start.1 = (bf16[128,4096]{1,0:T(8,128)(2,1)S(1)}, bf16[128,4096]{1,0:T(8,128)(2,1)}, u32[]{:S(2)}) copy-start(bf16[128,4096]{1,0:T(8,128)(2,1)} %all-gather.3.cloned.1.call-done) | copy-start | bytes 3145732
  371.6 12.1 %copy-start.2 = (bf16[128,4096]{1,0:T(8,128)(2,1)S(1)}, bf16[128,4096]{1,0:T(8,128)(2,1)}, u32[]{:S(2)}) copy-start(bf16[128,4096]{1,0:T(8,128)(2,1)} %all-gather.5.cloned.1.call-done) | copy-start | bytes 3145732
Sparse Core Ops, SparseCore 0:
  9.6 23.1 all-gather.4
  34.3 21.8 all-gather.2
  170.7 34.3 reduce-scatter.2
  365.9 32.2 reduce-scatter.4
where the time goes:
time: 442 us; the launch traced here: 435 us
  waiting for transfers between devices  160 us (36%)
  matrix products  90.2 us (20%)
  starting transfers between devices  89.8 us (20%)
  local copies, waits for them, and re-layouts  63.1 us (14%)
  other arithmetic  17.2 us (4%)
  between operations  14.1 us (3%)
    ppermute x7, waiting for transfers between devices, backward_step(): k_blk = lax.ppermute(k_blk, 'cp', send_perm)  60.3 us
    unnamed x29, local copies, waits for them, and re-layouts  38.2 us
    all_gather x1, waiting for transfers between devices, device_fn(): dy_rows = lax.all_gather(dy_blk, 'tp', axis=0, tiled=True)  23.7 us
    ppermute x7, starting transfers between devices, forward_step(): k_blk = lax.ppermute(k_blk, 'cp', send_perm)  20.7 us
    while x35, local copies, waits for them, and re-layouts  19.7 us
    ppermute x7, waiting for transfers between devices, forward_step(): v_blk = lax.ppermute(v_blk, 'cp', send_perm)  19 us
    ppermute x7, waiting for transfers between devices, forward_step(): k_blk = lax.ppermute(k_blk, 'cp', send_perm)  17.5 us
    ppermute x7, starting transfers between devices, backward_step(): dk_blk = lax.ppermute(dk_blk, 'cp', send_perm)  16.9 us
  transfers between devices with their start and end apart: 48, of which 32 were waited for; matrix products, arithmetic and copies ran while one was open for 27% of the time, Pallas kernels for 0%

commit v1 on v0

v1 whole, which is shorter than its diff:
```python
import functools

import jax
import jax.numpy as jnp
from jax import lax
from jax.experimental import pallas as pl
from jax.experimental.pallas import tpu as pltpu
from jax.sharding import PartitionSpec as P

ROW_SPEC = P(("dp", "cp", "tp"), None)
HEAD_SPEC = P(None, "tp", None)
OUT_W_SPEC = P("tp", None, None)
GRAD_SPEC = P(("dp", "cp"), None, "tp", None)
GRAD_OUT_SPEC = P(("dp", "cp"), "tp", None, None)
NT = (((1,), (1,)), ((), ()))
TN = (((0,), (0,)), ((), ()))
NN = (((1,), (0,)), ((), ()))
MESH = pl.DeviceIdType.MESH
VMEM_BYTES = 67_043_328
RS_TILES = 8
CHUNKS = 16
SLOTS = 4


def mm(a, b, dims=NN):
    return lax.dot_general(a, b, dims, preferred_element_type=jnp.float32)


def attention_kernel(tp, cp, *refs):
    (x_ref, dy_ref, wq_ref, wk_ref, wv_ref, wo_ref,
     y_ref, dx_ref, xr_ref, dyr_ref, o_ref, dq_ref, dk_ref, dv_ref,
     wbuf, wf32, wall, wo_all, flat, heads, o_send, g_send, stat, stat_t,
     part, r1, r2, r3, s2,
     w_sem, wo_sem, ag_send, ag_recv, in_send, in_recv, out_send, out_recv,
     r1_send, r1_recv, r2_send, r2_recv, r3_send, r3_recv) = refs
    me_t, me_c = lax.axis_index("tp"), lax.axis_index("cp")
    right, left, across = (me_t + 1) % tp, (me_t + tp - 1) % tp, (me_t + 2) % tp
    rb, dm = x_ref.shape
    rows = rb * tp
    half = rows // 2
    cols = dm // 2
    total, hd = heads.shape[1:]
    n_heads = cp
    scale = hd ** -0.5

    w_refs = (wq_ref, wk_ref, wv_ref)
    chunk = dm // CHUNKS

    def w_copy(t, c, slot):
        return pltpu.make_async_copy(w_refs[t].at[pl.ds(c * chunk * n_heads, chunk * n_heads)], wbuf.at[slot], w_sem.at[slot])

    for c in range(SLOTS):
        w_copy(0, c, c).start()

    barrier = pltpu.get_barrier_semaphore()
    for t_dev in (left, right):
        pl.semaphore_signal(barrier, inc=1, device_id={"tp": t_dev}, device_id_type=MESH)
    for k in range(1, cp):
        pl.semaphore_signal(barrier, inc=1, device_id={"cp": (me_c + k) % cp}, device_id_type=MESH)
    pl.semaphore_wait(barrier, 2 + cp - 1)

    def gather_copy(src, dst, which, idx, block, col_half, to):
        where = (pl.ds(block * rb, rb), pl.ds(col_half * cols, cols))
        src_view = src.at[:, pl.ds(col_half * cols, cols)] if src is not dst else dst.at[where]
        return pltpu.make_async_remote_copy(src_view, dst.at[where], ag_send.at[which, idx], ag_recv.at[which, idx],
                                            device_id={"tp": to}, device_id_type=MESH)

    def gather_start(which, src, dst):
        for idx, col_half, to in ((0, 0, right), (1, 1, left), (2, 1, right), (3, 0, left)):
            gather_copy(src, dst, which, idx, me_t, col_half, to).start()
        dst[pl.ds(pl.multiple_of(me_t * rb, rb), rb), :] = src[...]

    def gather_pass(which, src, dst):
        gather_copy(src, dst, which, 0, left, 0, right).wait_recv()
        gather_copy(dst, dst, which, 4, left, 0, right).start()
        gather_copy(src, dst, which, 1, right, 1, left).wait_recv()
        gather_copy(dst, dst, which, 5, right, 1, left).start()

    def gather_end(which, src, dst):
        gather_copy(src, dst, which, 2, left, 1, right).wait_recv()
        gather_copy(src, dst, which, 3, right, 0, left).wait_recv()
        gather_copy(dst, dst, which, 4, across, 0, right).wait_recv()
        gather_copy(dst, dst, which, 5, across, 1, left).wait_recv()

    def relayout(t):
        @pl.loop(0, CHUNKS)
        def _(c):
            slot = c % SLOTS
            w_copy(t, c, slot).wait()
            wf32[...] = wbuf[slot].astype(jnp.float32)
            at = pl.ds(pl.multiple_of(c * chunk, chunk), chunk)
            for h in range(n_heads):
                wall[t, at, h * hd:(h + 1) * hd] = wf32[pl.ds(h, chunk, stride=n_heads), :].astype(jnp.bfloat16)

            @pl.when(c + SLOTS < CHUNKS)
            def _():
                w_copy(t, c + SLOTS, slot).start()

            if t + 1 < len(w_refs):
                @pl.when(c + SLOTS >= CHUNKS)
                def _():
                    w_copy(t + 1, c + SLOTS - CHUNKS, slot).start()

    gather_start(0, x_ref, xr_ref)
    relayout(0)
    gather_pass(0, x_ref, xr_ref)
    gather_start(1, dy_ref, dyr_ref)
    relayout(1)
    wo_copy = pltpu.make_async_copy(wo_ref, wo_all, wo_sem)
    wo_copy.start()
    relayout(2)
    gather_end(0, x_ref, xr_ref)
    gather_pass(1, dy_ref, dyr_ref)

    def send_in(t, h):
        for part_half in range(2):
            block = me_c if part_half == 0 else 2 * cp - 1 - me_c
            src = flat.at[t, pl.ds(part_half * half, half), pl.ds(pl.multiple_of(h * hd, hd), hd)]
            dst = heads.at[t, pl.ds(pl.multiple_of(block * half, half), half)]

            @pl.when(h == me_c)
            def _():
                pltpu.make_async_copy(src, dst, in_recv.at[t]).start()

            @pl.when(h != me_c)
            def _():
                pltpu.make_async_remote_copy(src, dst, in_send.at[t], in_recv.at[t],
                                             device_id={"cp": h}, device_id_type=MESH).start()

    def wait_in(t):
        pltpu.make_async_copy(heads.at[t], heads.at[t], in_recv.at[t]).wait()

    pairs = cp // 2

    @pl.loop(0, 3 * pairs)
    def _(i):
        t = i // pairs
        pair = (me_c // 2 + 1 + i % pairs) % pairs
        at = pl.ds(pl.multiple_of(pair * 2 * hd, 2 * hd), 2 * hd)
        flat[t, :, at] = mm(xr_ref[...], wall[t, :, at]).astype(jnp.bfloat16)
        for e in range(2):
            send_in(t, pair * 2 + e)

    gather_end(1, dy_ref, dyr_ref)
    wo_copy.wait()

    @pl.loop(0, pairs)
    def _(i):
        pair = (me_c // 2 + 1 + i) % pairs
        at = pl.ds(pl.multiple_of(pair * 2 * hd, 2 * hd), 2 * hd)
        flat[3, :, at] = mm(dyr_ref[...], wo_all[at, :], NT).astype(jnp.bfloat16)
        for e in range(2):
            send_in(3, pair * 2 + e)

    outs = (o_ref, dq_ref, dk_ref, dv_ref)

    def send_out(t, src_ref, start, count):
        for b in range(start // half, (start + count) // half):
            s, part_half = (b, 0) if b < cp else (2 * cp - 1 - b, 1)
            src = src_ref.at[pl.ds(b * half, half)]
            dst = outs[t].at[pl.ds(part_half * half, half), pl.ds(pl.multiple_of(me_c * hd, hd), hd)]

            @pl.when(me_c == s)
            def _():
                pltpu.make_async_copy(src, dst, out_recv.at[t]).start()

            @pl.when(me_c != s)
            def _():
                pltpu.make_async_remote_copy(src, dst, out_send.at[t], out_recv.at[t],
                                             device_id={"cp": s}, device_id_type=MESH).start()

    def wait_out(t):
        pltpu.make_async_copy(outs[t], outs[t], out_recv.at[t]).wait()

    qb = min(256, total)
    blocks = total // qb

    def causal(shape, q_start, k_start, q_axis):
        q_pos = lax.broadcasted_iota(jnp.int32, shape, q_axis) + q_start
        k_pos = lax.broadcasted_iota(jnp.int32, shape, 1 - q_axis) + k_start
        return q_pos >= k_pos

    for t in range(3):
        wait_in(t)
    for i in range(blocks):
        at, n = pl.ds(i * qb, qb), (i + 1) * qb
        s = mm(heads[0, at, :], heads[1, :n, :], NT) * scale
        s = jnp.where(causal(s.shape, i * qb, 0, 0), s, -jnp.inf)
        m = jnp.max(s, axis=1, keepdims=True)
        p = jnp.exp(s - m)
        l = jnp.sum(p, axis=1, keepdims=True)
        o = mm(p.astype(jnp.bfloat16), heads[2, :n, :]) / l
        o_send[at, :] = o.astype(jnp.bfloat16)
        stat[0, at, :] = jnp.broadcast_to(m + jnp.log(l), (qb, hd))
        send_out(0, o_send, i * qb, qb)

    wait_in(3)
    for i in range(blocks):
        at = pl.ds(i * qb, qb)
        delta = jnp.sum(heads[3, at, :].astype(jnp.float32) * o_send[at, :].astype(jnp.float32), axis=1, keepdims=True)
        stat[1, at, :] = jnp.broadcast_to(delta, (qb, hd))
    for j in range(2):
        for i in range(total // hd):
            stat_t[j, :, i * hd:(i + 1) * hd] = stat[j, i * hd:(i + 1) * hd, :].T[:8]

    for i in range(blocks):
        at, n = pl.ds(i * qb, qb), (i + 1) * qb
        s = mm(heads[0, at, :], heads[1, :n, :], NT) * scale
        p = jnp.where(causal(s.shape, i * qb, 0, 0), jnp.exp(s - stat[0, at, :1]), 0.0)
        dp = mm(heads[3, at, :], heads[2, :n, :], NT)
        ds = (p * (dp - stat[1, at, :1])).astype(jnp.bfloat16)
        g_send[0, at, :] = (mm(ds, heads[1, :n, :]) * scale).astype(jnp.bfloat16)
        send_out(1, g_send.at[0], i * qb, qb)
    for i in range(blocks):
        at, after = pl.ds(i * qb, qb), pl.ds(i * qb, total - i * qb)
        s = mm(heads[1, at, :], heads[0, after, :], NT) * scale
        p = jnp.where(causal(s.shape, 0, 0, 1), jnp.exp(s - stat_t[0, :1, after]), 0.0)
        dp = mm(heads[2, at, :], heads[3, after, :], NT)
        ds = (p * (dp - stat_t[1, :1, after])).astype(jnp.bfloat16)
        g_send[2, at, :] = mm(p.astype(jnp.bfloat16), heads[3, after, :]).astype(jnp.bfloat16)
        send_out(3, g_send.at[2], i * qb, qb)
        g_send[1, at, :] = (mm(ds, heads[0, after, :]) * scale).astype(jnp.bfloat16)
        send_out(2, g_send.at[1], i * qb, qb)

    width = dm // RS_TILES

    def rs_parts(j, tile, odd):
        onward, back = (left, right) if odd else (right, left)
        at = pl.ds(pl.multiple_of(tile * width, width), width)

        def mine(d):
            return (j, pl.ds(pl.multiple_of(d * rb, rb), rb), at)

        def copy(src, dst, send, recv, to):
            return pltpu.make_async_remote_copy(src, dst.at[j, tile], send.at[j, tile], recv.at[j, tile],
                                                device_id={"tp": to}, device_id_type=MESH)

        first = lambda: copy(part.at[mine(across)], r1, r1_send, r1_recv, onward)
        second = lambda: copy(s2.at[j, tile], r2, r2_send, r2_recv, onward)
        direct = lambda: copy(part.at[mine(back)], r3, r3_send, r3_recv, back)
        return at, mine, onward, first, second, direct

    def reduce_start(j, compute):
        @pl.loop(0, RS_TILES // 2)
        def _(i):
            for odd in range(2):
                tile = i * 2 + odd
                at, _, _, first, _, _ = rs_parts(j, tile, odd)
                part[j, :, at] = compute(at)
                first().start()

        @pl.loop(0, RS_TILES // 2)
        def _(i):
            for odd in range(2):
                rs_parts(j, i * 2 + odd, odd)[5]().start()

        @pl.loop(0, RS_TILES // 2)
        def _(i):
            for odd in range(2):
                tile = i * 2 + odd
                _, mine, onward, first, second, _ = rs_parts(j, tile, odd)
                first().wait_recv()
                s2[j, tile] = r1[j, tile] + part[mine(onward)]
                second().start()

    def reduce_end(j, out):
        @pl.loop(0, RS_TILES // 2)
        def _(i):
            for odd in range(2):
                tile = i * 2 + odd
                at, mine, _, first, second, direct = rs_parts(j, tile, odd)
                direct().wait_recv()
                second().wait_recv()
                out[:, at] = (part[mine(me_t)] + r2[j, tile] + r3[j, tile]).astype(jnp.bfloat16)
                first().wait_send()
                second().wait_send()
                direct().wait_send()

    wait_out(0)
    reduce_start(0, lambda at: mm(o_ref[...], wo_all[:, at]))
    for t in range(1, 4):
        wait_out(t)
    reduce_start(1, lambda at: mm(dq_ref[...], wall[0, at, :], NT) + mm(dk_ref[...], wall[1, at, :], NT) + mm(dv_ref[...], wall[2, at, :], NT))
    reduce_end(0, y_ref)
    reduce_end(1, dx_ref)

    others = heads.at[0, pl.ds(0, (cp - 1) * rows)]
    for t in range(4):
        for sem in (in_send, out_send):
            pltpu.make_async_copy(others, others, sem.at[t]).wait()
    for which, src, dst in ((0, x_ref, xr_ref), (1, dy_ref, dyr_ref)):
        for idx, col_half, to in ((0, 0, right), (1, 1, left), (2, 1, right), (3, 0, left)):
            gather_copy(src, dst, which, idx, me_t, col_half, to).wait_send()
        gather_copy(dst, dst, which, 4, left, 0, right).wait_send()
        gather_copy(dst, dst, which, 5, right, 1, left).wait_send()


def attention_call(tp, cp, x_blk, dy_blk, wq, wk, wv, wo):
    rb, dm = x_blk.shape
    rows = rb * tp
    hc, _ = wo.shape
    hd = hc // cp
    total = rows * cp
    bf, f32 = jnp.bfloat16, jnp.float32
    chunk = dm // CHUNKS
    width = dm // RS_TILES
    vmem, hbm = pl.BlockSpec(memory_space=pltpu.VMEM), pl.BlockSpec(memory_space=pl.ANY)
    out = lambda r, c: jax.ShapeDtypeStruct((r, c), bf)
    dma = pltpu.SemaphoreType.DMA
    return pl.pallas_call(
        functools.partial(attention_kernel, tp, cp),
        out_shape=(out(rb, dm), out(rb, dm), out(rows, dm), out(rows, dm), out(rows, hc), out(rows, hc), out(rows, hc), out(rows, hc)),
        in_specs=[vmem, vmem, hbm, hbm, hbm, hbm],
        out_specs=[vmem] * 8,
        scratch_shapes=[
            pltpu.VMEM((SLOTS, chunk * cp, hd), bf), pltpu.VMEM((chunk * cp, hd), f32),
            pltpu.VMEM((3, dm, hc), bf), pltpu.VMEM((hc, dm), bf),
            pltpu.VMEM((4, rows, hc), bf), pltpu.VMEM((4, total, hd), bf),
            pltpu.VMEM((total, hd), bf), pltpu.VMEM((3, total, hd), bf),
            pltpu.VMEM((2, total, hd), f32), pltpu.VMEM((2, 8, total), f32),
            pltpu.VMEM((2, rows, dm), f32),
            pltpu.VMEM((2, RS_TILES, rb, width), f32), pltpu.VMEM((2, RS_TILES, rb, width), f32),
            pltpu.VMEM((2, RS_TILES, rb, width), f32), pltpu.VMEM((2, RS_TILES, rb, width), f32),
            dma((SLOTS,)), dma, dma((2, 6)), dma((2, 6)), dma((4,)), dma((4,)), dma((4,)), dma((4,)),
            dma((2, RS_TILES)), dma((2, RS_TILES)), dma((2, RS_TILES)), dma((2, RS_TILES)), dma((2, RS_TILES)), dma((2, RS_TILES)),
        ],
        compiler_params=pltpu.CompilerParams(collective_id=0, has_side_effects=True, vmem_limit_bytes=VMEM_BYTES),
    )(x_blk, dy_blk, wq, wk, wv, wo)


def grad_kernel(n_heads, x_ref, dy_ref, o_ref, dq_ref, dk_ref, dv_ref, gq_ref, gk_ref, gv_ref, go_ref, wide):
    hd = wide.shape[1]
    m_tile = x_ref.shape[1]
    for d_ref, g_ref in ((dq_ref, gq_ref), (dk_ref, gk_ref), (dv_ref, gv_ref)):
        grad = mm(x_ref[...], d_ref[...], TN)
        for h in range(n_heads):
            wide[pl.ds(h, m_tile, stride=n_heads), :] = grad[:, h * hd:(h + 1) * hd]
        g_ref[...] = wide[...].astype(jnp.bfloat16)
    go_ref[...] = mm(o_ref[...], dy_ref[...], TN).astype(jnp.bfloat16)


def grad_call(n_heads, x_rows, dy_rows, o_flat, dq, dk, dv):
    rows, dm = x_rows.shape
    hc = o_flat.shape[1]
    hd = hc // n_heads
    steps = n_heads
    m_tile, o_tile = dm // steps, hc // steps
    bf = jnp.bfloat16
    whole = lambda c: pl.BlockSpec((rows, c), lambda i: (0, 0))
    tiled = pl.BlockSpec((m_tile * n_heads, hd), lambda i: (i, 0))
    return pl.pallas_call(
        functools.partial(grad_kernel, n_heads),
        out_shape=[jax.ShapeDtypeStruct((dm * n_heads, hd), bf)] * 3 + [jax.ShapeDtypeStruct((hc, dm), bf)],
        grid=(steps,),
        in_specs=[pl.BlockSpec((rows, m_tile), lambda i: (0, i)), whole(dm), pl.BlockSpec((rows, o_tile), lambda i: (0, i)),
                  whole(hc), whole(hc), whole(hc)],
        out_specs=[tiled] * 3 + [pl.BlockSpec((o_tile, dm), lambda i: (i, 0))],
        scratch_shapes=[pltpu.VMEM((m_tile * n_heads, hd), jnp.float32)],
        compiler_params=pltpu.CompilerParams(vmem_limit_bytes=VMEM_BYTES),
    )(x_rows, dy_rows, o_flat, dq, dk, dv)


def solution(mesh):
    tp, cp = mesh.shape["tp"], mesh.shape["cp"]

    def device_fn(x_blk, w_query, w_key, w_value, w_out, dy_blk):
        dm, n_heads, hd = w_query.shape
        if tp != 4 or n_heads != cp or w_key.shape != w_query.shape:
            raise ValueError("unsupported split")
        tall = lambda w: w.reshape(dm * n_heads, hd)
        y_blk, dx_blk, x_rows, dy_rows, o_flat, dq, dk, dv = attention_call(
            tp, cp, x_blk, dy_blk, tall(w_query), tall(w_key), tall(w_value), w_out.reshape(n_heads * hd, dm))
        gq, gk, gv, go = grad_call(n_heads, x_rows, dy_rows, o_flat, dq, dk, dv)
        split = lambda g: g.reshape(1, dm, n_heads, hd)
        return y_blk, dx_blk, split(gq), split(gk), split(gv), go.reshape(1, n_heads, hd, dm)

    return jax.shard_map(device_fn, mesh=mesh,
                         in_specs=(ROW_SPEC, HEAD_SPEC, HEAD_SPEC, HEAD_SPEC, OUT_W_SPEC, ROW_SPEC),
                         out_specs=(ROW_SPEC, ROW_SPEC, GRAD_SPEC, GRAD_SPEC, GRAD_SPEC, GRAD_OUT_SPEC),
                         check_vma=False)
```

time: 442 us -> 110 us (0.25); the launches traced: 435 us -> 109 us
  waiting for transfers between devices: 160 us -> 0 us
  Pallas kernels: 0 us -> 105 us
  matrix products: 90.2 us -> 0 us
  starting transfers between devices: 89.8 us -> 0 us
  local copies, waits for them, and re-layouts: 63.1 us -> 3.34 us
  other arithmetic: 17.2 us -> 0 us
  between operations: 14.1 us -> 0.64 us
    ppermute x44 -> x0, waiting for transfers between devices: 119 us -> none  [the longest x7 60.3 us: backward_step(): k_blk = lax.ppermute(k_blk, 'cp', send_perm)]
    pallas_call x0 -> x2, Pallas kernels: none -> 105 us  [the longest x1 86.7 us: attention_call(): pl.pallas_call(functools.partial(attention_kernel, tp, cp), out_shape=(ou...]
    dot_general x67 -> x0, matrix products: 90.2 us -> none  [the longest x8 6.97 us: grad_update(): jnp.einsum('qhgk,qhgd->khd', d_scores, q_rows, preferred_element_type=jnp...]
    ppermute x44 -> x0, starting transfers between devices: 89.5 us -> none  [the longest x7 20.7 us: forward_step(): k_blk = lax.ppermute(k_blk, 'cp', send_perm)]
    all_gather x2 -> x0, waiting for transfers between devices: 39.5 us -> none  [the longest x1 23.7 us: device_fn(): dy_rows = lax.all_gather(dy_blk, 'tp', axis=0, tiled=True)]
    unnamed x29 -> x2, local copies, waits for them, and re-layouts: 38.2 us -> 3.34 us
    while x43 -> x0, local copies, waits for them, and re-layouts: 22.5 us -> none
    concatenate x20 -> x0, other arithmetic: 5.61 us -> none  [the longest x12 4.27 us: from_later(): jnp.concatenate([old_part[:half_rows], new_part])]
  transfers between devices with their start and end apart: 48 -> 0, of which waited for: 32 -> 0; matrix products, arithmetic and copies ran while one was open for 27% -> 0% of each run, Pallas kernels for 0% -> 0%
where the time goes in v1:
time: 110 us; the launch traced here: 109 us
  Pallas kernels  105 us (95%)
  local copies, waits for them, and re-layouts  3.34 us (3%)
    pallas_call x1, Pallas kernels, attention_call(): pl.pallas_call(functools.partial(attention_kernel, tp, cp), out_shape=(ou...  86.7 us
    pallas_call x1, Pallas kernels, grad_call(): pl.pallas_call(functools.partial(grad_kernel, n_heads), out_shape=[jax.Sh...  18.4 us
    unnamed x2, local copies, waits for them, and re-layouts  3.34 us

profile of v1, /device:TPU:97, one launch (start us, length us, event | category | flops | bytes accessed | tf_op | source)
XLA Modules:
  0.0 109.1 jit_solution(16191011265563803468)
XLA Ops:
  0.6 86.7 %shard_map.109 = (bf16[32,4096]{1,0:T(8,128)(2,1)}, bf16[32,4096]{1,0:T(8,128)(2,1)}, bf16[128,4096]{1,0:T(8,128)(2,1)}, bf16[128,4096]{1,0:T(8,128)(2,1)}, bf16...) custom-call(bf16[32,4096]{1,0:T(8,128)(2,1)} %refs_0_.1, ...), custom_call_target="tpu_custom_call" | custom-call | tf_op jit(solution)/shard_map/pallas_call | solution.py:310
  87.3 18.4 %shard_map.110 = (bf16[32768,128]{1,0:T(8,128)(2,1)}, bf16[32768,128]{1,0:T(8,128)(2,1)}, bf16[32768,128]{1,0:T(8,128)(2,1)}, bf16[1024,4096]{1,0:T(8,128)(2,1)}) custom-call(bf16[128,4096]{1,0:T(8,128)(2,1)} %get-tuple-element.20.x_ref, bf16[128,4096]{1,0:T(8,128)(2,1)} %get-tuple-element.21.dy_ref, bf16[128,1024]{1,0:T(8,128)(2,1)} %get-tuple-element.22.o_ref, ...), custom_call_target="tpu_custom_call" | custom-call | tf_op jit(solution)/shard_map/pallas_call | solution.py:351
  105.7 1.7 %copy.14 = bf16[32,4096]{1,0:T(8,128)(2,1)} copy(bf16[32,4096]{1,0:T(8,128)(2,1)} %get-tuple-element.36) | data formatting | bytes 524288
  107.4 1.7 %copy.15 = bf16[32,4096]{1,0:T(8,128)(2,1)} copy(bf16[32,4096]{1,0:T(8,128)(2,1)} %get-tuple-element.37) | data formatting | bytes 524288

commit v2 on v1

--- a/solution.py
+++ b/solution.py
@@ -28,9 +28,9 @@
 
 def attention_kernel(tp, cp, *refs):
     (x_ref, dy_ref, wq_ref, wk_ref, wv_ref, wo_ref,
-     y_ref, dx_ref, xr_ref, dyr_ref, o_ref, dq_ref, dk_ref, dv_ref,
+     y_ref, own_ref, far_r, far_l, back_l, back_r, on_r, on_l, xr_ref, dyr_ref, o_ref, dq_ref, dk_ref, dv_ref,
      wbuf, wf32, wall, wo_all, flat, heads, o_send, g_send, stat, stat_t,
-     part, r1, r2, r3, s2,
+     part, dx_part, r1, r2, r3, s2,
      w_sem, wo_sem, ag_send, ag_recv, in_send, in_recv, out_send, out_recv,
      r1_send, r1_recv, r2_send, r2_recv, r3_send, r3_recv) = refs
     me_t, me_c = lax.axis_index("tp"), lax.axis_index("cp")
@@ -211,6 +211,56 @@
         ds = (p * (dp - stat[1, at, :1])).astype(jnp.bfloat16)
         g_send[0, at, :] = (mm(ds, heads[1, :n, :]) * scale).astype(jnp.bfloat16)
         send_out(1, g_send.at[0], i * qb, qb)
+    width = dm // RS_TILES
+
+    def rs_parts(tile, odd):
+        onward, back = (left, right) if odd else (right, left)
+        at = pl.ds(pl.multiple_of(tile * width, width), width)
+
+        def mine(d):
+            return (pl.ds(pl.multiple_of(d * rb, rb), rb), at)
+
+        def copy(src, dst, send, recv, to):
+            return pltpu.make_async_remote_copy(src, dst.at[tile], send.at[tile], recv.at[tile],
+                                                device_id={"tp": to}, device_id_type=MESH)
+
+        first = lambda: copy(part.at[mine(across)], r1, r1_send, r1_recv, onward)
+        second = lambda: copy(s2.at[tile], r2, r2_send, r2_recv, onward)
+        direct = lambda: copy(part.at[mine(back)], r3, r3_send, r3_recv, back)
+        return at, mine, onward, first, second, direct
+
+    def pairs_of_tiles(step):
+        @pl.loop(0, RS_TILES // 2)
+        def _(i):
+            for odd in range(2):
+                step(i * 2 + odd, odd)
+
+    def reduce_first(tile, odd):
+        at, _, _, first, _, _ = rs_parts(tile, odd)
+        part[:, at] = mm(o_ref[...], wo_all[:, at])
+        first().start()
+
+    def reduce_direct(tile, odd):
+        rs_parts(tile, odd)[5]().start()
+
+    def reduce_second(tile, odd):
+        _, mine, onward, first, second, _ = rs_parts(tile, odd)
+        first().wait_recv()
+        s2[tile] = r1[tile] + part[mine(onward)]
+        second().start()
+
+    def reduce_last(tile, odd):
+        at, mine, _, first, second, direct = rs_parts(tile, odd)
+        direct().wait_recv()
+        second().wait_recv()
+        y_ref[:, at] = (part[mine(me_t)] + r2[tile] + r3[tile]).astype(jnp.bfloat16)
+        first().wait_send()
+        second().wait_send()
+        direct().wait_send()
+
+    wait_out(0)
+    pairs_of_tiles(reduce_first)
+    pairs_of_tiles(reduce_direct)
     for i in range(blocks):
         at, after = pl.ds(i * qb, qb), pl.ds(i * qb, total - i * qb)
         s = mm(heads[1, at, :], heads[0, after, :], NT) * scale
@@ -222,67 +272,28 @@
         g_send[1, at, :] = (mm(ds, heads[0, after, :]) * scale).astype(jnp.bfloat16)
         send_out(2, g_send.at[1], i * qb, qb)
 
-    width = dm // RS_TILES
-
-    def rs_parts(j, tile, odd):
-        onward, back = (left, right) if odd else (right, left)
-        at = pl.ds(pl.multiple_of(tile * width, width), width)
-
-        def mine(d):
-            return (j, pl.ds(pl.multiple_of(d * rb, rb), rb), at)
-
-        def copy(src, dst, send, recv, to):
-            return pltpu.make_async_remote_copy(src, dst.at[j, tile], send.at[j, tile], recv.at[j, tile],
-                                                device_id={"tp": to}, device_id_type=MESH)
-
-        first = lambda: copy(part.at[mine(across)], r1, r1_send, r1_recv, onward)
-        second = lambda: copy(s2.at[j, tile], r2, r2_send, r2_recv, onward)
-        direct = lambda: copy(part.at[mine(back)], r3, r3_send, r3_recv, back)
-        return at, mine, onward, first, second, direct
-
-    def reduce_start(j, compute):
-        @pl.loop(0, RS_TILES // 2)
-        def _(i):
-            for odd in range(2):
-                tile = i * 2 + odd
-                at, _, _, first, _, _ = rs_parts(j, tile, odd)
-                part[j, :, at] = compute(at)
-                first().start()
-
-        @pl.loop(0, RS_TILES // 2)
-        def _(i):
-            for odd in range(2):
-                rs_parts(j, i * 2 + odd, odd)[5]().start()
-
-        @pl.loop(0, RS_TILES // 2)
-        def _(i):
-            for odd in range(2):
-                tile = i * 2 + odd
-                _, mine, onward, first, second, _ = rs_parts(j, tile, odd)
-                first().wait_recv()
-                s2[j, tile] = r1[j, tile] + part[mine(onward)]
-                second().start()
-
-    def reduce_end(j, out):
-        @pl.loop(0, RS_TILES // 2)
-        def _(i):
-            for odd in range(2):
-                tile = i * 2 + odd
-                at, mine, _, first, second, direct = rs_parts(j, tile, odd)
-                direct().wait_recv()
-                second().wait_recv()
-                out[:, at] = (part[mine(me_t)] + r2[j, tile] + r3[j, tile]).astype(jnp.bfloat16)
-                first().wait_send()
-                second().wait_send()
-                direct().wait_send()
-
-    wait_out(0)
-    reduce_start(0, lambda at: mm(o_ref[...], wo_all[:, at]))
+    pairs_of_tiles(reduce_second)
+
     for t in range(1, 4):
         wait_out(t)
-    reduce_start(1, lambda at: mm(dq_ref[...], wall[0, at, :], NT) + mm(dk_ref[...], wall[1, at, :], NT) + mm(dv_ref[...], wall[2, at, :], NT))
-    reduce_end(0, y_ref)
-    reduce_end(1, dx_ref)
+
+    def dx_tile(tile, outs_of):
+        at = pl.ds(pl.multiple_of(tile * width, width), width)
+        dx_part[...] = (mm(dq_ref[...], wall[0, at, :], NT) + mm(dk_ref[...], wall[1, at, :], NT)
+                        + mm(dv_ref[...], wall[2, at, :], NT))
+        own_ref[:, at] = dx_part[pl.ds(pl.multiple_of(me_t * rb, rb), rb), :]
+        for ref, d in outs_of:
+            ref[:, pl.ds(pl.multiple_of(tile % (RS_TILES // 2) * width, width), width)] = dx_part[pl.ds(pl.multiple_of(d * rb, rb), rb), :]
+
+    @pl.loop(0, RS_TILES // 2)
+    def _(i):
+        dx_tile(i, ((far_r, across), (back_l, left), (on_r, right)))
+
+    @pl.loop(RS_TILES // 2, RS_TILES)
+    def _(i):
+        dx_tile(i, ((far_l, across), (back_r, right), (on_l, left)))
+
+    pairs_of_tiles(reduce_last)
 
     others = heads.at[0, pl.ds(0, (cp - 1) * rows)]
     for t in range(4):
@@ -306,58 +317,76 @@
     width = dm // RS_TILES
     vmem, hbm = pl.BlockSpec(memory_space=pltpu.VMEM), pl.BlockSpec(memory_space=pl.ANY)
     out = lambda r, c: jax.ShapeDtypeStruct((r, c), bf)
+    wide = lambda c: jax.ShapeDtypeStruct((rb, c), f32)
     dma = pltpu.SemaphoreType.DMA
     return pl.pallas_call(
         functools.partial(attention_kernel, tp, cp),
-        out_shape=(out(rb, dm), out(rb, dm), out(rows, dm), out(rows, dm), out(rows, hc), out(rows, hc), out(rows, hc), out(rows, hc)),
+        out_shape=(out(rb, dm), wide(dm), *[wide(dm // 2)] * 6, out(rows, dm), out(rows, dm), out(rows, hc), out(rows, hc), out(rows, hc), out(rows, hc)),
         in_specs=[vmem, vmem, hbm, hbm, hbm, hbm],
-        out_specs=[vmem] * 8,
+        out_specs=[vmem] * 14,
         scratch_shapes=[
             pltpu.VMEM((SLOTS, chunk * cp, hd), bf), pltpu.VMEM((chunk * cp, hd), f32),
             pltpu.VMEM((3, dm, hc), bf), pltpu.VMEM((hc, dm), bf),
             pltpu.VMEM((4, rows, hc), bf), pltpu.VMEM((4, total, hd), bf),
             pltpu.VMEM((total, hd), bf), pltpu.VMEM((3, total, hd), bf),
             pltpu.VMEM((2, total, hd), f32), pltpu.VMEM((2, 8, total), f32),
-            pltpu.VMEM((2, rows, dm), f32),
-            pltpu.VMEM((2, RS_TILES, rb, width), f32), pltpu.VMEM((2, RS_TILES, rb, width), f32),
-            pltpu.VMEM((2, RS_TILES, rb, width), f32), pltpu.VMEM((2, RS_TILES, rb, width), f32),
+            pltpu.VMEM((rows, dm), f32), pltpu.VMEM((rows, width), f32),
+            pltpu.VMEM((RS_TILES, rb, width), f32), pltpu.VMEM((RS_TILES, rb, width), f32),
+            pltpu.VMEM((RS_TILES, rb, width), f32), pltpu.VMEM((RS_TILES, rb, width), f32),
             dma((SLOTS,)), dma, dma((2, 6)), dma((2, 6)), dma((4,)), dma((4,)), dma((4,)), dma((4,)),
-            dma((2, RS_TILES)), dma((2, RS_TILES)), dma((2, RS_TILES)), dma((2, RS_TILES)), dma((2, RS_TILES)), dma((2, RS_TILES)),
+            *[dma((RS_TILES,))] * 6,
         ],
         compiler_params=pltpu.CompilerParams(collective_id=0, has_side_effects=True, vmem_limit_bytes=VMEM_BYTES),
     )(x_blk, dy_blk, wq, wk, wv, wo)
 
 
-def grad_kernel(n_heads, x_ref, dy_ref, o_ref, dq_ref, dk_ref, dv_ref, gq_ref, gk_ref, gv_ref, go_ref, wide):
+def head_major_grads(n_heads, x_ref, d_refs, g_refs, wide):
     hd = wide.shape[1]
     m_tile = x_ref.shape[1]
-    for d_ref, g_ref in ((dq_ref, gq_ref), (dk_ref, gk_ref), (dv_ref, gv_ref)):
+    for d_ref, g_ref in zip(d_refs, g_refs):
         grad = mm(x_ref[...], d_ref[...], TN)
         for h in range(n_heads):
             wide[pl.ds(h, m_tile, stride=n_heads), :] = grad[:, h * hd:(h + 1) * hd]
         g_ref[...] = wide[...].astype(jnp.bfloat16)
+
+
+def grad_kernel_qk(n_heads, x_ref, dq_ref, dk_ref, gq_ref, gk_ref, wide):
+    head_major_grads(n_heads, x_ref, (dq_ref, dk_ref), (gq_ref, gk_ref), wide)
+
+
+def grad_kernel_vo(n_heads, x_ref, dv_ref, o_ref, dy_ref, y_ref, gv_ref, go_ref, y_out, wide):
+    head_major_grads(n_heads, x_ref, (dv_ref,), (gv_ref,), wide)
     go_ref[...] = mm(o_ref[...], dy_ref[...], TN).astype(jnp.bfloat16)
-
-
-def grad_call(n_heads, x_rows, dy_rows, o_flat, dq, dk, dv):
+    y_out[...] = y_ref[...]
+
+
+def grad_call(body, n_heads, x_rows, wholes, tall_count, o_flat=None, dy_rows=None, y_blk=None):
     rows, dm = x_rows.shape
-    hc = o_flat.shape[1]
+    hc = wholes[0].shape[1]
     hd = hc // n_heads
     steps = n_heads
     m_tile, o_tile = dm // steps, hc // steps
     bf = jnp.bfloat16
-    whole = lambda c: pl.BlockSpec((rows, c), lambda i: (0, 0))
-    tiled = pl.BlockSpec((m_tile * n_heads, hd), lambda i: (i, 0))
+    whole = lambda a: pl.BlockSpec(a.shape, lambda i: (0, 0))
+    args = [x_rows, *wholes]
+    in_specs = [pl.BlockSpec((rows, m_tile), lambda i: (0, i)), *map(whole, wholes)]
+    out_shape = [jax.ShapeDtypeStruct((dm * n_heads, hd), bf)] * tall_count
+    out_specs = [pl.BlockSpec((m_tile * n_heads, hd), lambda i: (i, 0))] * tall_count
+    if o_flat is not None:
+        args += [o_flat, dy_rows, y_blk]
+        in_specs += [pl.BlockSpec((rows, o_tile), lambda i: (0, i)), whole(dy_rows), whole(y_blk)]
+        out_shape += [jax.ShapeDtypeStruct((hc, dm), bf), jax.ShapeDtypeStruct(y_blk.shape, bf)]
+        out_specs += [pl.BlockSpec((o_tile, dm), lambda i: (i, 0)), whole(y_blk)]
     return pl.pallas_call(
-        functools.partial(grad_kernel, n_heads),
-        out_shape=[jax.ShapeDtypeStruct((dm * n_heads, hd), bf)] * 3 + [jax.ShapeDtypeStruct((hc, dm), bf)],
+        functools.partial(body, n_heads),
+        out_shape=out_shape,
         grid=(steps,),
-        in_specs=[pl.BlockSpec((rows, m_tile), lambda i: (0, i)), whole(dm), pl.BlockSpec((rows, o_tile), lambda i: (0, i)),
-                  whole(hc), whole(hc), whole(hc)],
-        out_specs=[tiled] * 3 + [pl.BlockSpec((o_tile, dm), lambda i: (i, 0))],
+        in_specs=in_specs,
+        out_specs=out_specs,
         scratch_shapes=[pltpu.VMEM((m_tile * n_heads, hd), jnp.float32)],
         compiler_params=pltpu.CompilerParams(vmem_limit_bytes=VMEM_BYTES),
-    )(x_rows, dy_rows, o_flat, dq, dk, dv)
+        cost_estimate=pl.CostEstimate(flops=4 * rows * dm * hc, bytes_accessed=4 * dm * hc + 8 * rows * dm, transcendentals=0),
+    )(*args)
 
 
 def solution(mesh):
@@ -368,9 +397,20 @@
         if tp != 4 or n_heads != cp or w_key.shape != w_query.shape:
             raise ValueError("unsupported split")
         tall = lambda w: w.reshape(dm * n_heads, hd)
-        y_blk, dx_blk, x_rows, dy_rows, o_flat, dq, dk, dv = attention_call(
+        y_blk, own, far_r, far_l, back_l, back_r, on_r, on_l, x_rows, dy_rows, o_flat, dq, dk, dv = attention_call(
             tp, cp, x_blk, dy_blk, tall(w_query), tall(w_key), tall(w_value), w_out.reshape(n_heads * hd, dm))
-        gq, gk, gv, go = grad_call(n_heads, x_rows, dy_rows, o_flat, dq, dk, dv)
+        to_right = lambda a: lax.ppermute(a, "tp", [(i, (i + 1) % tp) for i in range(tp)])
+        to_left = lambda a: lax.ppermute(a, "tp", [(i, (i - 1) % tp) for i in range(tp)])
+        came_r, came_l = to_right(far_r), to_left(far_l)
+        direct_a, direct_b = to_left(back_l), to_right(back_r)
+        gq, gk = grad_call(grad_kernel_qk, n_heads, x_rows, (dq, dk), 2)
+        gq, gk, on_r, on_l = lax.optimization_barrier((gq, gk, on_r, on_l))
+        sum_r, sum_l = on_r + came_r, on_l + came_l
+        sum_r, sum_l, x_rows = lax.optimization_barrier((sum_r, sum_l, x_rows))
+        gv, go, y_blk = grad_call(grad_kernel_vo, n_heads, x_rows, (dv,), 1, o_flat, dy_rows, y_blk)
+        last_a, last_b = to_right(sum_r), to_left(sum_l)
+        half_cols = dm // 2
+        dx_blk = jnp.concatenate([own[:, :half_cols] + direct_a + last_a, own[:, half_cols:] + direct_b + last_b], axis=1).astype(jnp.bfloat16)
         split = lambda g: g.reshape(1, dm, n_heads, hd)
         return y_blk, dx_blk, split(gq), split(gk), split(gv), go.reshape(1, n_heads, hd, dm)
 

time: 110 us -> 106 us (0.964)
  Pallas kernels: 105 us -> 91.5 us
  starting transfers between devices: 0 us -> 6.9 us
  other arithmetic: 0 us -> 5.66 us
  local copies, waits for them, and re-layouts: 3.34 us -> 0 us
    pallas_call x1, Pallas kernels: 86.7 us -> 69.4 us  [attention_call(): pl.pallas_call(functools.partial(attention_kernel, tp, cp), out_shape=(ou...]
    ppermute x0 -> x6, starting transfers between devices: none -> 6.9 us  [the longest x3 5.34 us: device_fn(): lax.ppermute(a, 'tp', [(i, (i - 1) % tp) for i in range(tp)])]
    pallas_call x1 -> x2, Pallas kernels: 18.4 us -> 22.1 us  [grad_call(): pl.pallas_call(functools.partial(body, n_heads), out_shape=out_shape, gri...]
    add x0 -> x2, other arithmetic: none -> 3.51 us  [device_fn(): sum_r, sum_l = (on_r + came_r, on_l + came_l)]
    unnamed x2 -> x0, local copies, waits for them, and re-layouts: 3.34 us -> none
    another operation x0 -> x1, other arithmetic: none -> 1.43 us
  transfers between devices with their start and end apart: 0 -> 6, of which waited for: 0 -> 0; matrix products, arithmetic and copies ran while one was open for 0% -> 3% of each run, Pallas kernels for 0% -> 21%
where the time goes in v2:
time: 106 us; the launch traced here: 105 us
  Pallas kernels  91.5 us (86%)
  starting transfers between devices  6.9 us (7%)
  other arithmetic  5.66 us (5%)
    pallas_call x1, Pallas kernels, attention_call(): pl.pallas_call(functools.partial(attention_kernel, tp, cp), out_shape=(ou...  69.4 us
    pallas_call x2, Pallas kernels, grad_call(): pl.pallas_call(functools.partial(body, n_heads), out_shape=out_shape, gri...  22.1 us
    ppermute x3, starting transfers between devices, device_fn(): lax.ppermute(a, 'tp', [(i, (i - 1) % tp) for i in range(tp)])  5.34 us
    add x2, other arithmetic, device_fn(): sum_r, sum_l = (on_r + came_r, on_l + came_l)  3.51 us
  transfers between devices with their start and end apart: 6, of which 0 were waited for; matrix products, arithmetic and copies ran while one was open for 3% of the time, Pallas kernels for 21%

profile of v2, /device:TPU:97, one launch (start us, length us, event | category | flops | bytes accessed | tf_op | source)
XLA Modules:
  0.0 104.8 jit_solution(3278444140963004236)
XLA Ops:
  0.6 69.4 %shard_map.109 = (bf16[32,4096]{1,0:T(8,128)(2,1)}, f32[32,4096]{1,0:T(8,128)}, f32[32,2048]{1,0:T(8,128)}, f32[32,2048]{1,0:T(8,128)}, f32[32,2048]{1,0:T(8,128...) custom-call(bf16[32,4096]{1,0:T(8,128)(2,1)} %refs_0_.1, ...), custom_call_target="tpu_custom_call" | custom-call | tf_op jit(solution)/shard_map/pallas_call | solution.py:322
  70.1 0.1 collective-permute-start
  70.2 2.6 %collective-permute-start.1 = (f32[32,2048]{1,0:T(8,128)}, f32[32,2048]{1,0:T(8,128)}, u32[]{:S(2)}, u32[]{:S(2)}) collective-permute-start(f32[32,2048]{1,0:T(8,128)} %get-tuple-element.42), channel_id=1, source_target_pairs={{0,24},{8,0},{16,8},{24,16},{1,25},{9,1},{17,9},{25,17},{2,26},{10... | collective-permute-start | bytes 786440 | tf_op jit(solution)/shard_map/ppermute | solution.py:403
  72.8 0.0 collective-permute-start.2
  72.9 1.4 %collective-permute-start.4 = (f32[32,2048]{1,0:T(8,128)}, f32[32,2048]{1,0:T(8,128)}, u32[]{:S(2)}, u32[]{:S(2)}) collective-permute-start(f32[32,2048]{1,0:T(8,128)} %get-tuple-element.52), channel_id=1, source_target_pairs={{0,8},{8,16},{16,24},{24,0},{1,9},{9,17},{17,25},{25,1},{2,10},{10... | collective-permute-start | bytes 786440 | tf_op jit(solution)/shard_map/ppermute | solution.py:402
  74.3 11.4 %shard_map.110 = (bf16[32768,128]{1,0:T(8,128)(2,1)}, bf16[32768,128]{1,0:T(8,128)(2,1)}) custom-call(bf16[128,4096]{1,0:T(8,128)(2,1)} %get-tuple-element.43.x_ref, bf16[128,1024]{1,0:T(8,128)(2,1)} %get-tuple-element.33.dq_ref, bf16[128,1024]{1,0:T(8,128)(2,1)} %get-tuple-element.34.dk_ref), custom_call_target="tpu_custom_call" | custom-call | flops 2147483648 | bytes 20971520 | tf_op jit(solution)/shard_map/pallas_call | solution.py:380
  85.7 0.0 collective-permute-done
  85.7 1.8 %add.18 = f32[32,2048]{1,0:T(8,128)} add(f32[32,2048]{1,0:T(8,128)} %get-tuple-element.39, f32[32,2048]{1,0:T(8,128)} %collective-permute-done) | non-fusion elementwise | flops 65536 | bytes 786432 | tf_op jit(solution)/shard_map/add | solution.py:408
  87.5 0.0 collective-permute-done.1
  87.5 1.7 %add.19 = f32[32,2048]{1,0:T(8,128)} add(f32[32,2048]{1,0:T(8,128)} %get-tuple-element.41, f32[32,2048]{1,0:T(8,128)} %collective-permute-done.1) | non-fusion elementwise | flops 65536 | bytes 786432 | tf_op jit(solution)/shard_map/add | solution.py:408
  89.2 0.0 collective-permute-start.3
  89.3 2.7 %collective-permute-start.5 = (f32[32,2048]{1,0:T(8,128)}, f32[32,2048]{1,0:T(8,128)}, u32[]{:S(2)}, u32[]{:S(2)}) collective-permute-start(f32[32,2048]{1,0:T(8,128)} %add.19), channel_id=1, source_target_pairs={{0,24},{8,0},{16,8},{24,16},{1,25},{9,1},{17,9},{25,17},{2,26},{10... | collective-permute-start | bytes 786440 | tf_op jit(solution)/shard_map/ppermute | solution.py:403
  91.9 10.6 %shard_map.111 = (bf16[32768,128]{1,0:T(8,128)(2,1)}, bf16[1024,4096]{1,0:T(8,128)(2,1)}, bf16[32,4096]{1,0:T(8,128)(2,1)}) custom-call(bf16[128,4096]{1,0:T(8,128)(2,1)} %get-tuple-element.43.x_ref, bf16[128,1024]{1,0:T(8,128)(2,1)} %get-tuple-element.44.dv_ref, bf16[128,1024]{1,0:T(8,128)(2,1)} %get-tuple-element.45.o_ref, ...), custom_call_target="tpu_custom_call" | custom-call | flops 2147483648 | bytes 20971520 | tf_op jit(solution)/shard_map/pallas_call | solution.py:380
  102.6 0.0 collective-permute-done.2
  102.6 0.0 collective-permute-done.4
  102.6 0.0 collective-permute-done.3
  102.6 0.0 collective-permute-done.5
  102.6 1.4 %add_convert_fusion.1 = (bf16[32,2048]{1,0:T(8,128)(2,1)S(1)}, bf16[32,2048]{1,0:T(8,128)(2,1)S(1)}) fusion(f32[32,2048]{1,0:T(8,128)} %collective-permute-done.3, f32[32,2048]{1,0:T(8,128)} %collective-permute-done.2, f32[32,4096]{1,0:T(8,128)} %get-tuple-element.49, f32[32,2048]{1,0:T(8,128)} %collective-permute-done.5, f32[32,2048]{1,0:T(8,128)} %collective-permute-done.4), kind=kLoop, calls=%fused_computation.2 | loop fusion | flops 393216 | bytes 1835008 | tf_op jit(solution)/shard_map/convert
  104.0 0.7 pad_maximum_fusion
Async XLA Ops:
  70.1 15.6 %collective-permute-start = (f32[32,2048]{1,0:T(8,128)}, f32[32,2048]{1,0:T(8,128)}, u32[]{:S(2)}, u32[]{:S(2)}) collective-permute-start(f32[32,2048]{1,0:T(8,128)} %get-tuple-element.40), channel_id=1, source_target_pairs={{0,8},{8,16},{16,24},{24,0},{1,9},{9,17},{17,25},{25,1},{2,10},{10... | collective-permute-start | bytes 786440 | tf_op jit(solution)/shard_map/ppermute | solution.py:402
  70.2 17.3 %collective-permute-start.1 = (f32[32,2048]{1,0:T(8,128)}, f32[32,2048]{1,0:T(8,128)}, u32[]{:S(2)}, u32[]{:S(2)}) collective-permute-start(f32[32,2048]{1,0:T(8,128)} %get-tuple-element.42), channel_id=1, source_target_pairs={{0,24},{8,0},{16,8},{24,16},{1,25},{9,1},{17,9},{25,17},{2,26},{10... | collective-permute-start | bytes 786440 | tf_op jit(solution)/shard_map/ppermute | solution.py:403
  72.8 29.7 %collective-permute-start.2 = (f32[32,2048]{1,0:T(8,128)}, f32[32,2048]{1,0:T(8,128)}, u32[]{:S(2)}, u32[]{:S(2)}) collective-permute-start(f32[32,2048]{1,0:T(8,128)} %get-tuple-element.50), channel_id=1, source_target_pairs={{0,24},{8,0},{16,8},{24,16},{1,25},{9,1},{17,9},{25,17},{2,26},{10... | collective-permute-start | bytes 786440 | tf_op jit(solution)/shard_map/ppermute | solution.py:403
  72.9 29.7 %collective-permute-start.4 = (f32[32,2048]{1,0:T(8,128)}, f32[32,2048]{1,0:T(8,128)}, u32[]{:S(2)}, u32[]{:S(2)}) collective-permute-start(f32[32,2048]{1,0:T(8,128)} %get-tuple-element.52), channel_id=1, source_target_pairs={{0,8},{8,16},{16,24},{24,0},{1,9},{9,17},{17,25},{25,1},{2,10},{10... | collective-permute-start | bytes 786440 | tf_op jit(solution)/shard_map/ppermute | solution.py:402
  89.2 13.3 %collective-permute-start.3 = (f32[32,2048]{1,0:T(8,128)}, f32[32,2048]{1,0:T(8,128)}, u32[]{:S(2)}, u32[]{:S(2)}) collective-permute-start(f32[32,2048]{1,0:T(8,128)} %add.18), channel_id=1, source_target_pairs={{0,8},{8,16},{16,24},{24,0},{1,9},{9,17},{17,25},{25,1},{2,10},{10... | collective-permute-start | bytes 786440 | tf_op jit(solution)/shard_map/ppermute | solution.py:402
  89.3 13.3 %collective-permute-start.5 = (f32[32,2048]{1,0:T(8,128)}, f32[32,2048]{1,0:T(8,128)}, u32[]{:S(2)}, u32[]{:S(2)}) collective-permute-start(f32[32,2048]{1,0:T(8,128)} %add.19), channel_id=1, source_target_pairs={{0,24},{8,0},{16,8},{24,16},{1,25},{9,1},{17,9},{25,17},{2,26},{10... | collective-permute-start | bytes 786440 | tf_op jit(solution)/shard_map/ppermute | solution.py:403

commit v3 on v2

v3 whole, which is shorter than its diff:
```python
import functools

import jax
import jax.numpy as jnp
from jax import lax
from jax.experimental import pallas as pl
from jax.experimental.pallas import tpu as pltpu
from jax.sharding import PartitionSpec as P

ROW_SPEC = P(("dp", "cp", "tp"), None)
HEAD_SPEC = P(None, "tp", None)
OUT_W_SPEC = P("tp", None, None)
GRAD_SPEC = P(("dp", "cp"), None, "tp", None)
GRAD_OUT_SPEC = P(("dp", "cp"), "tp", None, None)
NT = (((1,), (1,)), ((), ()))
TN = (((0,), (0,)), ((), ()))
NN = (((1,), (0,)), ((), ()))
MESH = pl.DeviceIdType.MESH
VMEM_BYTES = 67_043_328
RS_TILES = 8
CHUNKS = 16
SLOTS = 8
STRIPS = 4


def mm(a, b, dims=NN):
    return lax.dot_general(a, b, dims, preferred_element_type=jnp.float32)


def attention_kernel(tp, cp, *refs):
    (x_ref, dy_ref, wq_ref, wk_ref, wv_ref, wo_ref,
     y_ref, own_ref, back_l, back_r, on_r, on_l, xr_ref, dyr_ref, o_ref, dq_ref, dk_ref, dv_ref,
     wbuf, wf32, wall, wo_all, flat, heads, sorted_heads, sorted_o, out_heads, stat, stat_t,
     part, dx_part, r1, r2, r3, s2, r4,
     w_sem, wo_sem, ag_send, ag_recv, in_send, in_recv, out_send, out_recv,
     r1_send, r1_recv, r2_send, r2_recv, r3_send, r3_recv, r4_send, r4_recv) = refs
    me_t, me_c = lax.axis_index("tp"), lax.axis_index("cp")
    right, left, across = (me_t + 1) % tp, (me_t + tp - 1) % tp, (me_t + 2) % tp
    rb, dm = x_ref.shape
    rows = rb * tp
    half = rows // 2
    cols = dm // 2
    total, hd = heads.shape[1:]
    n_heads = cp
    scale = hd ** -0.5

    w_refs = (wq_ref, wk_ref, wv_ref)
    others = heads.at[0, pl.ds(0, (cp - 1) * rows)]
    chunk = dm // CHUNKS

    def w_copy(t, c, slot):
        return pltpu.make_async_copy(w_refs[t].at[pl.ds(c * chunk * n_heads, chunk * n_heads)], wbuf.at[slot], w_sem.at[slot])

    for c in range(SLOTS):
        w_copy(0, c, c).start()

    barrier = pltpu.get_barrier_semaphore()
    for t_dev in (left, right):
        pl.semaphore_signal(barrier, inc=1, device_id={"tp": t_dev}, device_id_type=MESH)
    for k in range(1, cp):
        pl.semaphore_signal(barrier, inc=1, device_id={"cp": (me_c + k) % cp}, device_id_type=MESH)
    pl.semaphore_wait(barrier, 2 + cp - 1)

    def gather_copy(src, dst, which, idx, block, col_half, to):
        where = (pl.ds(block * rb, rb), pl.ds(col_half * cols, cols))
        src_view = src.at[:, pl.ds(col_half * cols, cols)] if src is not dst else dst.at[where]
        return pltpu.make_async_remote_copy(src_view, dst.at[where], ag_send.at[which, idx], ag_recv.at[which, idx],
                                            device_id={"tp": to}, device_id_type=MESH)

    def gather_start(which, src, dst):
        for idx, col_half, to in ((0, 0, right), (1, 1, left), (2, 1, right), (3, 0, left)):
            gather_copy(src, dst, which, idx, me_t, col_half, to).start()
        dst[pl.ds(pl.multiple_of(me_t * rb, rb), rb), :] = src[...]

    def gather_pass(which, src, dst):
        gather_copy(src, dst, which, 0, left, 0, right).wait_recv()
        gather_copy(dst, dst, which, 4, left, 0, right).start()
        gather_copy(src, dst, which, 1, right, 1, left).wait_recv()
        gather_copy(dst, dst, which, 5, right, 1, left).start()

    def gather_end(which, src, dst):
        gather_copy(src, dst, which, 2, left, 1, right).wait_recv()
        gather_copy(src, dst, which, 3, right, 0, left).wait_recv()
        gather_copy(dst, dst, which, 4, across, 0, right).wait_recv()
        gather_copy(dst, dst, which, 5, across, 1, left).wait_recv()

    def relayout(t):
        @pl.loop(0, CHUNKS)
        def _(c):
            slot = c % SLOTS
            w_copy(t, c, slot).wait()
            strip = chunk // STRIPS
            for k in range(STRIPS + 1):
                if k < STRIPS:
                    wf32[k] = wbuf[slot, k * strip * n_heads:(k + 1) * strip * n_heads].astype(jnp.float32)
                if k > 0:
                    at = pl.ds(pl.multiple_of(c * chunk + (k - 1) * strip, strip), strip)
                    for h in range(n_heads):
                        wall[t, at, h * hd:(h + 1) * hd] = wf32[k - 1, pl.ds(h, strip, stride=n_heads), :].astype(jnp.bfloat16)

            @pl.when(c + SLOTS < CHUNKS)
            def _():
                w_copy(t, c + SLOTS, slot).start()

            if t + 1 < len(w_refs):
                @pl.when(c + SLOTS >= CHUNKS)
                def _():
                    w_copy(t + 1, c + SLOTS - CHUNKS, slot).start()

    gather_start(0, x_ref, xr_ref)
    relayout(0)
    gather_pass(0, x_ref, xr_ref)
    gather_start(1, dy_ref, dyr_ref)
    relayout(1)
    wo_copy = pltpu.make_async_copy(wo_ref, wo_all, wo_sem)
    wo_copy.start()
    relayout(2)
    gather_end(0, x_ref, xr_ref)
    gather_pass(1, dy_ref, dyr_ref)

    mine_at = pl.ds(pl.multiple_of(me_c * hd, hd), hd)
    my_rows = pl.ds(pl.multiple_of(me_c * rows, rows), rows)

    def send_in(t, h):
        @pl.when(h != me_c)
        def _():
            pltpu.make_async_remote_copy(flat.at[t, :, pl.ds(pl.multiple_of(h * hd, hd), hd)], heads.at[t, my_rows],
                                         in_send.at[t], in_recv.at[t], device_id={"cp": h}, device_id_type=MESH).start()

    order = [s if s < cp else 2 * cp - 1 - s for s in range(2 * cp)]

    def wait_in(t):
        pltpu.make_async_copy(others, others, in_recv.at[t]).wait()
        heads[t, my_rows, :] = flat[t, :, mine_at]
        for b, s in enumerate(order):
            start = s * rows + (half if b >= cp else 0)
            sorted_heads[t, b * half:(b + 1) * half, :] = heads[t, start:start + half, :]

    pairs = cp // 2

    @pl.loop(0, 3 * pairs)
    def _(i):
        t = i // pairs
        pair = (me_c // 2 + 1 + i % pairs) % pairs
        at = pl.ds(pl.multiple_of(pair * 2 * hd, 2 * hd), 2 * hd)
        flat[t, :, at] = mm(xr_ref[...], wall[t, :, at]).astype(jnp.bfloat16)
        for e in range(2):
            send_in(t, pair * 2 + e)

    gather_end(1, dy_ref, dyr_ref)
    wo_copy.wait()

    @pl.loop(0, pairs)
    def _(i):
        pair = (me_c // 2 + 1 + i) % pairs
        at = pl.ds(pl.multiple_of(pair * 2 * hd, 2 * hd), 2 * hd)
        flat[3, :, at] = mm(dyr_ref[...], wo_all[at, :], NT).astype(jnp.bfloat16)
        for e in range(2):
            send_in(3, pair * 2 + e)

    outs = (o_ref, dq_ref, dk_ref, dv_ref)

    def put(t, i, value):
        for k in range(qb // half):
            b = i * (qb // half) + k
            start = order[b] * rows + (half if b >= cp else 0)
            out_heads[t, start:start + half, :] = value[k * half:(k + 1) * half]

    def send_out(t, i):
        done = walk[:walk.index(i) + 1]
        blocks_of = lambda i: range(i * (qb // half), (i + 1) * (qb // half))
        ready = [b for j in done for b in blocks_of(j)]
        now = [order[b] for b in blocks_of(i)]
        for s in sorted({s for s in now if all(b in ready for b in (s, 2 * cp - 1 - s))}):
            @pl.when(me_c != s)
            def _():
                pltpu.make_async_remote_copy(out_heads.at[t, pl.ds(s * rows, rows)], outs[t].at[:, mine_at],
                                             out_send.at[t], out_recv.at[t], device_id={"cp": s}, device_id_type=MESH).start()

    def wait_out(t):
        outs[t][:, mine_at] = out_heads[t, my_rows, :]
        pltpu.make_async_copy(others, others, out_recv.at[t]).wait()

    qb = min(256, total)
    blocks = total // qb
    walk = sorted(range(blocks), key=lambda i: -min(i, blocks - 1 - i))

    def causal(shape, q_start, k_start, q_axis):
        q_pos = lax.broadcasted_iota(jnp.int32, shape, q_axis) + q_start
        k_pos = lax.broadcasted_iota(jnp.int32, shape, 1 - q_axis) + k_start
        return q_pos >= k_pos

    for t in range(3):
        wait_in(t)
    for i in walk:
        at, n = pl.ds(i * qb, qb), (i + 1) * qb
        s = mm(sorted_heads[0, at, :], sorted_heads[1, :n, :], NT) * scale
        s = jnp.where(causal(s.shape, i * qb, 0, 0), s, -jnp.inf)
        m = jnp.max(s, axis=1, keepdims=True)
        p = jnp.exp(s - m)
        l = jnp.sum(p, axis=1, keepdims=True)
        o = mm(p.astype(jnp.bfloat16), sorted_heads[2, :n, :]) / l
        o = o.astype(jnp.bfloat16)
        sorted_o[at, :] = o
        put(0, i, o)
        stat[0, at, :] = jnp.broadcast_to(m + jnp.log(l), (qb, hd))
        send_out(0, i)

    wait_in(3)
    for i in range(blocks):
        at = pl.ds(i * qb, qb)
        delta = jnp.sum(sorted_heads[3, at, :].astype(jnp.float32) * sorted_o[at, :].astype(jnp.float32), axis=1, keepdims=True)
        stat[1, at, :] = jnp.broadcast_to(delta, (qb, hd))
    for j in range(2):
        for i in range(total // hd):
            stat_t[j, :, i * hd:(i + 1) * hd] = stat[j, i * hd:(i + 1) * hd, :].T[:8]

    for i in walk:
        at, n = pl.ds(i * qb, qb), (i + 1) * qb
        s = mm(sorted_heads[0, at, :], sorted_heads[1, :n, :], NT) * scale
        p = jnp.where(causal(s.shape, i * qb, 0, 0), jnp.exp(s - stat[0, at, :1]), 0.0)
        dp = mm(sorted_heads[3, at, :], sorted_heads[2, :n, :], NT)
        ds = (p * (dp - stat[1, at, :1])).astype(jnp.bfloat16)
        put(1, i, (mm(ds, sorted_heads[1, :n, :]) * scale).astype(jnp.bfloat16))
        send_out(1, i)
    width = dm // RS_TILES

    def rs_parts(tile, odd):
        onward, back = (left, right) if odd else (right, left)
        at = pl.ds(pl.multiple_of(tile * width, width), width)

        def mine(d):
            return (pl.ds(pl.multiple_of(d * rb, rb), rb), at)

        def copy(src, dst, send, recv, to):
            return pltpu.make_async_remote_copy(src, dst.at[tile], send.at[tile], recv.at[tile],
                                                device_id={"tp": to}, device_id_type=MESH)

        first = lambda: copy(part.at[mine(across)], r1, r1_send, r1_recv, onward)
        second = lambda: copy(s2.at[tile], r2, r2_send, r2_recv, onward)
        direct = lambda: copy(part.at[mine(back)], r3, r3_send, r3_recv, back)
        return at, mine, onward, first, second, direct

    def pairs_of_tiles(step):
        @pl.loop(0, RS_TILES // 2)
        def _(i):
            for odd in range(2):
                step(i * 2 + odd, odd)

    def reduce_first(tile, odd):
        at, _, _, first, _, _ = rs_parts(tile, odd)
        part[:, at] = mm(o_ref[...], wo_all[:, at])
        first().start()

    def reduce_direct(tile, odd):
        rs_parts(tile, odd)[5]().start()

    def reduce_second(tile, odd):
        _, mine, onward, first, second, _ = rs_parts(tile, odd)
        first().wait_recv()
        s2[tile] = r1[tile] + part[mine(onward)]
        second().start()

    def reduce_last(tile, odd):
        at, mine, _, first, second, direct = rs_parts(tile, odd)
        direct().wait_recv()
        second().wait_recv()
        y_ref[:, at] = (part[mine(me_t)] + r2[tile] + r3[tile]).astype(jnp.bfloat16)
        first().wait_send()
        second().wait_send()
        direct().wait_send()

    wait_out(0)
    pairs_of_tiles(reduce_first)
    pairs_of_tiles(reduce_direct)
    for i in walk:
        at, after = pl.ds(i * qb, qb), pl.ds(i * qb, total - i * qb)
        s = mm(sorted_heads[1, at, :], sorted_heads[0, after, :], NT) * scale
        p = jnp.where(causal(s.shape, 0, 0, 1), jnp.exp(s - stat_t[0, :1, after]), 0.0)
        dp = mm(sorted_heads[2, at, :], sorted_heads[3, after, :], NT)
        ds = (p * (dp - stat_t[1, :1, after])).astype(jnp.bfloat16)
        put(3, i, mm(p.astype(jnp.bfloat16), sorted_heads[3, after, :]).astype(jnp.bfloat16))
        send_out(3, i)
        put(2, i, (mm(ds, sorted_heads[0, after, :]) * scale).astype(jnp.bfloat16))
        send_out(2, i)

    pairs_of_tiles(reduce_second)

    for t in range(1, 4):
        wait_out(t)

    def dx_copy(tile, odd):
        spot = (pl.ds(pl.multiple_of(across * rb, rb), rb), pl.ds(pl.multiple_of((tile + odd * RS_TILES // 2) * width, width), width))
        return pltpu.make_async_remote_copy(dx_part.at[spot], r4.at[odd, tile], r4_send.at[odd, tile], r4_recv.at[odd, tile],
                                            device_id={"tp": left if odd else right}, device_id_type=MESH)

    def block_of(d, at):
        return dx_part[pl.ds(pl.multiple_of(d * rb, rb), rb), at]

    @pl.loop(0, RS_TILES // 2)
    def _(i):
        for odd, (back_ref, back) in enumerate(((back_l, left), (back_r, right))):
            at = pl.ds(pl.multiple_of((i + odd * RS_TILES // 2) * width, width), width)
            dx_part[:, at] = (mm(dq_ref[...], wall[0, at, :], NT) + mm(dk_ref[...], wall[1, at, :], NT)
                              + mm(dv_ref[...], wall[2, at, :], NT))
            dx_copy(i, odd).start()
            own_ref[:, at] = block_of(me_t, at)
            back_ref[:, pl.ds(pl.multiple_of(i * width, width), width)] = block_of(back, at)

    pairs_of_tiles(reduce_last)

    @pl.loop(0, RS_TILES // 2)
    def _(i):
        for odd, (on_ref, onward) in enumerate(((on_r, right), (on_l, left))):
            at = pl.ds(pl.multiple_of((i + odd * RS_TILES // 2) * width, width), width)
            dx_copy(i, odd).wait_recv()
            on_ref[:, pl.ds(pl.multiple_of(i * width, width), width)] = r4[odd, i] + block_of(onward, at)
            dx_copy(i, odd).wait_send()

    for t in range(4):
        for sem in (in_send, out_send):
            pltpu.make_async_copy(others, others, sem.at[t]).wait()
    for which, src, dst in ((0, x_ref, xr_ref), (1, dy_ref, dyr_ref)):
        for idx, col_half, to in ((0, 0, right), (1, 1, left), (2, 1, right), (3, 0, left)):
            gather_copy(src, dst, which, idx, me_t, col_half, to).wait_send()
        gather_copy(dst, dst, which, 4, left, 0, right).wait_send()
        gather_copy(dst, dst, which, 5, right, 1, left).wait_send()


def attention_call(tp, cp, x_blk, dy_blk, wq, wk, wv, wo):
    rb, dm = x_blk.shape
    rows = rb * tp
    hc, _ = wo.shape
    hd = hc // cp
    total = rows * cp
    bf, f32 = jnp.bfloat16, jnp.float32
    chunk = dm // CHUNKS
    width = dm // RS_TILES
    vmem, hbm = pl.BlockSpec(memory_space=pltpu.VMEM), pl.BlockSpec(memory_space=pl.ANY)
    out = lambda r, c: jax.ShapeDtypeStruct((r, c), bf)
    wide = lambda c: jax.ShapeDtypeStruct((rb, c), f32)
    dma = pltpu.SemaphoreType.DMA
    return pl.pallas_call(
        functools.partial(attention_kernel, tp, cp),
        out_shape=(out(rb, dm), wide(dm), *[wide(dm // 2)] * 4, out(rows, dm), out(rows, dm), out(rows, hc), out(rows, hc), out(rows, hc), out(rows, hc)),
        in_specs=[vmem, vmem, hbm, hbm, hbm, hbm],
        out_specs=[vmem] * 12,
        scratch_shapes=[
            pltpu.VMEM((SLOTS, chunk * cp, hd), bf), pltpu.VMEM((STRIPS, chunk // STRIPS * cp, hd), f32),
            pltpu.VMEM((3, dm, hc), bf), pltpu.VMEM((hc, dm), bf),
            pltpu.VMEM((4, rows, hc), bf), pltpu.VMEM((4, total, hd), bf),
            pltpu.VMEM((4, total, hd), bf), pltpu.VMEM((total, hd), bf), pltpu.VMEM((4, total, hd), bf),
            pltpu.VMEM((2, total, hd), f32), pltpu.VMEM((2, 8, total), f32),
            pltpu.VMEM((rows, dm), f32), pltpu.VMEM((rows, dm), f32),
            pltpu.VMEM((RS_TILES, rb, width), f32), pltpu.VMEM((RS_TILES, rb, width), f32),
            pltpu.VMEM((RS_TILES, rb, width), f32), pltpu.VMEM((RS_TILES, rb, width), f32),
            pltpu.VMEM((2, RS_TILES // 2, rb, width), f32),
            dma((SLOTS,)), dma, dma((2, 6)), dma((2, 6)), dma((4,)), dma((4,)), dma((4,)), dma((4,)),
            *[dma((RS_TILES,))] * 6, *[dma((2, RS_TILES // 2))] * 2,
        ],
        compiler_params=pltpu.CompilerParams(collective_id=0, has_side_effects=True, vmem_limit_bytes=VMEM_BYTES),
    )(x_blk, dy_blk, wq, wk, wv, wo)


def grad_kernel(n_heads, x_hbm, dy_hbm, o_hbm, dq_hbm, dk_hbm, dv_hbm, y_ref, gq_ref, gk_ref, gv_ref, go_ref, y_out,
                x_ref, dy_ref, o_ref, dq_ref, dk_ref, dv_ref, wide, grads, out_grad, in_sem, out_sem):
    rows, dm = x_ref.shape
    hd = wide.shape[-1]
    tiles = grads.shape[1]
    m_tile, o_tile = dm // tiles, n_heads * hd // tiles
    loads = [pltpu.make_async_copy(src, dst, in_sem.at[i]) for i, (src, dst) in enumerate(
        ((dq_hbm, dq_ref), (x_hbm, x_ref), (dk_hbm, dk_ref), (dv_hbm, dv_ref), (o_hbm, o_ref), (dy_hbm, dy_ref)))]
    for load in loads:
        load.start()
    y_out[...] = y_ref[...]
    for load in loads[:4]:
        load.wait()

    @pl.loop(0, tiles)
    def _(i):
        at = pl.ds(pl.multiple_of(i * m_tile, m_tile), m_tile)
        tall = pl.ds(pl.multiple_of(i * m_tile * n_heads, m_tile * n_heads), m_tile * n_heads)
        x_t = x_ref[:, at].T
        for t, (d_ref, g_ref) in enumerate(((dq_ref, gq_ref), (dk_ref, gk_ref), (dv_ref, gv_ref))):
            for h in range(0, n_heads, 2):
                grad = mm(x_t, d_ref[:, h * hd:(h + 2) * hd])
                for e in range(2):
                    wide[t, pl.ds(h + e, m_tile, stride=n_heads), :] = grad[:, e * hd:(e + 1) * hd]
            grads[t, i] = wide[t].astype(jnp.bfloat16)
            pltpu.make_async_copy(grads.at[t, i], g_ref.at[tall], out_sem.at[t]).start()

    for load in loads[4:]:
        load.wait()

    @pl.loop(0, tiles)
    def _(i):
        at = pl.ds(pl.multiple_of(i * o_tile, o_tile), o_tile)
        out_grad[at, :] = mm(o_ref[:, at], dy_ref[...], TN).astype(jnp.bfloat16)
        pltpu.make_async_copy(out_grad.at[at], go_ref.at[at], out_sem.at[3]).start()

    for t, g_ref in enumerate((gq_ref, gk_ref, gv_ref, go_ref)):
        pltpu.make_async_copy(g_ref, g_ref, out_sem.at[t]).wait()


def grad_call(n_heads, x_rows, dy_rows, o_flat, dq, dk, dv, y_blk):
    rows, dm = x_rows.shape
    hc = o_flat.shape[1]
    hd = hc // n_heads
    tiles = n_heads
    bf, f32 = jnp.bfloat16, jnp.float32
    hbm, vmem = pl.BlockSpec(memory_space=pl.ANY), pl.BlockSpec(memory_space=pltpu.VMEM)
    inputs = (x_rows, dy_rows, o_flat, dq, dk, dv)
    return pl.pallas_call(
        functools.partial(grad_kernel, n_heads),
        out_shape=[jax.ShapeDtypeStruct((dm * n_heads, hd), bf)] * 3 + [jax.ShapeDtypeStruct((hc, dm), bf), jax.ShapeDtypeStruct(y_blk.shape, bf)],
        in_specs=[hbm] * 6 + [vmem],
        out_specs=[hbm] * 4 + [vmem],
        scratch_shapes=[*[pltpu.VMEM(a.shape, bf) for a in inputs],
                        pltpu.VMEM((3, dm // tiles * n_heads, hd), f32), pltpu.VMEM((3, tiles, dm // tiles * n_heads, hd), bf),
                        pltpu.VMEM((hc, dm), bf), pltpu.SemaphoreType.DMA((6,)), pltpu.SemaphoreType.DMA((4,))],
        compiler_params=pltpu.CompilerParams(vmem_limit_bytes=VMEM_BYTES),
        cost_estimate=pl.CostEstimate(flops=8 * rows * dm * hc, bytes_accessed=8 * dm * hc + 8 * rows * dm, transcendentals=0),
    )(*inputs, y_blk)


def add_kernel(own, direct_a, last_a, direct_b, last_b, dx_ref):
    cols = direct_a.shape[1]
    dx_ref[:, :cols] = (own[:, :cols] + direct_a[...] + last_a[...]).astype(jnp.bfloat16)
    dx_ref[:, cols:] = (own[:, cols:] + direct_b[...] + last_b[...]).astype(jnp.bfloat16)


def solution(mesh):
    tp, cp = mesh.shape["tp"], mesh.shape["cp"]

    def device_fn(x_blk, w_query, w_key, w_value, w_out, dy_blk):
        dm, n_heads, hd = w_query.shape
        if tp != 4 or n_heads != cp or w_key.shape != w_query.shape:
            raise ValueError("unsupported split")
        tall = lambda w: w.reshape(dm * n_heads, hd)
        y_blk, own, back_l, back_r, on_r, on_l, x_rows, dy_rows, o_flat, dq, dk, dv = attention_call(
            tp, cp, x_blk, dy_blk, tall(w_query), tall(w_key), tall(w_value), w_out.reshape(n_heads * hd, dm))
        to_right = lambda a: lax.ppermute(a, "tp", [(i, (i + 1) % tp) for i in range(tp)])
        to_left = lambda a: lax.ppermute(a, "tp", [(i, (i - 1) % tp) for i in range(tp)])
        last_a, last_b, direct_a, direct_b = to_right(on_r), to_left(on_l), to_left(back_l), to_right(back_r)
        gq, gk, gv, go, y_blk = grad_call(n_heads, x_rows, dy_rows, o_flat, dq, dk, dv, y_blk)
        vmem = pl.BlockSpec(memory_space=pltpu.VMEM)
        dx_blk = pl.pallas_call(add_kernel, out_shape=jax.ShapeDtypeStruct(own.shape, jnp.bfloat16), in_specs=[vmem] * 5, out_specs=vmem)(
            own, direct_a, last_a, direct_b, last_b)
        split = lambda g: g.reshape(1, dm, n_heads, hd)
        return y_blk, dx_blk, split(gq), split(gk), split(gv), go.reshape(1, n_heads, hd, dm)

    return jax.shard_map(device_fn, mesh=mesh,
                         in_specs=(ROW_SPEC, HEAD_SPEC, HEAD_SPEC, HEAD_SPEC, OUT_W_SPEC, ROW_SPEC),
                         out_specs=(ROW_SPEC, ROW_SPEC, GRAD_SPEC, GRAD_SPEC, GRAD_SPEC, GRAD_OUT_SPEC),
                         check_vma=False)
```

time: 106 us -> 101 us (0.953)
  other arithmetic: 5.66 us -> 0 us
  Pallas kernels: 91.5 us -> 95 us
  starting transfers between devices: 6.9 us -> 4.67 us
    add x2 -> x0, other arithmetic: 3.51 us -> none  [device_fn(): sum_r, sum_l = (on_r + came_r, on_l + came_l)]
    pallas_call x1, Pallas kernels: 69.4 us -> 71.9 us  [attention_call(): pl.pallas_call(functools.partial(attention_kernel, tp, cp), out_shape=(ou...]
    ppermute x3 -> x2, starting transfers between devices: 1.56 us -> 0.01 us  [device_fn(): lax.ppermute(a, 'tp', [(i, (i + 1) % tp) for i in range(tp)])]
    another operation x1 -> x0, other arithmetic: 1.43 us -> none
    ppermute x3 -> x2, starting transfers between devices: 5.34 us -> 4.66 us  [device_fn(): lax.ppermute(a, 'tp', [(i, (i - 1) % tp) for i in range(tp)])]
  transfers between devices with their start and end apart: 6 -> 4, of which waited for: 0 -> 0; matrix products, arithmetic and copies ran while one was open for 3% -> 0% of each run, Pallas kernels for 21% -> 21%
where the time goes in v3:
time: 101 us; the launch traced here: 100 us
  Pallas kernels  95 us (94%)
  starting transfers between devices  4.67 us (5%)
    pallas_call x1, Pallas kernels, attention_call(): pl.pallas_call(functools.partial(attention_kernel, tp, cp), out_shape=(ou...  71.9 us
    pallas_call x1, Pallas kernels, grad_call(): pl.pallas_call(functools.partial(grad_kernel, n_heads), out_shape=[jax.Sh...  20.9 us
    ppermute x2, starting transfers between devices, device_fn(): lax.ppermute(a, 'tp', [(i, (i - 1) % tp) for i in range(tp)])  4.66 us
    pallas_call x1, Pallas kernels, device_fn(): pl.pallas_call(add_kernel, out_shape=jax.ShapeDtypeStruct(own.shape, jnp....  2.12 us
  transfers between devices with their start and end apart: 4, of which 0 were waited for; matrix products, arithmetic and copies ran while one was open for 0% of the time, Pallas kernels for 21%

profile of v3, /device:TPU:97, one launch (start us, length us, event | category | flops | bytes accessed | tf_op | source)
XLA Modules:
  0.0 100.4 jit_solution(8826582559696989849)
XLA Ops:
  0.6 71.9 %shard_map.109 = (bf16[32,4096]{1,0:T(8,128)(2,1)}, f32[32,4096]{1,0:T(8,128)}, f32[32,2048]{1,0:T(8,128)}, f32[32,2048]{1,0:T(8,128)}, f32[32,2048]{1,0:T(8,128...) custom-call(bf16[32,4096]{1,0:T(8,128)(2,1)} %refs_0_.1, ...), custom_call_target="tpu_custom_call" | custom-call | tf_op jit(solution)/shard_map/pallas_call | solution.py:343
  72.6 2.0 %collective-permute-start = (f32[32,2048]{1,0:T(8,128)}, f32[32,2048]{1,0:T(8,128)}, u32[]{:S(2)}, u32[]{:S(2)}) collective-permute-start(f32[32,2048]{1,0:T(8,128)} %get-tuple-element.32), channel_id=1, source_target_pairs={{0,24},{8,0},{16,8},{24,16},{1,25},{9,1},{17,9},{25,17},{2,26},{10... | collective-permute-start | bytes 786440 | tf_op jit(solution)/shard_map/ppermute | solution.py:443
  74.6 0.0 collective-permute-start.1
  74.6 0.0 collective-permute-start.2
  74.6 2.7 %collective-permute-start.3 = (f32[32,2048]{1,0:T(8,128)}, f32[32,2048]{1,0:T(8,128)}, u32[]{:S(2)}, u32[]{:S(2)}) collective-permute-start(f32[32,2048]{1,0:T(8,128)} %get-tuple-element.35), channel_id=1, source_target_pairs={{0,24},{8,0},{16,8},{24,16},{1,25},{9,1},{17,9},{25,17},{2,26},{10... | collective-permute-start | bytes 786440 | tf_op jit(solution)/shard_map/ppermute | solution.py:443
  77.3 20.9 %shard_map.110 = (bf16[32768,128]{1,0:T(8,128)(2,1)}, bf16[32768,128]{1,0:T(8,128)(2,1)}, bf16[32768,128]{1,0:T(8,128)(2,1)}, bf16[1024,4096]{1,0:T(8,128)(2,1)}, bf16[32,4096]{1,0:T(8,128)(2,1)}) custom-call(bf16[128,4096]{1,0:T(8,128)(2,1)} %get-tuple-element.23.x_hbm, bf16[128,4096]{1,0:T(8,128)(2,1)} %get-tuple-element.24.dy_hbm, ...), custom_call_target="tpu_custom_call" | custom-call | flops 4294967296 | bytes 37748736 | tf_op jit(solution)/shard_map/pallas_call | solution.py:413
  98.2 0.0 collective-permute-done.direct_a
  98.2 0.0 collective-permute-done.1.last_a
  98.2 0.0 collective-permute-done.2.direct_b
  98.2 0.0 collective-permute-done.3.last_b
  98.2 2.1 %shard_map.111 = bf16[32,4096]{1,0:T(8,128)(2,1)} custom-call(f32[32,4096]{1,0:T(8,128)} %get-tuple-element.31.own, f32[32,2048]{1,0:T(8,128)} %collective-permute-done.direct_a, f32[32,2048]{1,0:T(8,128)} %collective-permute-done.1.last_a, f32[32,2048]{1,0:T(8,128)} %collective-permute-done.2.direct_b, f32[32,2048]{1,0:T(8,128)} %collective-permute-done.3.last_b), custom_call_target="tpu_custom_call" | custom-call | tf_op jit(solution)/shard_map/pallas_call | solution.py:447
Async XLA Ops:
  72.6 25.6 %collective-permute-start = (f32[32,2048]{1,0:T(8,128)}, f32[32,2048]{1,0:T(8,128)}, u32[]{:S(2)}, u32[]{:S(2)}) collective-permute-start(f32[32,2048]{1,0:T(8,128)} %get-tuple-element.32), channel_id=1, source_target_pairs={{0,24},{8,0},{16,8},{24,16},{1,25},{9,1},{17,9},{25,17},{2,26},{10... | collective-permute-start | bytes 786440 | tf_op jit(solution)/shard_map/ppermute | solution.py:443
  74.6 23.6 %collective-permute-start.1 = (f32[32,2048]{1,0:T(8,128)}, f32[32,2048]{1,0:T(8,128)}, u32[]{:S(2)}, u32[]{:S(2)}) collective-permute-start(f32[32,2048]{1,0:T(8,128)} %get-tuple-element.33), channel_id=1, source_target_pairs={{0,8},{8,16},{16,24},{24,0},{1,9},{9,17},{17,25},{25,1},{2,10},{10... | collective-permute-start | bytes 786440 | tf_op jit(solution)/shard_map/ppermute | solution.py:442
  74.6 23.7 %collective-permute-start.2 = (f32[32,2048]{1,0:T(8,128)}, f32[32,2048]{1,0:T(8,128)}, u32[]{:S(2)}, u32[]{:S(2)}) collective-permute-start(f32[32,2048]{1,0:T(8,128)} %get-tuple-element.34), channel_id=1, source_target_pairs={{0,8},{8,16},{16,24},{24,0},{1,9},{9,17},{17,25},{25,1},{2,10},{10... | collective-permute-start | bytes 786440 | tf_op jit(solution)/shard_map/ppermute | solution.py:442
  74.6 23.7 %collective-permute-start.3 = (f32[32,2048]{1,0:T(8,128)}, f32[32,2048]{1,0:T(8,128)}, u32[]{:S(2)}, u32[]{:S(2)}) collective-permute-start(f32[32,2048]{1,0:T(8,128)} %get-tuple-element.35), channel_id=1, source_target_pairs={{0,24},{8,0},{16,8},{24,16},{1,25},{9,1},{17,9},{25,17},{2,26},{10... | collective-permute-start | bytes 786440 | tf_op jit(solution)/shard_map/ppermute | solution.py:443

commit v4 on v3

--- a/solution.py
+++ b/solution.py
@@ -21,6 +21,7 @@
 CHUNKS = 16
 SLOTS = 8
 STRIPS = 4
+PITCH = 12
 
 
 def mm(a, b, dims=NN):
@@ -29,10 +30,10 @@
 
 def attention_kernel(tp, cp, *refs):
     (x_ref, dy_ref, wq_ref, wk_ref, wv_ref, wo_ref,
-     y_ref, own_ref, back_l, back_r, on_r, on_l, xr_ref, dyr_ref, o_ref, dq_ref, dk_ref, dv_ref,
-     wbuf, wf32, wall, wo_all, flat, heads, sorted_heads, sorted_o, out_heads, stat, stat_t,
+     y_ref, own_ref, back_l, back_r, on_r, on_l, x_out, dy_out, o_ref, dq_ref, dk_ref, dv_ref,
+     xr_ref, dyr_ref, wbuf, wf32, wall, wo_all, flat, heads, sorted_heads, sorted_o, out_heads, stat, stat_t,
      part, dx_part, r1, r2, r3, s2, r4,
-     w_sem, wo_sem, ag_send, ag_recv, in_send, in_recv, out_send, out_recv,
+     w_sem, wo_sem, row_sem, ag_send, ag_recv, in_send, in_recv, out_send, out_recv,
      r1_send, r1_recv, r2_send, r2_recv, r3_send, r3_recv, r4_send, r4_recv) = refs
     me_t, me_c = lax.axis_index("tp"), lax.axis_index("cp")
     right, left, across = (me_t + 1) % tp, (me_t + tp - 1) % tp, (me_t + 2) % tp
@@ -84,6 +85,8 @@
         gather_copy(dst, dst, which, 4, across, 0, right).wait_recv()
         gather_copy(dst, dst, which, 5, across, 1, left).wait_recv()
 
+    pitch = wf32.shape[1] // (chunk // STRIPS)
+
     def relayout(t):
         @pl.loop(0, CHUNKS)
         def _(c):
@@ -92,11 +95,15 @@
             strip = chunk // STRIPS
             for k in range(STRIPS + 1):
                 if k < STRIPS:
-                    wf32[k] = wbuf[slot, k * strip * n_heads:(k + 1) * strip * n_heads].astype(jnp.float32)
+                    for r in range(0, strip, 2):
+                        at = (k * strip + r) * n_heads
+                        pair = wbuf[slot, at:at + 2 * n_heads].astype(jnp.float32)
+                        for e in range(2):
+                            wf32[k, (r + e) * pitch:(r + e) * pitch + n_heads] = pair[e * n_heads:(e + 1) * n_heads]
                 if k > 0:
                     at = pl.ds(pl.multiple_of(c * chunk + (k - 1) * strip, strip), strip)
                     for h in range(n_heads):
-                        wall[t, at, h * hd:(h + 1) * hd] = wf32[k - 1, pl.ds(h, strip, stride=n_heads), :].astype(jnp.bfloat16)
+                        wall[t, at, h * hd:(h + 1) * hd] = wf32[k - 1, pl.ds(h, strip, stride=pitch), :].astype(jnp.bfloat16)
 
             @pl.when(c + SLOTS < CHUNKS)
             def _():
@@ -116,6 +123,8 @@
     wo_copy.start()
     relayout(2)
     gather_end(0, x_ref, xr_ref)
+    x_copy = pltpu.make_async_copy(xr_ref, x_out, row_sem.at[0])
+    x_copy.start()
     gather_pass(1, dy_ref, dyr_ref)
 
     mine_at = pl.ds(pl.multiple_of(me_c * hd, hd), hd)
@@ -148,6 +157,8 @@
             send_in(t, pair * 2 + e)
 
     gather_end(1, dy_ref, dyr_ref)
+    dy_copy = pltpu.make_async_copy(dyr_ref, dy_out, row_sem.at[1])
+    dy_copy.start()
     wo_copy.wait()
 
     @pl.loop(0, pairs)
@@ -286,8 +297,6 @@
 
     pairs_of_tiles(reduce_second)
 
-    for t in range(1, 4):
-        wait_out(t)
 
     def dx_copy(tile, odd):
         spot = (pl.ds(pl.multiple_of(across * rb, rb), rb), pl.ds(pl.multiple_of((tile + odd * RS_TILES // 2) * width, width), width))
@@ -297,12 +306,25 @@
     def block_of(d, at):
         return dx_part[pl.ds(pl.multiple_of(d * rb, rb), rb), at]
 
+    def dx_term(t, w, at):
+        return mm(outs[t][...], wall[w, at, :], NT)
+
+    for t, w in ((1, 0), (3, 2)):
+        wait_out(t)
+
+        @pl.loop(0, RS_TILES)
+        def _(i):
+            at = pl.ds(pl.multiple_of(i * width, width), width)
+            term = dx_term(t, w, at)
+            dx_part[:, at] = term if t == 1 else dx_part[:, at] + term
+
+    wait_out(2)
+
     @pl.loop(0, RS_TILES // 2)
     def _(i):
         for odd, (back_ref, back) in enumerate(((back_l, left), (back_r, right))):
             at = pl.ds(pl.multiple_of((i + odd * RS_TILES // 2) * width, width), width)
-            dx_part[:, at] = (mm(dq_ref[...], wall[0, at, :], NT) + mm(dk_ref[...], wall[1, at, :], NT)
-                              + mm(dv_ref[...], wall[2, at, :], NT))
+            dx_part[:, at] += dx_term(2, 1, at)
             dx_copy(i, odd).start()
             own_ref[:, at] = block_of(me_t, at)
             back_ref[:, pl.ds(pl.multiple_of(i * width, width), width)] = block_of(back, at)
@@ -317,6 +339,8 @@
             on_ref[:, pl.ds(pl.multiple_of(i * width, width), width)] = r4[odd, i] + block_of(onward, at)
             dx_copy(i, odd).wait_send()
 
+    x_copy.wait()
+    dy_copy.wait()
     for t in range(4):
         for sem in (in_send, out_send):
             pltpu.make_async_copy(others, others, sem.at[t]).wait()
@@ -344,9 +368,10 @@
         functools.partial(attention_kernel, tp, cp),
         out_shape=(out(rb, dm), wide(dm), *[wide(dm // 2)] * 4, out(rows, dm), out(rows, dm), out(rows, hc), out(rows, hc), out(rows, hc), out(rows, hc)),
         in_specs=[vmem, vmem, hbm, hbm, hbm, hbm],
-        out_specs=[vmem] * 12,
+        out_specs=[vmem] * 6 + [hbm] * 2 + [vmem] * 4,
         scratch_shapes=[
-            pltpu.VMEM((SLOTS, chunk * cp, hd), bf), pltpu.VMEM((STRIPS, chunk // STRIPS * cp, hd), f32),
+            pltpu.VMEM((rows, dm), bf), pltpu.VMEM((rows, dm), bf),
+            pltpu.VMEM((SLOTS, chunk * cp, hd), bf), pltpu.VMEM((STRIPS, chunk // STRIPS * max(cp, PITCH), hd), f32),
             pltpu.VMEM((3, dm, hc), bf), pltpu.VMEM((hc, dm), bf),
             pltpu.VMEM((4, rows, hc), bf), pltpu.VMEM((4, total, hd), bf),
             pltpu.VMEM((4, total, hd), bf), pltpu.VMEM((total, hd), bf), pltpu.VMEM((4, total, hd), bf),
@@ -355,7 +380,7 @@
             pltpu.VMEM((RS_TILES, rb, width), f32), pltpu.VMEM((RS_TILES, rb, width), f32),
             pltpu.VMEM((RS_TILES, rb, width), f32), pltpu.VMEM((RS_TILES, rb, width), f32),
             pltpu.VMEM((2, RS_TILES // 2, rb, width), f32),
-            dma((SLOTS,)), dma, dma((2, 6)), dma((2, 6)), dma((4,)), dma((4,)), dma((4,)), dma((4,)),
+            dma((SLOTS,)), dma, dma((2,)), dma((2, 6)), dma((2, 6)), dma((4,)), dma((4,)), dma((4,)), dma((4,)),
             *[dma((RS_TILES,))] * 6, *[dma((2, RS_TILES // 2))] * 2,
         ],
         compiler_params=pltpu.CompilerParams(collective_id=0, has_side_effects=True, vmem_limit_bytes=VMEM_BYTES),
@@ -368,6 +393,7 @@
     hd = wide.shape[-1]
     tiles = grads.shape[1]
     m_tile, o_tile = dm // tiles, n_heads * hd // tiles
+    pitch = wide.shape[1] // m_tile
     loads = [pltpu.make_async_copy(src, dst, in_sem.at[i]) for i, (src, dst) in enumerate(
         ((dq_hbm, dq_ref), (x_hbm, x_ref), (dk_hbm, dk_ref), (dv_hbm, dv_ref), (o_hbm, o_ref), (dy_hbm, dy_ref)))]
     for load in loads:
@@ -385,8 +411,10 @@
             for h in range(0, n_heads, 2):
                 grad = mm(x_t, d_ref[:, h * hd:(h + 2) * hd])
                 for e in range(2):
-                    wide[t, pl.ds(h + e, m_tile, stride=n_heads), :] = grad[:, e * hd:(e + 1) * hd]
-            grads[t, i] = wide[t].astype(jnp.bfloat16)
+                    wide[t, pl.ds(h + e, m_tile, stride=pitch), :] = grad[:, e * hd:(e + 1) * hd]
+            for r in range(0, m_tile, 2):
+                pair = jnp.concatenate([wide[t, (r + e) * pitch:(r + e) * pitch + n_heads, :] for e in range(2)], axis=0)
+                grads[t, i, r * n_heads:(r + 2) * n_heads, :] = pair.astype(jnp.bfloat16)
             pltpu.make_async_copy(grads.at[t, i], g_ref.at[tall], out_sem.at[t]).start()
 
     for load in loads[4:]:
@@ -416,7 +444,7 @@
         in_specs=[hbm] * 6 + [vmem],
         out_specs=[hbm] * 4 + [vmem],
         scratch_shapes=[*[pltpu.VMEM(a.shape, bf) for a in inputs],
-                        pltpu.VMEM((3, dm // tiles * n_heads, hd), f32), pltpu.VMEM((3, tiles, dm // tiles * n_heads, hd), bf),
+                        pltpu.VMEM((3, dm // tiles * max(n_heads, PITCH), hd), f32), pltpu.VMEM((3, tiles, dm // tiles * n_heads, hd), bf),
                         pltpu.VMEM((hc, dm), bf), pltpu.SemaphoreType.DMA((6,)), pltpu.SemaphoreType.DMA((4,))],
         compiler_params=pltpu.CompilerParams(vmem_limit_bytes=VMEM_BYTES),
         cost_estimate=pl.CostEstimate(flops=8 * rows * dm * hc, bytes_accessed=8 * dm * hc + 8 * rows * dm, transcendentals=0),

time: 101 us -> 95 us (0.941)
  Pallas kernels: 95 us -> 89.9 us
    pallas_call x1, Pallas kernels: 20.9 us -> 17.3 us  [grad_call(): pl.pallas_call(functools.partial(grad_kernel, n_heads), out_shape=[jax.Sh...]
    pallas_call x1, Pallas kernels: 71.9 us -> 70.5 us  [attention_call(): pl.pallas_call(functools.partial(attention_kernel, tp, cp), out_shape=(ou...]
  transfers between devices with their start and end apart: 4 -> 4, of which waited for: 0 -> 0; matrix products, arithmetic and copies ran while one was open for 0% -> 0% of each run, Pallas kernels for 21% -> 18%
where the time goes in v4:
time: 95 us; the launch traced here: 94.8 us
  Pallas kernels  89.9 us (95%)
  starting transfers between devices  4.23 us (4%)
    pallas_call x1, Pallas kernels, attention_call(): pl.pallas_call(functools.partial(attention_kernel, tp, cp), out_shape=(ou...  70.5 us
    pallas_call x1, Pallas kernels, grad_call(): pl.pallas_call(functools.partial(grad_kernel, n_heads), out_shape=[jax.Sh...  17.3 us
    ppermute x2, starting transfers between devices, device_fn(): lax.ppermute(a, 'tp', [(i, (i - 1) % tp) for i in range(tp)])  3.85 us
    pallas_call x1, Pallas kernels, device_fn(): pl.pallas_call(add_kernel, out_shape=jax.ShapeDtypeStruct(own.shape, jnp....  2.12 us
  transfers between devices with their start and end apart: 4, of which 0 were waited for; matrix products, arithmetic and copies ran while one was open for 0% of the time, Pallas kernels for 18%

profile of v4, /device:TPU:97, one launch (start us, length us, event | category | flops | bytes accessed | tf_op | source)
XLA Modules:
  0.0 94.8 jit_solution(10165704100559745951)
XLA Ops:
  0.6 70.5 %shard_map.109 = (bf16[32,4096]{1,0:T(8,128)(2,1)}, f32[32,4096]{1,0:T(8,128)}, f32[32,2048]{1,0:T(8,128)}, f32[32,2048]{1,0:T(8,128)}, f32[32,2048]{1,0:T(8,128...) custom-call(bf16[32,4096]{1,0:T(8,128)(2,1)} %refs_0_.1, ...), custom_call_target="tpu_custom_call" | custom-call | tf_op jit(solution)/shard_map/pallas_call | solution.py:367
  71.1 1.2 %collective-permute-start = (f32[32,2048]{1,0:T(8,128)}, f32[32,2048]{1,0:T(8,128)}, u32[]{:S(2)}, u32[]{:S(2)}) collective-permute-start(f32[32,2048]{1,0:T(8,128)} %get-tuple-element.32), channel_id=1, source_target_pairs={{0,24},{8,0},{16,8},{24,16},{1,25},{9,1},{17,9},{25,17},{2,26},{10... | collective-permute-start | bytes 786440 | tf_op jit(solution)/shard_map/ppermute | solution.py:471
  72.3 0.4 collective-permute-start.1
  72.7 0.0 collective-permute-start.2
  72.7 2.7 %collective-permute-start.3 = (f32[32,2048]{1,0:T(8,128)}, f32[32,2048]{1,0:T(8,128)}, u32[]{:S(2)}, u32[]{:S(2)}) collective-permute-start(f32[32,2048]{1,0:T(8,128)} %get-tuple-element.35), channel_id=1, source_target_pairs={{0,24},{8,0},{16,8},{24,16},{1,25},{9,1},{17,9},{25,17},{2,26},{10... | collective-permute-start | bytes 786440 | tf_op jit(solution)/shard_map/ppermute | solution.py:471
  75.4 17.3 %shard_map.110 = (bf16[32768,128]{1,0:T(8,128)(2,1)}, bf16[32768,128]{1,0:T(8,128)(2,1)}, bf16[32768,128]{1,0:T(8,128)(2,1)}, bf16[1024,4096]{1,0:T(8,128)(2,1)}, bf16[32,4096]{1,0:T(8,128)(2,1)}) custom-call(bf16[128,4096]{1,0:T(8,128)(2,1)} %get-tuple-element.23.x_hbm, bf16[128,4096]{1,0:T(8,128)(2,1)} %get-tuple-element.24.dy_hbm, ...), custom_call_target="tpu_custom_call" | custom-call | flops 4294967296 | bytes 37748736 | tf_op jit(solution)/shard_map/pallas_call | solution.py:441
  92.7 0.0 collective-permute-done.direct_a
  92.7 0.0 collective-permute-done.1.last_a
  92.7 0.0 collective-permute-done.2.direct_b
  92.7 0.0 collective-permute-done.3.last_b
  92.7 2.1 %shard_map.111 = bf16[32,4096]{1,0:T(8,128)(2,1)} custom-call(f32[32,4096]{1,0:T(8,128)} %get-tuple-element.31.own, f32[32,2048]{1,0:T(8,128)} %collective-permute-done.direct_a, f32[32,2048]{1,0:T(8,128)} %collective-permute-done.1.last_a, f32[32,2048]{1,0:T(8,128)} %collective-permute-done.2.direct_b, f32[32,2048]{1,0:T(8,128)} %collective-permute-done.3.last_b), custom_call_target="tpu_custom_call" | custom-call | tf_op jit(solution)/shard_map/pallas_call | solution.py:475
Async XLA Ops:
  71.1 21.5 %collective-permute-start = (f32[32,2048]{1,0:T(8,128)}, f32[32,2048]{1,0:T(8,128)}, u32[]{:S(2)}, u32[]{:S(2)}) collective-permute-start(f32[32,2048]{1,0:T(8,128)} %get-tuple-element.32), channel_id=1, source_target_pairs={{0,24},{8,0},{16,8},{24,16},{1,25},{9,1},{17,9},{25,17},{2,26},{10... | collective-permute-start | bytes 786440 | tf_op jit(solution)/shard_map/ppermute | solution.py:471
  72.3 20.3 %collective-permute-start.1 = (f32[32,2048]{1,0:T(8,128)}, f32[32,2048]{1,0:T(8,128)}, u32[]{:S(2)}, u32[]{:S(2)}) collective-permute-start(f32[32,2048]{1,0:T(8,128)} %get-tuple-element.33), channel_id=1, source_target_pairs={{0,8},{8,16},{16,24},{24,0},{1,9},{9,17},{17,25},{25,1},{2,10},{10... | collective-permute-start | bytes 786440 | tf_op jit(solution)/shard_map/ppermute | solution.py:470
  72.7 20.0 %collective-permute-start.2 = (f32[32,2048]{1,0:T(8,128)}, f32[32,2048]{1,0:T(8,128)}, u32[]{:S(2)}, u32[]{:S(2)}) collective-permute-start(f32[32,2048]{1,0:T(8,128)} %get-tuple-element.34), channel_id=1, source_target_pairs={{0,8},{8,16},{16,24},{24,0},{1,9},{9,17},{17,25},{25,1},{2,10},{10... | collective-permute-start | bytes 786440 | tf_op jit(solution)/shard_map/ppermute | solution.py:470
  72.7 20.0 %collective-permute-start.3 = (f32[32,2048]{1,0:T(8,128)}, f32[32,2048]{1,0:T(8,128)}, u32[]{:S(2)}, u32[]{:S(2)}) collective-permute-start(f32[32,2048]{1,0:T(8,128)} %get-tuple-element.35), channel_id=1, source_target_pairs={{0,24},{8,0},{16,8},{24,16},{1,25},{9,1},{17,9},{25,17},{2,26},{10... | collective-permute-start | bytes 786440 | tf_op jit(solution)/shard_map/ppermute | solution.py:471

commit v5 on v4

--- a/solution.py
+++ b/solution.py
@@ -29,11 +29,11 @@
 
 
 def attention_kernel(tp, cp, *refs):
-    (x_ref, dy_ref, wq_ref, wk_ref, wv_ref, wo_ref,
+    (x_hbm, dy_hbm, wq_ref, wk_ref, wv_ref, wo_ref,
      y_ref, own_ref, back_l, back_r, on_r, on_l, x_out, dy_out, o_ref, dq_ref, dk_ref, dv_ref,
-     xr_ref, dyr_ref, wbuf, wf32, wall, wo_all, flat, heads, sorted_heads, sorted_o, out_heads, stat, stat_t,
+     x_ref, dy_ref, xr_ref, dyr_ref, wbuf, wf32, wall, wo_all, flat, heads, relay, sorted_heads, sorted_o, out_heads, stat, stat_t,
      part, dx_part, r1, r2, r3, s2, r4,
-     w_sem, wo_sem, row_sem, ag_send, ag_recv, in_send, in_recv, out_send, out_recv,
+     w_sem, wo_sem, load_sem, row_sem, ag_send, ag_recv, in_send, in_recv, relay_send, relay_recv, out_send, out_recv,
      r1_send, r1_recv, r2_send, r2_recv, r3_send, r3_recv, r4_send, r4_recv) = refs
     me_t, me_c = lax.axis_index("tp"), lax.axis_index("cp")
     right, left, across = (me_t + 1) % tp, (me_t + tp - 1) % tp, (me_t + 2) % tp
@@ -52,6 +52,9 @@
     def w_copy(t, c, slot):
         return pltpu.make_async_copy(w_refs[t].at[pl.ds(c * chunk * n_heads, chunk * n_heads)], wbuf.at[slot], w_sem.at[slot])
 
+    loads = [pltpu.make_async_copy(src, dst, load_sem.at[i]) for i, (src, dst) in enumerate(((x_hbm, x_ref), (dy_hbm, dy_ref)))]
+    for load in loads:
+        load.start()
     for c in range(SLOTS):
         w_copy(0, c, c).start()
 
@@ -114,6 +117,8 @@
                 def _():
                     w_copy(t + 1, c + SLOTS - CHUNKS, slot).start()
 
+    for load in loads:
+        load.wait()
     gather_start(0, x_ref, xr_ref)
     relayout(0)
     gather_pass(0, x_ref, xr_ref)
@@ -146,28 +151,55 @@
             sorted_heads[t, b * half:(b + 1) * half, :] = heads[t, start:start + half, :]
 
     pairs = cp // 2
-
-    @pl.loop(0, 3 * pairs)
-    def _(i):
-        t = i // pairs
-        pair = (me_c // 2 + 1 + i % pairs) % pairs
-        at = pl.ds(pl.multiple_of(pair * 2 * hd, 2 * hd), 2 * hd)
-        flat[t, :, at] = mm(xr_ref[...], wall[t, :, at]).astype(jnp.bfloat16)
-        for e in range(2):
-            send_in(t, pair * 2 + e)
+    chip, core = me_c // 2, me_c % 2
+    ways = ((1, 0), (pairs - 1, half)) if pairs == 4 else ()
+
+    def relay_start(t):
+        for d, (step, start) in enumerate(ways):
+            far = pl.ds(pl.multiple_of((chip + 2) % pairs * 2 * hd, 2 * hd), 2 * hd)
+            pltpu.make_async_remote_copy(flat.at[t, pl.ds(start, half), far], relay.at[t, d], relay_send.at[t, d], relay_recv.at[t, d],
+                                         device_id={"cp": (chip + step) % pairs * 2 + core}, device_id_type=MESH).start()
+
+    def relay_wait(t, d, sem):
+        pltpu.make_async_copy(relay.at[t, d], relay.at[t, d], sem.at[t, d]).wait()
+
+    def relay_pass(t):
+        for d, (step, start) in enumerate(ways):
+            relay_wait(t, d, relay_recv)
+            source = (chip + pairs - step) % pairs * 2 + core
+            for e in range(2):
+                pltpu.make_async_remote_copy(relay.at[t, d, :, pl.ds(e * hd, hd)],
+                                             heads.at[t, pl.ds(pl.multiple_of(source * rows + start, half), half)],
+                                             in_send.at[t], in_recv.at[t],
+                                             device_id={"cp": (chip + step) % pairs * 2 + e}, device_id_type=MESH).start()
+
+    def project(t, compute):
+        @pl.loop(0, pairs)
+        def _(i):
+            pair = (chip + pairs // 2 + i) % pairs
+            at = pl.ds(pl.multiple_of(pair * 2 * hd, 2 * hd), 2 * hd)
+            flat[t, :, at] = compute(at).astype(jnp.bfloat16)
+
+            def direct():
+                for e in range(2):
+                    send_in(t, pair * 2 + e)
+
+            if ways:
+                pl.when(i == 0)(lambda: relay_start(t))
+                pl.when(i != 0)(direct)
+            else:
+                direct()
+
+    @pl.loop(0, 3)
+    def _(t):
+        project(t, lambda at: mm(xr_ref[...], wall[t, :, at]))
+        relay_pass(t)
 
     gather_end(1, dy_ref, dyr_ref)
     dy_copy = pltpu.make_async_copy(dyr_ref, dy_out, row_sem.at[1])
     dy_copy.start()
     wo_copy.wait()
-
-    @pl.loop(0, pairs)
-    def _(i):
-        pair = (me_c // 2 + 1 + i) % pairs
-        at = pl.ds(pl.multiple_of(pair * 2 * hd, 2 * hd), 2 * hd)
-        flat[3, :, at] = mm(dyr_ref[...], wo_all[at, :], NT).astype(jnp.bfloat16)
-        for e in range(2):
-            send_in(3, pair * 2 + e)
+    project(3, lambda at: mm(dyr_ref[...], wo_all[at, :], NT))
 
     outs = (o_ref, dq_ref, dk_ref, dv_ref)
 
@@ -217,6 +249,7 @@
         stat[0, at, :] = jnp.broadcast_to(m + jnp.log(l), (qb, hd))
         send_out(0, i)
 
+    relay_pass(3)
     wait_in(3)
     for i in range(blocks):
         at = pl.ds(i * qb, qb)
@@ -342,6 +375,8 @@
     x_copy.wait()
     dy_copy.wait()
     for t in range(4):
+        for d in range(len(ways)):
+            relay_wait(t, d, relay_send)
         for sem in (in_send, out_send):
             pltpu.make_async_copy(others, others, sem.at[t]).wait()
     for which, src, dst in ((0, x_ref, xr_ref), (1, dy_ref, dyr_ref)):
@@ -367,38 +402,37 @@
     return pl.pallas_call(
         functools.partial(attention_kernel, tp, cp),
         out_shape=(out(rb, dm), wide(dm), *[wide(dm // 2)] * 4, out(rows, dm), out(rows, dm), out(rows, hc), out(rows, hc), out(rows, hc), out(rows, hc)),
-        in_specs=[vmem, vmem, hbm, hbm, hbm, hbm],
+        in_specs=[hbm] * 6,
         out_specs=[vmem] * 6 + [hbm] * 2 + [vmem] * 4,
         scratch_shapes=[
-            pltpu.VMEM((rows, dm), bf), pltpu.VMEM((rows, dm), bf),
+            pltpu.VMEM((rb, dm), bf), pltpu.VMEM((rb, dm), bf), pltpu.VMEM((rows, dm), bf), pltpu.VMEM((rows, dm), bf),
             pltpu.VMEM((SLOTS, chunk * cp, hd), bf), pltpu.VMEM((STRIPS, chunk // STRIPS * max(cp, PITCH), hd), f32),
             pltpu.VMEM((3, dm, hc), bf), pltpu.VMEM((hc, dm), bf),
-            pltpu.VMEM((4, rows, hc), bf), pltpu.VMEM((4, total, hd), bf),
+            pltpu.VMEM((4, rows, hc), bf), pltpu.VMEM((4, total, hd), bf), pltpu.VMEM((4, 2, rows // 2, 2 * hd), bf),
             pltpu.VMEM((4, total, hd), bf), pltpu.VMEM((total, hd), bf), pltpu.VMEM((4, total, hd), bf),
             pltpu.VMEM((2, total, hd), f32), pltpu.VMEM((2, 8, total), f32),
             pltpu.VMEM((rows, dm), f32), pltpu.VMEM((rows, dm), f32),
             pltpu.VMEM((RS_TILES, rb, width), f32), pltpu.VMEM((RS_TILES, rb, width), f32),
             pltpu.VMEM((RS_TILES, rb, width), f32), pltpu.VMEM((RS_TILES, rb, width), f32),
             pltpu.VMEM((2, RS_TILES // 2, rb, width), f32),
-            dma((SLOTS,)), dma, dma((2,)), dma((2, 6)), dma((2, 6)), dma((4,)), dma((4,)), dma((4,)), dma((4,)),
+            dma((SLOTS,)), dma, dma((2,)), dma((2,)), dma((2, 6)), dma((2, 6)), dma((4,)), dma((4,)), dma((4, 2)), dma((4, 2)), dma((4,)), dma((4,)),
             *[dma((RS_TILES,))] * 6, *[dma((2, RS_TILES // 2))] * 2,
         ],
         compiler_params=pltpu.CompilerParams(collective_id=0, has_side_effects=True, vmem_limit_bytes=VMEM_BYTES),
     )(x_blk, dy_blk, wq, wk, wv, wo)
 
 
-def grad_kernel(n_heads, x_hbm, dy_hbm, o_hbm, dq_hbm, dk_hbm, dv_hbm, y_ref, gq_ref, gk_ref, gv_ref, go_ref, y_out,
-                x_ref, dy_ref, o_ref, dq_ref, dk_ref, dv_ref, wide, grads, out_grad, in_sem, out_sem):
+def grad_kernel(n_heads, x_hbm, dy_hbm, o_hbm, dq_hbm, dk_hbm, dv_hbm, y_hbm, gq_ref, gk_ref, gv_ref, go_ref, y_out,
+                x_ref, dy_ref, o_ref, dq_ref, dk_ref, dv_ref, y_ref, wide, grads, out_grad, in_sem, out_sem):
     rows, dm = x_ref.shape
     hd = wide.shape[-1]
     tiles = grads.shape[1]
-    m_tile, o_tile = dm // tiles, n_heads * hd // tiles
+    m_tile = dm // tiles
     pitch = wide.shape[1] // m_tile
     loads = [pltpu.make_async_copy(src, dst, in_sem.at[i]) for i, (src, dst) in enumerate(
-        ((dq_hbm, dq_ref), (x_hbm, x_ref), (dk_hbm, dk_ref), (dv_hbm, dv_ref), (o_hbm, o_ref), (dy_hbm, dy_ref)))]
+        ((dq_hbm, dq_ref), (x_hbm, x_ref), (dk_hbm, dk_ref), (dv_hbm, dv_ref), (o_hbm, o_ref), (dy_hbm, dy_ref), (y_hbm, y_ref)))]
     for load in loads:
         load.start()
-    y_out[...] = y_ref[...]
     for load in loads[:4]:
         load.wait()
 
@@ -419,13 +453,19 @@
 
     for load in loads[4:]:
         load.wait()
-
-    @pl.loop(0, tiles)
+    y_out_copy = pltpu.make_async_copy(y_ref, y_out, out_sem.at[4])
+    y_out_copy.start()
+
+    o_rows, o_cols = out_grad.shape[1:]
+    across = dm // o_cols
+
+    @pl.loop(0, out_grad.shape[0])
     def _(i):
-        at = pl.ds(pl.multiple_of(i * o_tile, o_tile), o_tile)
-        out_grad[at, :] = mm(o_ref[:, at], dy_ref[...], TN).astype(jnp.bfloat16)
-        pltpu.make_async_copy(out_grad.at[at], go_ref.at[at], out_sem.at[3]).start()
-
+        r, c = pl.multiple_of(i // across * o_rows, o_rows), pl.multiple_of(i % across * o_cols, o_cols)
+        out_grad[i] = mm(o_ref[:, pl.ds(r, o_rows)], dy_ref[:, pl.ds(c, o_cols)], TN).astype(jnp.bfloat16)
+        pltpu.make_async_copy(out_grad.at[i], go_ref.at[pl.ds(r, o_rows), pl.ds(c, o_cols)], out_sem.at[3]).start()
+
+    y_out_copy.wait()
     for t, g_ref in enumerate((gq_ref, gk_ref, gv_ref, go_ref)):
         pltpu.make_async_copy(g_ref, g_ref, out_sem.at[t]).wait()
 
@@ -436,19 +476,20 @@
     hd = hc // n_heads
     tiles = n_heads
     bf, f32 = jnp.bfloat16, jnp.float32
-    hbm, vmem = pl.BlockSpec(memory_space=pl.ANY), pl.BlockSpec(memory_space=pltpu.VMEM)
-    inputs = (x_rows, dy_rows, o_flat, dq, dk, dv)
+    hbm = pl.BlockSpec(memory_space=pl.ANY)
+    inputs = (x_rows, dy_rows, o_flat, dq, dk, dv, y_blk)
+    o_rows, o_cols = hc // 2, dm // 4
     return pl.pallas_call(
         functools.partial(grad_kernel, n_heads),
         out_shape=[jax.ShapeDtypeStruct((dm * n_heads, hd), bf)] * 3 + [jax.ShapeDtypeStruct((hc, dm), bf), jax.ShapeDtypeStruct(y_blk.shape, bf)],
-        in_specs=[hbm] * 6 + [vmem],
-        out_specs=[hbm] * 4 + [vmem],
+        in_specs=[hbm] * 7,
+        out_specs=[hbm] * 5,
         scratch_shapes=[*[pltpu.VMEM(a.shape, bf) for a in inputs],
                         pltpu.VMEM((3, dm // tiles * max(n_heads, PITCH), hd), f32), pltpu.VMEM((3, tiles, dm // tiles * n_heads, hd), bf),
-                        pltpu.VMEM((hc, dm), bf), pltpu.SemaphoreType.DMA((6,)), pltpu.SemaphoreType.DMA((4,))],
+                        pltpu.VMEM((8, o_rows, o_cols), bf), pltpu.SemaphoreType.DMA((7,)), pltpu.SemaphoreType.DMA((5,))],
         compiler_params=pltpu.CompilerParams(vmem_limit_bytes=VMEM_BYTES),
         cost_estimate=pl.CostEstimate(flops=8 * rows * dm * hc, bytes_accessed=8 * dm * hc + 8 * rows * dm, transcendentals=0),
-    )(*inputs, y_blk)
+    )(*inputs)
 
 
 def add_kernel(own, direct_a, last_a, direct_b, last_b, dx_ref):

time: 95 us -> 98.3 us (1.035)
  Pallas kernels: 89.9 us -> 92.6 us
    pallas_call x1, Pallas kernels: 70.5 us -> 74.8 us  [attention_call(): pl.pallas_call(functools.partial(attention_kernel, tp, cp), out_shape=(ou...]
    pallas_call x1, Pallas kernels: 17.3 us -> 15.6 us  [grad_call(): pl.pallas_call(functools.partial(grad_kernel, n_heads), out_shape=[jax.Sh...]
  transfers between devices with their start and end apart: 4 -> 4, of which waited for: 0 -> 0; matrix products, arithmetic and copies ran while one was open for 0% -> 0% of each run, Pallas kernels for 18% -> 16%
where the time goes in v5:
time: 98.3 us; the launch traced here: 98.1 us
  Pallas kernels  92.6 us (94%)
  starting transfers between devices  4.81 us (5%)
    pallas_call x1, Pallas kernels, attention_call(): pl.pallas_call(functools.partial(attention_kernel, tp, cp), out_shape=(ou...  74.8 us
    pallas_call x1, Pallas kernels, grad_call(): pl.pallas_call(functools.partial(grad_kernel, n_heads), out_shape=[jax.Sh...  15.6 us
    ppermute x2, starting transfers between devices, device_fn(): lax.ppermute(a, 'tp', [(i, (i - 1) % tp) for i in range(tp)])  4.23 us
    pallas_call x1, Pallas kernels, device_fn(): pl.pallas_call(add_kernel, out_shape=jax.ShapeDtypeStruct(own.shape, jnp....  2.12 us
  transfers between devices with their start and end apart: 4, of which 0 were waited for; matrix products, arithmetic and copies ran while one was open for 0% of the time, Pallas kernels for 16%

profile of v5, /device:TPU:97, one launch (start us, length us, event | category | flops | bytes accessed | tf_op | source)
XLA Modules:
  0.0 98.1 jit_solution(11678343717938997793)
XLA Ops:
  0.6 74.8 %shard_map.109 = (bf16[32,4096]{1,0:T(8,128)(2,1)}, f32[32,4096]{1,0:T(8,128)}, f32[32,2048]{1,0:T(8,128)}, f32[32,2048]{1,0:T(8,128)}, f32[32,2048]{1,0:T(8,128...) custom-call(bf16[32,4096]{1,0:T(8,128)(2,1)} %refs_0_.1, ...), custom_call_target="tpu_custom_call" | custom-call | tf_op jit(solution)/shard_map/pallas_call | solution.py:402
  75.5 2.1 %collective-permute-start = (f32[32,2048]{1,0:T(8,128)}, f32[32,2048]{1,0:T(8,128)}, u32[]{:S(2)}, u32[]{:S(2)}) collective-permute-start(f32[32,2048]{1,0:T(8,128)} %get-tuple-element.32), channel_id=1, source_target_pairs={{0,24},{8,0},{16,8},{24,16},{1,25},{9,1},{17,9},{25,17},{2,26},{10... | collective-permute-start | bytes 786440 | tf_op jit(solution)/shard_map/ppermute | solution.py:512
  77.6 0.0 collective-permute-start.1
  77.6 0.6 collective-permute-start.2
  78.2 2.1 %collective-permute-start.3 = (f32[32,2048]{1,0:T(8,128)}, f32[32,2048]{1,0:T(8,128)}, u32[]{:S(2)}, u32[]{:S(2)}) collective-permute-start(f32[32,2048]{1,0:T(8,128)} %get-tuple-element.35), channel_id=1, source_target_pairs={{0,24},{8,0},{16,8},{24,16},{1,25},{9,1},{17,9},{25,17},{2,26},{10... | collective-permute-start | bytes 786440 | tf_op jit(solution)/shard_map/ppermute | solution.py:512
  80.3 15.6 %shard_map.110 = (bf16[32768,128]{1,0:T(8,128)(2,1)}, bf16[32768,128]{1,0:T(8,128)(2,1)}, bf16[32768,128]{1,0:T(8,128)(2,1)}, bf16[1024,4096]{1,0:T(8,128)(2,1)}, bf16[32,4096]{1,0:T(8,128)(2,1)}) custom-call(bf16[128,4096]{1,0:T(8,128)(2,1)} %get-tuple-element.23.x_hbm, bf16[128,4096]{1,0:T(8,128)(2,1)} %get-tuple-element.24.dy_hbm, ...), custom_call_target="tpu_custom_call" | custom-call | flops 4294967296 | bytes 37748736 | tf_op jit(solution)/shard_map/pallas_call | solution.py:482
  95.9 0.0 collective-permute-done.direct_a
  95.9 0.0 collective-permute-done.1.last_a
  95.9 0.0 collective-permute-done.2.direct_b
  95.9 0.0 collective-permute-done.3.last_b
  96.0 2.1 %shard_map.111 = bf16[32,4096]{1,0:T(8,128)(2,1)} custom-call(f32[32,4096]{1,0:T(8,128)} %get-tuple-element.31.own, f32[32,2048]{1,0:T(8,128)} %collective-permute-done.direct_a, f32[32,2048]{1,0:T(8,128)} %collective-permute-done.1.last_a, f32[32,2048]{1,0:T(8,128)} %collective-permute-done.2.direct_b, f32[32,2048]{1,0:T(8,128)} %collective-permute-done.3.last_b), custom_call_target="tpu_custom_call" | custom-call | tf_op jit(solution)/shard_map/pallas_call | solution.py:516
Async XLA Ops:
  75.5 20.4 %collective-permute-start = (f32[32,2048]{1,0:T(8,128)}, f32[32,2048]{1,0:T(8,128)}, u32[]{:S(2)}, u32[]{:S(2)}) collective-permute-start(f32[32,2048]{1,0:T(8,128)} %get-tuple-element.32), channel_id=1, source_target_pairs={{0,24},{8,0},{16,8},{24,16},{1,25},{9,1},{17,9},{25,17},{2,26},{10... | collective-permute-start | bytes 786440 | tf_op jit(solution)/shard_map/ppermute | solution.py:512
  77.6 18.3 %collective-permute-start.1 = (f32[32,2048]{1,0:T(8,128)}, f32[32,2048]{1,0:T(8,128)}, u32[]{:S(2)}, u32[]{:S(2)}) collective-permute-start(f32[32,2048]{1,0:T(8,128)} %get-tuple-element.33), channel_id=1, source_target_pairs={{0,8},{8,16},{16,24},{24,0},{1,9},{9,17},{17,25},{25,1},{2,10},{10... | collective-permute-start | bytes 786440 | tf_op jit(solution)/shard_map/ppermute | solution.py:511
  77.6 18.3 %collective-permute-start.2 = (f32[32,2048]{1,0:T(8,128)}, f32[32,2048]{1,0:T(8,128)}, u32[]{:S(2)}, u32[]{:S(2)}) collective-permute-start(f32[32,2048]{1,0:T(8,128)} %get-tuple-element.34), channel_id=1, source_target_pairs={{0,8},{8,16},{16,24},{24,0},{1,9},{9,17},{17,25},{25,1},{2,10},{10... | collective-permute-start | bytes 786440 | tf_op jit(solution)/shard_map/ppermute | solution.py:511
  78.2 17.8 %collective-permute-start.3 = (f32[32,2048]{1,0:T(8,128)}, f32[32,2048]{1,0:T(8,128)}, u32[]{:S(2)}, u32[]{:S(2)}) collective-permute-start(f32[32,2048]{1,0:T(8,128)} %get-tuple-element.35), channel_id=1, source_target_pairs={{0,24},{8,0},{16,8},{24,16},{1,25},{9,1},{17,9},{25,17},{2,26},{10... | collective-permute-start | bytes 786440 | tf_op jit(solution)/shard_map/ppermute | solution.py:512

commit v6 on v5

--- a/solution.py
+++ b/solution.py
@@ -31,9 +31,9 @@
 def attention_kernel(tp, cp, *refs):
     (x_hbm, dy_hbm, wq_ref, wk_ref, wv_ref, wo_ref,
      y_ref, own_ref, back_l, back_r, on_r, on_l, x_out, dy_out, o_ref, dq_ref, dk_ref, dv_ref,
-     x_ref, dy_ref, xr_ref, dyr_ref, wbuf, wf32, wall, wo_all, flat, heads, relay, sorted_heads, sorted_o, out_heads, stat, stat_t,
+     x_ref, dy_ref, xr_ref, dyr_ref, wbuf, wf32, wall, wo_all, flat, heads, sorted_heads, sorted_o, out_heads, stat, stat_t,
      part, dx_part, r1, r2, r3, s2, r4,
-     w_sem, wo_sem, load_sem, row_sem, ag_send, ag_recv, in_send, in_recv, relay_send, relay_recv, out_send, out_recv,
+     w_sem, wo_sem, load_sem, row_sem, ag_send, ag_recv, in_send, in_recv, out_send, out_recv,
      r1_send, r1_recv, r2_send, r2_recv, r3_send, r3_recv, r4_send, r4_recv) = refs
     me_t, me_c = lax.axis_index("tp"), lax.axis_index("cp")
     right, left, across = (me_t + 1) % tp, (me_t + tp - 1) % tp, (me_t + 2) % tp
@@ -130,7 +130,6 @@
     gather_end(0, x_ref, xr_ref)
     x_copy = pltpu.make_async_copy(xr_ref, x_out, row_sem.at[0])
     x_copy.start()
-    gather_pass(1, dy_ref, dyr_ref)
 
     mine_at = pl.ds(pl.multiple_of(me_c * hd, hd), hd)
     my_rows = pl.ds(pl.multiple_of(me_c * rows, rows), rows)
@@ -151,55 +150,21 @@
             sorted_heads[t, b * half:(b + 1) * half, :] = heads[t, start:start + half, :]
 
     pairs = cp // 2
-    chip, core = me_c // 2, me_c % 2
-    ways = ((1, 0), (pairs - 1, half)) if pairs == 4 else ()
-
-    def relay_start(t):
-        for d, (step, start) in enumerate(ways):
-            far = pl.ds(pl.multiple_of((chip + 2) % pairs * 2 * hd, 2 * hd), 2 * hd)
-            pltpu.make_async_remote_copy(flat.at[t, pl.ds(start, half), far], relay.at[t, d], relay_send.at[t, d], relay_recv.at[t, d],
-                                         device_id={"cp": (chip + step) % pairs * 2 + core}, device_id_type=MESH).start()
-
-    def relay_wait(t, d, sem):
-        pltpu.make_async_copy(relay.at[t, d], relay.at[t, d], sem.at[t, d]).wait()
-
-    def relay_pass(t):
-        for d, (step, start) in enumerate(ways):
-            relay_wait(t, d, relay_recv)
-            source = (chip + pairs - step) % pairs * 2 + core
-            for e in range(2):
-                pltpu.make_async_remote_copy(relay.at[t, d, :, pl.ds(e * hd, hd)],
-                                             heads.at[t, pl.ds(pl.multiple_of(source * rows + start, half), half)],
-                                             in_send.at[t], in_recv.at[t],
-                                             device_id={"cp": (chip + step) % pairs * 2 + e}, device_id_type=MESH).start()
+    chip = me_c // 2
 
     def project(t, compute):
         @pl.loop(0, pairs)
         def _(i):
-            pair = (chip + pairs // 2 + i) % pairs
+            pair = (chip + 1 + i) % pairs
             at = pl.ds(pl.multiple_of(pair * 2 * hd, 2 * hd), 2 * hd)
             flat[t, :, at] = compute(at).astype(jnp.bfloat16)
-
-            def direct():
-                for e in range(2):
-                    send_in(t, pair * 2 + e)
-
-            if ways:
-                pl.when(i == 0)(lambda: relay_start(t))
-                pl.when(i != 0)(direct)
-            else:
-                direct()
-
-    @pl.loop(0, 3)
-    def _(t):
+            for e in range(2):
+                send_in(t, pair * 2 + e)
+
+    project(0, lambda at: mm(xr_ref[...], wall[0, :, at]))
+    gather_pass(1, dy_ref, dyr_ref)
+    for t in range(1, 3):
         project(t, lambda at: mm(xr_ref[...], wall[t, :, at]))
-        relay_pass(t)
-
-    gather_end(1, dy_ref, dyr_ref)
-    dy_copy = pltpu.make_async_copy(dyr_ref, dy_out, row_sem.at[1])
-    dy_copy.start()
-    wo_copy.wait()
-    project(3, lambda at: mm(dyr_ref[...], wo_all[at, :], NT))
 
     outs = (o_ref, dq_ref, dk_ref, dv_ref)
 
@@ -249,7 +214,61 @@
         stat[0, at, :] = jnp.broadcast_to(m + jnp.log(l), (qb, hd))
         send_out(0, i)
 
-    relay_pass(3)
+    gather_end(1, dy_ref, dyr_ref)
+    dy_copy = pltpu.make_async_copy(dyr_ref, dy_out, row_sem.at[1])
+    dy_copy.start()
+    wo_copy.wait()
+    project(3, lambda at: mm(dyr_ref[...], wo_all[at, :], NT))
+    width = dm // RS_TILES
+
+    def rs_parts(tile, odd):
+        onward, back = (left, right) if odd else (right, left)
+        at = pl.ds(pl.multiple_of(tile * width, width), width)
+
+        def mine(d):
+            return (pl.ds(pl.multiple_of(d * rb, rb), rb), at)
+
+        def copy(src, dst, send, recv, to):
+            return pltpu.make_async_remote_copy(src, dst.at[tile], send.at[tile], recv.at[tile],
+                                                device_id={"tp": to}, device_id_type=MESH)
+
+        first = lambda: copy(part.at[mine(across)], r1, r1_send, r1_recv, onward)
+        second = lambda: copy(s2.at[tile], r2, r2_send, r2_recv, onward)
+        direct = lambda: copy(part.at[mine(back)], r3, r3_send, r3_recv, back)
+        return at, mine, onward, first, second, direct
+
+    def pairs_of_tiles(step):
+        @pl.loop(0, RS_TILES // 2)
+        def _(i):
+            for odd in range(2):
+                step(i * 2 + odd, odd)
+
+    def reduce_first(tile, odd):
+        at, _, _, first, _, _ = rs_parts(tile, odd)
+        part[:, at] = mm(o_ref[...], wo_all[:, at])
+        first().start()
+
+    def reduce_direct(tile, odd):
+        rs_parts(tile, odd)[5]().start()
+
+    def reduce_second(tile, odd):
+        _, mine, onward, first, second, _ = rs_parts(tile, odd)
+        first().wait_recv()
+        s2[tile] = r1[tile] + part[mine(onward)]
+        second().start()
+
+    def reduce_last(tile, odd):
+        at, mine, _, first, second, direct = rs_parts(tile, odd)
+        direct().wait_recv()
+        second().wait_recv()
+        y_ref[:, at] = (part[mine(me_t)] + r2[tile] + r3[tile]).astype(jnp.bfloat16)
+        first().wait_send()
+        second().wait_send()
+        direct().wait_send()
+
+    wait_out(0)
+    pairs_of_tiles(reduce_first)
+    pairs_of_tiles(reduce_direct)
     wait_in(3)
     for i in range(blocks):
         at = pl.ds(i * qb, qb)
@@ -267,56 +286,6 @@
         ds = (p * (dp - stat[1, at, :1])).astype(jnp.bfloat16)
         put(1, i, (mm(ds, sorted_heads[1, :n, :]) * scale).astype(jnp.bfloat16))
         send_out(1, i)
-    width = dm // RS_TILES
-
-    def rs_parts(tile, odd):
-        onward, back = (left, right) if odd else (right, left)
-        at = pl.ds(pl.multiple_of(tile * width, width), width)
-
-        def mine(d):
-            return (pl.ds(pl.multiple_of(d * rb, rb), rb), at)
-
-        def copy(src, dst, send, recv, to):
-            return pltpu.make_async_remote_copy(src, dst.at[tile], send.at[tile], recv.at[tile],
-                                                device_id={"tp": to}, device_id_type=MESH)
-
-        first = lambda: copy(part.at[mine(across)], r1, r1_send, r1_recv, onward)
-        second = lambda: copy(s2.at[tile], r2, r2_send, r2_recv, onward)
-        direct = lambda: copy(part.at[mine(back)], r3, r3_send, r3_recv, back)
-        return at, mine, onward, first, second, direct
-
-    def pairs_of_tiles(step):
-        @pl.loop(0, RS_TILES // 2)
-        def _(i):
-            for odd in range(2):
-                step(i * 2 + odd, odd)
-
-    def reduce_first(tile, odd):
-        at, _, _, first, _, _ = rs_parts(tile, odd)
-        part[:, at] = mm(o_ref[...], wo_all[:, at])
-        first().start()
-
-    def reduce_direct(tile, odd):
-        rs_parts(tile, odd)[5]().start()
-
-    def reduce_second(tile, odd):
-        _, mine, onward, first, second, _ = rs_parts(tile, odd)
-        first().wait_recv()
-        s2[tile] = r1[tile] + part[mine(onward)]
-        second().start()
-
-    def reduce_last(tile, odd):
-        at, mine, _, first, second, direct = rs_parts(tile, odd)
-        direct().wait_recv()
-        second().wait_recv()
-        y_ref[:, at] = (part[mine(me_t)] + r2[tile] + r3[tile]).astype(jnp.bfloat16)
-        first().wait_send()
-        second().wait_send()
-        direct().wait_send()
-
-    wait_out(0)
-    pairs_of_tiles(reduce_first)
-    pairs_of_tiles(reduce_direct)
     for i in walk:
         at, after = pl.ds(i * qb, qb), pl.ds(i * qb, total - i * qb)
         s = mm(sorted_heads[1, at, :], sorted_heads[0, after, :], NT) * scale
@@ -375,8 +344,6 @@
     x_copy.wait()
     dy_copy.wait()
     for t in range(4):
-        for d in range(len(ways)):
-            relay_wait(t, d, relay_send)
         for sem in (in_send, out_send):
             pltpu.make_async_copy(others, others, sem.at[t]).wait()
     for which, src, dst in ((0, x_ref, xr_ref), (1, dy_ref, dyr_ref)):
@@ -408,14 +375,14 @@
             pltpu.VMEM((rb, dm), bf), pltpu.VMEM((rb, dm), bf), pltpu.VMEM((rows, dm), bf), pltpu.VMEM((rows, dm), bf),
             pltpu.VMEM((SLOTS, chunk * cp, hd), bf), pltpu.VMEM((STRIPS, chunk // STRIPS * max(cp, PITCH), hd), f32),
             pltpu.VMEM((3, dm, hc), bf), pltpu.VMEM((hc, dm), bf),
-            pltpu.VMEM((4, rows, hc), bf), pltpu.VMEM((4, total, hd), bf), pltpu.VMEM((4, 2, rows // 2, 2 * hd), bf),
+            pltpu.VMEM((4, rows, hc), bf), pltpu.VMEM((4, total, hd), bf),
             pltpu.VMEM((4, total, hd), bf), pltpu.VMEM((total, hd), bf), pltpu.VMEM((4, total, hd), bf),
             pltpu.VMEM((2, total, hd), f32), pltpu.VMEM((2, 8, total), f32),
             pltpu.VMEM((rows, dm), f32), pltpu.VMEM((rows, dm), f32),
             pltpu.VMEM((RS_TILES, rb, width), f32), pltpu.VMEM((RS_TILES, rb, width), f32),
             pltpu.VMEM((RS_TILES, rb, width), f32), pltpu.VMEM((RS_TILES, rb, width), f32),
             pltpu.VMEM((2, RS_TILES // 2, rb, width), f32),
-            dma((SLOTS,)), dma, dma((2,)), dma((2,)), dma((2, 6)), dma((2, 6)), dma((4,)), dma((4,)), dma((4, 2)), dma((4, 2)), dma((4,)), dma((4,)),
+            dma((SLOTS,)), dma, dma((2,)), dma((2,)), dma((2, 6)), dma((2, 6)), dma((4,)), dma((4,)), dma((4,)), dma((4,)),
             *[dma((RS_TILES,))] * 6, *[dma((2, RS_TILES // 2))] * 2,
         ],
         compiler_params=pltpu.CompilerParams(collective_id=0, has_side_effects=True, vmem_limit_bytes=VMEM_BYTES),

time: 98.3 us -> 90.9 us (0.925)
  Pallas kernels: 92.6 us -> 85.3 us
    pallas_call x1, Pallas kernels: 74.8 us -> 67.5 us  [attention_call(): pl.pallas_call(functools.partial(attention_kernel, tp, cp), out_shape=(ou...]
  transfers between devices with their start and end apart: 4 -> 4, of which waited for: 0 -> 0; matrix products, arithmetic and copies ran while one was open for 0% -> 0% of each run, Pallas kernels for 16% -> 17%
where the time goes in v6:
time: 90.9 us; the launch traced here: 90.7 us
  Pallas kernels  85.3 us (94%)
  starting transfers between devices  4.76 us (5%)
    pallas_call x1, Pallas kernels, attention_call(): pl.pallas_call(functools.partial(attention_kernel, tp, cp), out_shape=(ou...  67.5 us
    pallas_call x1, Pallas kernels, grad_call(): pl.pallas_call(functools.partial(grad_kernel, n_heads), out_shape=[jax.Sh...  15.6 us
    ppermute x2, starting transfers between devices, device_fn(): lax.ppermute(a, 'tp', [(i, (i - 1) % tp) for i in range(tp)])  4.76 us
    pallas_call x1, Pallas kernels, device_fn(): pl.pallas_call(add_kernel, out_shape=jax.ShapeDtypeStruct(own.shape, jnp....  2.12 us
  transfers between devices with their start and end apart: 4, of which 0 were waited for; matrix products, arithmetic and copies ran while one was open for 0% of the time, Pallas kernels for 17%

profile of v6, /device:TPU:97, one launch (start us, length us, event | category | flops | bytes accessed | tf_op | source)
XLA Modules:
  0.0 90.7 jit_solution(17087152465507248840)
XLA Ops:
  0.6 67.5 %shard_map.109 = (bf16[32,4096]{1,0:T(8,128)(2,1)}, f32[32,4096]{1,0:T(8,128)}, f32[32,2048]{1,0:T(8,128)}, f32[32,2048]{1,0:T(8,128)}, f32[32,2048]{1,0:T(8,128...) custom-call(bf16[32,4096]{1,0:T(8,128)(2,1)} %refs_0_.1, ...), custom_call_target="tpu_custom_call" | custom-call | tf_op jit(solution)/shard_map/pallas_call | solution.py:369
  68.2 2.1 %collective-permute-start = (f32[32,2048]{1,0:T(8,128)}, f32[32,2048]{1,0:T(8,128)}, u32[]{:S(2)}, u32[]{:S(2)}) collective-permute-start(f32[32,2048]{1,0:T(8,128)} %get-tuple-element.32), channel_id=1, source_target_pairs={{0,24},{8,0},{16,8},{24,16},{1,25},{9,1},{17,9},{25,17},{2,26},{10... | collective-permute-start | bytes 786440 | tf_op jit(solution)/shard_map/ppermute | solution.py:479
  70.3 0.0 collective-permute-start.1
  70.3 0.0 collective-permute-start.2
  70.3 2.7 %collective-permute-start.3 = (f32[32,2048]{1,0:T(8,128)}, f32[32,2048]{1,0:T(8,128)}, u32[]{:S(2)}, u32[]{:S(2)}) collective-permute-start(f32[32,2048]{1,0:T(8,128)} %get-tuple-element.35), channel_id=1, source_target_pairs={{0,24},{8,0},{16,8},{24,16},{1,25},{9,1},{17,9},{25,17},{2,26},{10... | collective-permute-start | bytes 786440 | tf_op jit(solution)/shard_map/ppermute | solution.py:479
  72.9 15.6 %shard_map.110 = (bf16[32768,128]{1,0:T(8,128)(2,1)}, bf16[32768,128]{1,0:T(8,128)(2,1)}, bf16[32768,128]{1,0:T(8,128)(2,1)}, bf16[1024,4096]{1,0:T(8,128)(2,1)}, bf16[32,4096]{1,0:T(8,128)(2,1)}) custom-call(bf16[128,4096]{1,0:T(8,128)(2,1)} %get-tuple-element.23.x_hbm, bf16[128,4096]{1,0:T(8,128)(2,1)} %get-tuple-element.24.dy_hbm, ...), custom_call_target="tpu_custom_call" | custom-call | flops 4294967296 | bytes 37748736 | tf_op jit(solution)/shard_map/pallas_call | solution.py:449
  88.6 0.0 collective-permute-done.direct_a
  88.6 0.0 collective-permute-done.1.last_a
  88.6 0.0 collective-permute-done.2.direct_b
  88.6 0.0 collective-permute-done.3.last_b
  88.6 2.1 %shard_map.111 = bf16[32,4096]{1,0:T(8,128)(2,1)} custom-call(f32[32,4096]{1,0:T(8,128)} %get-tuple-element.31.own, f32[32,2048]{1,0:T(8,128)} %collective-permute-done.direct_a, f32[32,2048]{1,0:T(8,128)} %collective-permute-done.1.last_a, f32[32,2048]{1,0:T(8,128)} %collective-permute-done.2.direct_b, f32[32,2048]{1,0:T(8,128)} %collective-permute-done.3.last_b), custom_call_target="tpu_custom_call" | custom-call | tf_op jit(solution)/shard_map/pallas_call | solution.py:483
Async XLA Ops:
  68.2 20.4 %collective-permute-start = (f32[32,2048]{1,0:T(8,128)}, f32[32,2048]{1,0:T(8,128)}, u32[]{:S(2)}, u32[]{:S(2)}) collective-permute-start(f32[32,2048]{1,0:T(8,128)} %get-tuple-element.32), channel_id=1, source_target_pairs={{0,24},{8,0},{16,8},{24,16},{1,25},{9,1},{17,9},{25,17},{2,26},{10... | collective-permute-start | bytes 786440 | tf_op jit(solution)/shard_map/ppermute | solution.py:479
  70.3 18.3 %collective-permute-start.1 = (f32[32,2048]{1,0:T(8,128)}, f32[32,2048]{1,0:T(8,128)}, u32[]{:S(2)}, u32[]{:S(2)}) collective-permute-start(f32[32,2048]{1,0:T(8,128)} %get-tuple-element.33), channel_id=1, source_target_pairs={{0,8},{8,16},{16,24},{24,0},{1,9},{9,17},{17,25},{25,1},{2,10},{10... | collective-permute-start | bytes 786440 | tf_op jit(solution)/shard_map/ppermute | solution.py:478
  70.3 18.3 %collective-permute-start.2 = (f32[32,2048]{1,0:T(8,128)}, f32[32,2048]{1,0:T(8,128)}, u32[]{:S(2)}, u32[]{:S(2)}) collective-permute-start(f32[32,2048]{1,0:T(8,128)} %get-tuple-element.34), channel_id=1, source_target_pairs={{0,8},{8,16},{16,24},{24,0},{1,9},{9,17},{17,25},{25,1},{2,10},{10... | collective-permute-start | bytes 786440 | tf_op jit(solution)/shard_map/ppermute | solution.py:478
  70.3 18.3 %collective-permute-start.3 = (f32[32,2048]{1,0:T(8,128)}, f32[32,2048]{1,0:T(8,128)}, u32[]{:S(2)}, u32[]{:S(2)}) collective-permute-start(f32[32,2048]{1,0:T(8,128)} %get-tuple-element.35), channel_id=1, source_target_pairs={{0,24},{8,0},{16,8},{24,16},{1,25},{9,1},{17,9},{25,17},{2,26},{10... | collective-permute-start | bytes 786440 | tf_op jit(solution)/shard_map/ppermute | solution.py:479
